TPU v7x, 256 devices: a whole 4x4x8 slice. The times are simulated.
256 devices in a mesh: seq: 8 (over z), head: 16 (over y, x), batch: 2 (over core).
Axes of the slice: x: 4, y: 4, z: 8, core: 2. Of those that a mesh axis runs over, the one named last changes fastest.
Arguments:
- ssm_input: bfloat16 [32768, 5120], P(('batch', 'seq'), 'head'), parts along dimension 0, may hold values from -500 to 500
- gate_input: bfloat16 [32768, 5120], P(('batch', 'seq'), 'head'), parts along dimension 0, may hold values from -6 to 6
- b_proj: bfloat16 [32768, 1024], P(('batch', 'seq')), parts along dimension 0, may hold values from -2 to 2
- c_proj: bfloat16 [32768, 1024], P(('batch', 'seq')), parts along dimension 0, may hold values from -2 to 2
- step_size: float32 [80, 32768], P('head', ('batch', 'seq')), parts along dimension 1, may hold values from 0.02 to 0.2
- log_decay: float32 [80, 32768], P('head', ('batch', 'seq')), parts along dimension 1, may hold values from -1.5 to 0, as said below
- skip_gain: float32 [80], P('head'), may hold values from 0.5 to 1.5
- norm_gain: float32 [5120], replicated, may hold values from 0.1 to 1.9
- out_weight: bfloat16 [5120, 2560], P('head'), may hold values from -0.078125 to 0.078125
Outputs:
- layer_out: bfloat16 [32768, 2560], P(('batch', 'seq', 'head')), parts along dimension 0
There are 2 independent parts, one for each index of `batch`. A program takes and returns all parts, laid end to end along the dimension named above; an argument that names none is the same for every part. Nothing has to cross between parts.
Inputs may be any that keep to these rules, and one draw needn't show every extreme that they name: `log_decay`: negative.
All inputs are finite; a program needn't handle non-finite values.
Results may differ from a plain program's by a relative error of at most 0.018.
Values may be sent and summed in bfloat16 or wider, within the bound.
No kernel may reach another device: no remote copies, remote signals or barrier semaphores. Data moves between devices by JAX's collectives and lax.ppermute only.
A program may use at most 128 MiB of HBM per device.

v0:
```python
import jax
import jax.numpy as jnp
from jax import lax
from jax.experimental import pallas as pl
from jax.experimental.pallas import tpu as pltpu
from jax.sharding import PartitionSpec as P


HEAD_COUNT = 80
HEAD_DIM = 64
STATE = 128
GROUPS = 8
BLOCK = 256
RING = 4
SUB = 128
EXTRA = 8
PAD = 8

epsilon = 1e-05


f32 = jnp.float32
bf16 = jnp.bfloat16
TT = (((1,), (1,)), ((), ()))


def triangle(size, dtype):
    rows = lax.broadcasted_iota(jnp.int32, (size, size), 0)
    columns = lax.broadcasted_iota(jnp.int32, (size, size), 1)
    return (rows <= columns).astype(dtype)


def split3(value):
    high = value.astype(bf16)
    rest = value - high.astype(f32)
    middle = rest.astype(bf16)
    return high, middle, (rest - middle.astype(f32)).astype(bf16)


def join3(stacked, rows):
    return stacked[0:rows].astype(f32) + stacked[rows : 2 * rows].astype(f32) + stacked[2 * rows : 3 * rows].astype(f32)


def per_head(column, heads, lanes):
    return jnp.concatenate(
        [jnp.broadcast_to(column[h : h + 1, 0:1], (HEAD_DIM, lanes)) for h in range(heads)], axis=0
    )


def state_kernel(x_ref, b_hbm, c_hbm, step_ref, decay_ref, prefix_ref, total_ref, cum_ref, factor_ref, b_ref, c_ref, sems):
    heads, tokens = step_ref.shape
    blocks = tokens // BLOCK
    group = lax.axis_index("head") * heads * GROUPS // HEAD_COUNT
    columns = pl.ds(pl.multiple_of(group * STATE, STATE), STATE)
    fetch_b = pltpu.make_async_copy(b_hbm.at[:, columns], b_ref, sems.at[0])
    fetch_c = pltpu.make_async_copy(c_hbm.at[:, columns], c_ref, sems.at[1])
    fetch_b.start()
    fetch_c.start()
    fill = jnp.zeros((PAD - heads, BLOCK), f32)
    decay = jnp.concatenate(
        [piece for c in range(blocks) for piece in (decay_ref[:, c * BLOCK : (c + 1) * BLOCK], fill)], axis=0
    )
    sums = jnp.dot(
        jnp.concatenate(split3(decay), axis=0), triangle(BLOCK, bf16), preferred_element_type=f32
    )
    sums = join3(sums, blocks * PAD)
    offset = jnp.zeros((PAD, 1), f32)
    for c in range(blocks):
        span = slice(c * BLOCK, (c + 1) * BLOCK)
        cumulative = sums[c * PAD : (c + 1) * PAD]
        cum_ref[:, span] = cumulative
        factor_ref[:, span] = jnp.exp(cumulative + offset)
        offset = offset + cumulative[:, BLOCK - 1 :]
    fetch_b.wait()
    state = jnp.zeros((heads * HEAD_DIM, STATE), f32)
    for c in range(blocks):
        span = slice(c * BLOCK, (c + 1) * BLOCK)
        cumulative = sums[c * PAD : (c + 1) * PAD]
        end = cumulative[:, BLOCK - 1 :]
        prefix_ref[c] = state.astype(bf16)
        to_end = jnp.exp(end - cumulative)[0:heads] * step_ref[:, span]
        scaled = jnp.concatenate(
            [
                (x_ref[h * HEAD_DIM : (h + 1) * HEAD_DIM, span].astype(f32) * to_end[h : h + 1]).astype(bf16)
                for h in range(heads)
            ],
            axis=0,
        )
        block_state = jnp.dot(scaled, b_ref[span, :], preferred_element_type=f32)
        state = per_head(jnp.exp(end), heads, STATE) * state + block_state
    total_ref[0 : heads * HEAD_DIM, :] = state.astype(bf16)
    parts = split3(jnp.broadcast_to(offset, (PAD, STATE)))
    total_ref[heads * HEAD_DIM :, :] = jnp.concatenate(parts, axis=0)
    fetch_c.wait()


def within_kernel(skip_ref, x_ref, b_ref, c_ref, cum_ref, step_ref, prefix_ref, out_ref):
    heads = step_ref.shape[0]
    half = BLOCK // 2
    causal = triangle(half, f32).T > 0
    for k in range(step_ref.shape[1] // BLOCK):
        span = slice(k * BLOCK, (k + 1) * BLOCK)
        c_block = c_ref[span, :]
        b_block = b_ref[span, :]
        scores_first = lax.dot_general(c_block[:half], b_block[:half], TT, preferred_element_type=f32)
        scores_second = lax.dot_general(c_block[half:], b_block, TT, preferred_element_type=f32)
        across = lax.dot_general(prefix_ref[k], c_block, TT, preferred_element_type=f32)
        cumulative = cum_ref[:, span]
        factor = jnp.exp(cumulative)
        columns = cumulative.T
        for h in range(heads):
            channels = slice(h * HEAD_DIM, (h + 1) * HEAD_DIM)
            x_head = x_ref[channels, span]
            row = cumulative[h : h + 1]
            step = step_ref[h : h + 1, span]
            differ = columns[:half, h : h + 1] - row[:, :half]
            first = scores_first * jnp.exp(jnp.where(causal, differ, -jnp.inf)) * step[:, :half]
            column = columns[half:, h : h + 1]
            full = scores_second[:, :half] * jnp.exp(column - row[:, :half]) * step[:, :half]
            differ = column - row[:, half:]
            last = scores_second[:, half:] * jnp.exp(jnp.where(causal, differ, -jnp.inf)) * step[:, half:]
            second = jnp.concatenate([full, last], axis=1)
            within = jnp.concatenate(
                [
                    lax.dot_general(x_head[:, :half], first.astype(bf16), TT, preferred_element_type=f32),
                    lax.dot_general(x_head, second.astype(bf16), TT, preferred_element_type=f32),
                ],
                axis=1,
            )
            out_ref[channels, span] = (
                within + across[channels] * factor[h : h + 1] + skip_ref[h] * x_head.astype(f32)
            )


def ring_place():
    head_index = lax.axis_index("head")
    core = lax.axis_index("batch")
    y, x = head_index // RING, head_index % RING
    return core, jnp.where(core == 0, x, y), jnp.where(core == 0, y, x)


def head_at(core, u, v):
    return jnp.where(core == 0, v * RING + u, u * RING + v)


def gate_kernel(out_ref, gate_ref, c_ref, factor_ref, *refs):
    totals, results = refs[:-RING], refs[-RING:]
    channels = out_ref.shape[0]
    heads = channels // HEAD_DIM
    incoming = jnp.zeros((channels, STATE), f32)
    log_sum = jnp.zeros((PAD, STATE), f32)
    for total in totals:
        incoming = incoming + per_head(jnp.exp(log_sum), heads, STATE) * total[0:channels, :].astype(f32)
        log_sum = log_sum + join3(total[channels:, :], PAD)
    incoming = incoming.astype(bf16)
    core, u, v = ring_place()
    for su in range(RING):
        for sv in range(RING):
            place = head_at(core, (u + su) % RING, (v + sv) % RING)
            span = pl.ds(pl.multiple_of(place * SUB, SUB), SUB)
            across = lax.dot_general(incoming, c_ref[span, :], TT, preferred_element_type=f32)
            factor = factor_ref[:, span]
            for h in range(heads):
                rows = slice(h * HEAD_DIM, (h + 1) * HEAD_DIM)
                gate = gate_ref[rows, span].astype(f32)
                output = out_ref[rows, span] + across[rows] * factor[h : h + 1]
                gated = output * (gate / (1.0 + jnp.exp(-gate)))
                results[su][rows, sv * SUB : (sv + 1) * SUB] = gated.astype(bf16)


def gain_row(gain_ref, head, channels):
    first = head * channels
    lines = gain_ref[pl.ds(first // SUB, 3), :]
    line = jnp.concatenate([lines[i : i + 1] for i in range(3)], axis=1)
    shifted = jnp.concatenate([line[:, SUB // 2 :], line[:, : SUB // 2]], axis=1)
    return jnp.where(first % SUB == 0, line, shifted)[:, :channels]


def left_side(gain_ref, rows, blocks):
    core, u, v = ring_place()
    channels = rows[0].shape[0]
    pick = [slice(k * SUB, (k + 1) * SUB) for k in blocks]
    values = jnp.concatenate([jnp.concatenate([r[:, span] for span in pick], axis=1) for r in rows], axis=0)
    wide = values.astype(f32)
    squares = jnp.sum(wide * wide, axis=0, keepdims=True)
    gains = jnp.concatenate(
        [gain_row(gain_ref, head_at(core, (u - s + RING) % RING, v), channels) for s in range(RING)], axis=1
    )
    return (values.T.astype(f32) * gains).astype(bf16), squares


def tail_rows(squares, width):
    parts = [part.astype(f32) for part in split3(squares)]
    tail = jnp.concatenate(parts + [jnp.zeros((EXTRA - 3, SUB), f32)], axis=0)
    return jnp.concatenate([tail] * (width // SUB), axis=1).astype(bf16)


def tail_squares(part):
    return jnp.sum(part[SUB:, 0:SUB].astype(f32), axis=0, keepdims=True)


def opposite_kernel(gain_ref, *refs):
    rows, weights = refs[:RING], refs[RING:-3]
    first_ref, second_ref, left = refs[-3:]
    half = first_ref.shape[1]
    left[...], squares = left_side(gain_ref, rows, (2,))
    first_ref[SUB:, :] = tail_rows(squares, half)
    tile = 256
    for n in range(2 * half // tile):
        right = jnp.concatenate([w[:, n * tile : (n + 1) * tile] for w in weights], axis=0)
        product = jnp.dot(left[...], right, preferred_element_type=f32).astype(bf16)
        if n * tile < half:
            first_ref[0:SUB, n * tile : (n + 1) * tile] = product
        else:
            second_ref[:, n * tile - half : (n + 1) * tile - half] = product


def project_kernel(gain_ref, *refs):
    rows, weights = refs[:RING], refs[RING:-7]
    next_first, next_second, last_first, last_second, own_ref, own_squares, left = refs[-7:]
    half = next_first.shape[1]
    left[...], squares = left_side(gain_ref, rows, (1, 3, 0))
    next_first[SUB:, :] = tail_rows(squares[:, 0:SUB], half)
    last_first[SUB:, :] = tail_rows(squares[:, SUB : 2 * SUB], half)
    own_squares[...] = jnp.broadcast_to(squares[:, 2 * SUB :], own_squares.shape)
    tile = 256
    for n in range(2 * half // tile):
        span = slice(n * tile, (n + 1) * tile)
        right = jnp.concatenate([w[:, span] for w in weights], axis=0)
        product = jnp.dot(left[...], right, preferred_element_type=f32)
        own_ref[:, span] = product[2 * SUB :]
        if n * tile < half:
            next_first[0:SUB, span] = product[0:SUB].astype(bf16)
            last_first[0:SUB, span] = product[SUB : 2 * SUB].astype(bf16)
        else:
            span = slice(n * tile - half, (n + 1) * tile - half)
            next_second[:, span] = product[0:SUB].astype(bf16)
            last_second[:, span] = product[SUB : 2 * SUB].astype(bf16)


def merge_kernel(next_first, last_second, got_first, got_second, next_ref, last_ref):
    next_ref[0:SUB, :] = (next_first[0:SUB, :].astype(f32) + got_first[0:SUB, :].astype(f32)).astype(bf16)
    squares = tail_squares(next_first) + tail_squares(got_first)
    next_ref[SUB:, :] = tail_rows(squares, next_ref.shape[1])
    last_ref[...] = (last_second[...].astype(f32) + got_second[...].astype(f32)).astype(bf16)


def finish_kernel(channels, own_ref, own_squares, next_first, next_second, last_first, last_second, out_ref):
    half = next_first.shape[1]
    squares = own_squares[0:1, :] + tail_squares(next_first) + tail_squares(last_first)
    scale = lax.rsqrt(squares / channels + epsilon)
    column = jnp.broadcast_to(scale, (SUB, SUB)).T[:, 0:1]
    first = own_ref[:, :half] + next_first[0:SUB, :].astype(f32) + last_first[0:SUB, :].astype(f32)
    second = own_ref[:, half:] + next_second[...].astype(f32) + last_second[...].astype(f32)
    out_ref[:, :half] = (first * column).astype(bf16)
    out_ref[:, half:] = (second * column).astype(bf16)


def ring_pairs(shift, gather):
    pairs = []
    for y in range(RING):
        for x in range(RING):
            for core in range(2):
                if (core == 0) == gather:
                    there = y * RING + (x + shift) % RING
                else:
                    there = ((y + shift) % RING) * RING + x
                pairs.append(((y * RING + x) * 2 + core, there * 2 + core))
    return pairs


def ring(value, shift, gather):
    return lax.ppermute(value, ("head", "batch"), ring_pairs(shift, gather))


def body(
    ssm_input, gate_input, b_proj, c_proj, step_size, log_decay, skip_gain, norm_gain, out_weight
):
    tokens, channels = ssm_input.shape
    width = out_weight.shape[1]
    blocks = tokens // BLOCK
    seq_count = lax.axis_size("seq")
    core, u, v = ring_place()
    following = RING - 1
    weight_before, weight_after = ring(out_weight, 1, True), ring(out_weight, following, True)

    params = pltpu.CompilerParams(vmem_limit_bytes=24 * 1024 * 1024)
    near = pl.BlockSpec(memory_space=pltpu.VMEM)

    def hold(*values):
        return [pltpu.with_memory_space_constraint(value, pltpu.VMEM) for value in values]

    def far(value):
        return pltpu.with_memory_space_constraint(value, pltpu.HBM)

    payload = channels + 3 * PAD
    ssm_columns, gate_columns = ssm_input.T, gate_input.T
    prefix, total, cum, factor, b_own, c_own = pl.pallas_call(
        state_kernel,
        in_specs=[near, pl.BlockSpec(memory_space=pltpu.HBM), pl.BlockSpec(memory_space=pltpu.HBM), near, near],
        out_specs=[near] * 6,
        out_shape=[
            pltpu.VMEM((blocks, channels, STATE), bf16),
            pltpu.VMEM((payload, STATE), bf16),
            pltpu.VMEM((PAD, tokens), f32),
            pltpu.VMEM((PAD, tokens), f32),
            pltpu.VMEM((tokens, STATE), bf16),
            pltpu.VMEM((tokens, STATE), bf16),
        ],
        scratch_shapes=[pltpu.SemaphoreType.DMA((2,))],
        compiler_params=params,
        name="state",
    )(*hold(ssm_columns), far(b_proj), far(c_proj), *hold(step_size, log_decay))

    totals = [
        lax.ppermute(total, "seq", [(k, k + s) for k in range(seq_count - s)]) for s in range(1, seq_count)
    ]

    local = pl.pallas_call(
        within_kernel,
        in_specs=[pl.BlockSpec(memory_space=pltpu.SMEM)] + [near] * 6,
        out_specs=near,
        out_shape=pltpu.VMEM((channels, tokens), f32),
        compiler_params=params,
        name="within",
    )(skip_gain, *hold(ssm_columns, b_own, c_own, cum, step_size, prefix))

    local, weight_before, weight_after = lax.optimization_barrier((local, weight_before, weight_after))
    middle = channels // 2
    upper, lower = weight_before[:middle], weight_after[middle:]
    upper, lower = ring(upper, 1, True), ring(lower, following, True)
    weights = [out_weight, weight_before, upper, lower, weight_after]

    quarter = tokens // RING
    gated = pl.pallas_call(
        gate_kernel,
        in_specs=[near] * (4 + seq_count - 1),
        out_specs=[near] * RING,
        out_shape=[pltpu.VMEM((channels, quarter), bf16)] * RING,
        compiler_params=params,
        name="gate",
    )(*hold(local, gate_columns, c_own, factor, *totals))

    rows = [gated[0]] + [ring(gated[s], s, True) for s in range(1, RING)]

    half = width // 2
    with_tail, without = pltpu.VMEM((SUB + EXTRA, half), bf16), pltpu.VMEM((SUB, half), bf16)
    operands = hold(norm_gain.reshape(-1, SUB), *rows, *weights)
    opposite_first, opposite_second = pl.pallas_call(
        opposite_kernel,
        in_specs=[near] * len(operands),
        out_specs=[near] * 2,
        scratch_shapes=[pltpu.VMEM((SUB, RING * channels), bf16)],
        out_shape=[with_tail, without],
        compiler_params=params,
        name="opposite",
    )(*operands)
    got_first = ring(opposite_first, 1, False)
    got_second = ring(opposite_second, following, False)
    next_first, next_second, last_first, last_second, own, own_squares = pl.pallas_call(
        project_kernel,
        in_specs=[near] * len(operands),
        out_specs=[near] * 6,
        scratch_shapes=[pltpu.VMEM((3 * SUB, RING * channels), bf16)],
        out_shape=[with_tail, without, with_tail, without, pltpu.VMEM((SUB, width), f32), pltpu.VMEM((PAD, SUB), f32)],
        compiler_params=params,
        name="project",
    )(*operands)
    sent_second = ring(next_second, 1, False)
    sent_first = ring(last_first, following, False)
    next_sum, last_sum = pl.pallas_call(
        merge_kernel,
        in_specs=[near] * 4,
        out_specs=[near] * 2,
        out_shape=[with_tail, without],
        compiler_params=params,
        name="merge",
    )(*hold(next_first, last_second, got_first, got_second))
    from_before = ring(next_sum, 1, False)
    from_after = ring(last_sum, following, False)

    return pl.pallas_call(
        lambda *refs: finish_kernel(HEAD_COUNT * HEAD_DIM, *refs),
        in_specs=[near] * 6,
        out_specs=pl.BlockSpec((SUB, width), lambda: (0, 0)),
        out_shape=jax.ShapeDtypeStruct((SUB, width), bf16),
        compiler_params=params,
        name="finish",
    )(*hold(own, own_squares, from_before, sent_second, sent_first, from_after))


def solution(mesh):
    in_specs = (
        P(("batch", "seq"), "head"),
        P(("batch", "seq"), "head"),
        P(("batch", "seq"), None),
        P(("batch", "seq"), None),
        P("head", ("batch", "seq")),
        P("head", ("batch", "seq")),
        P("head"),
        P(),
        P("head", None),
    )
    out_specs = P(("batch", "seq", "head"), None)

    return jax.shard_map(body, mesh=mesh, in_specs=in_specs, out_specs=out_specs, check_vma=False)
```

profile of v0, /device:TPU:6, one launch (start us, length us, event | category | flops | bytes accessed | tf_op | source)
XLA Modules:
  0.0 93.1 jit_solution(10940071631327243479)
XLA Ops:
  0.0 2.2 %collective-permute-start = (bf16[320,2560]{1,0:T(8,128)(2,1)}, bf16[320,2560]{1,0:T(8,128)(2,1)S(1)}, u32[]{:S(2)}, u32[]{:S(2)}) collective-permute-start(bf16[320,2560]{1,0:T(8,128)(2,1)} %refs_4_.3), channel_id=1, source_target_pairs={{0,2},{1,9},{2,4},{3,11},{4,6},{5,13},{6,0},{7,15},{8,10},{9,17},{... | collective-permute-start | bytes 4915208 | tf_op jit(solution)/shard_map/ppermute | solution.py:273
  2.2 1.3 %copy-done.1 = bf16[2048,320]{0,1:T(8,128)(2,1)S(1)} copy-done((bf16[2048,320]{0,1:T(8,128)(2,1)S(1)}, bf16[2048,320]{0,1:T(8,128)(2,1)}, u32[]{:S(2)}) %copy-start.1) | copy-done | bytes 1310744
  3.5 0.8 copy-done.3
  4.3 0.8 copy-done.5
  5.2 1.7 %state.1 = (bf16[8,320,128]{2,1,0:T(8,128)(2,1)S(1)}, bf16[344,128]{1,0:T(8,128)(2,1)S(1)}, f32[8,2048]{1,0:T(8,128)S(1)}, f32[8,2048]{1,0:T(8,128)S(1)}, bf16[2...) custom-call(bf16[320,2048]{1,0:T(8,128)(2,1)S(1)} %bitcast.3, bf16[2048,1024]{1,0:T(8,128)(2,1)} %b_hbm.1, ...), custom_call_target="tpu_custom_call" | custom-call | tf_op jit(solution)/shard_map/state/pallas_call | solution.py:298
  6.9 4.2 %within.1.out_ref = f32[320,2048]{1,0:T(8,128)S(1)} custom-call(f32[5]{0:T(128)S(1)} %copy-done.6, bf16[320,2048]{1,0:T(8,128)(2,1)S(1)} %bitcast.4, bf16[2048,128]{1,0:T(8,128)(2,1)S(1)} %get-tuple-element.28.b_ref, bf16[2048,128]{1,0:T(8,128)(2,1)S(1)} %get-tuple-element.29.c_ref, f32[8,2048]{1,0:T(8,128)S(1)} %get-tuple-element.30.cum_ref, ...), custom_call_target="tpu_custom_call" | custom-call | tf_op jit(solution)/shard_map/within/pallas_call | solution.py:319
  11.1 10.2 %collective-permute-done.refs_5_ = bf16[320,2560]{1,0:T(8,128)(2,1)S(1)} collective-permute-done((bf16[320,2560]{1,0:T(8,128)(2,1)}, bf16[320,2560]{1,0:T(8,128)(2,1)S(1)}, u32[]{:S(2)}, u32[]{:S(2)}) %collective-permute-start) | collective-permute-done | bytes 1638432 | tf_op jit(solution)/shard_map/ppermute | solution.py:273
  21.3 3.4 %collective-permute-done.1.refs_8_ = bf16[320,2560]{1,0:T(8,128)(2,1)S(1)} collective-permute-done((bf16[320,2560]{1,0:T(8,128)(2,1)}, bf16[320,2560]{1,0:T(8,128)(2,1)S(1)}, u32[]{:S(2)}, u32[]{:S(2)}) %collective-permute-start.1) | collective-permute-done | bytes 1638432 | tf_op jit(solution)/shard_map/ppermute | solution.py:273
  24.9 2.1 %collective-permute-start.13 = (bf16[160,2560]{1,0:T(8,128)(2,1)S(1)}, bf16[160,2560]{1,0:T(8,128)(2,1)S(1)}, u32[]{:S(2)}, u32[]{:S(2)}) collective-permute-start(bf16[160,2560]{1,0:T(8,128)(2,1)S(1)} %slice.7), channel_id=1, source_target_pairs={{0,6},{1,25},{2,0},{3,27},{4,2},{5,29},{6,4},{7,31},{8,14},{9,1},{... | collective-permute-start | bytes 2457608 | tf_op jit(solution)/shard_map/ppermute | solution.py:273
  27.0 2.1 %collective-permute-start.2 = (bf16[344,128]{1,0:T(8,128)(2,1)S(1)}, bf16[344,128]{1,0:T(8,128)(2,1)S(1)}, u32[]{:S(2)}, u32[]{:S(2)}) collective-permute-start(bf16[344,128]{1,0:T(8,128)(2,1)S(1)} %get-tuple-element.34), channel_id=1, source_target_pairs={{0,32},{32,64},{64,96},{96,128},{128,160},{160,192},{192,224},{1,3... | collective-permute-start | bytes 264200 | tf_op jit(solution)/shard_map/ppermute | solution.py:316
  29.1 5.2 %collective-permute-start.3 = (bf16[344,128]{1,0:T(8,128)(2,1)S(1)}, bf16[344,128]{1,0:T(8,128)(2,1)S(1)}, u32[]{:S(2)}, u32[]{:S(2)}) collective-permute-start(bf16[344,128]{1,0:T(8,128)(2,1)S(1)} %get-tuple-element.34), channel_id=1, source_target_pairs={{0,64},{32,96},{64,128},{96,160},{128,192},{160,224},{1,65},{33,97... | collective-permute-start | bytes 264200 | tf_op jit(solution)/shard_map/ppermute | solution.py:316
  34.3 5.9 %collective-permute-start.4 = (bf16[344,128]{1,0:T(8,128)(2,1)S(1)}, bf16[344,128]{1,0:T(8,128)(2,1)S(1)}, u32[]{:S(2)}, u32[]{:S(2)}) collective-permute-start(bf16[344,128]{1,0:T(8,128)(2,1)S(1)} %get-tuple-element.34), channel_id=1, source_target_pairs={{0,96},{32,128},{64,160},{96,192},{128,224},{1,97},{33,129},{65,16... | collective-permute-start | bytes 264200 | tf_op jit(solution)/shard_map/ppermute | solution.py:316
  40.3 2.4 %collective-permute-start.5 = (bf16[344,128]{1,0:T(8,128)(2,1)S(1)}, bf16[344,128]{1,0:T(8,128)(2,1)S(1)}, u32[]{:S(2)}, u32[]{:S(2)}) collective-permute-start(bf16[344,128]{1,0:T(8,128)(2,1)S(1)} %get-tuple-element.34), channel_id=1, source_target_pairs={{0,128},{32,160},{64,192},{96,224},{1,129},{33,161},{65,193},{97,2... | collective-permute-start | bytes 264200 | tf_op jit(solution)/shard_map/ppermute | solution.py:316
  42.7 5.0 %collective-permute-start.6 = (bf16[344,128]{1,0:T(8,128)(2,1)S(1)}, bf16[344,128]{1,0:T(8,128)(2,1)S(1)}, u32[]{:S(2)}, u32[]{:S(2)}) collective-permute-start(bf16[344,128]{1,0:T(8,128)(2,1)S(1)} %get-tuple-element.34), channel_id=1, source_target_pairs={{0,160},{32,192},{64,224},{1,161},{33,193},{65,225},{2,162},{34,19... | collective-permute-start | bytes 264200 | tf_op jit(solution)/shard_map/ppermute | solution.py:316
  47.7 2.2 %collective-permute-start.7 = (bf16[344,128]{1,0:T(8,128)(2,1)S(1)}, bf16[344,128]{1,0:T(8,128)(2,1)S(1)}, u32[]{:S(2)}, u32[]{:S(2)}) collective-permute-start(bf16[344,128]{1,0:T(8,128)(2,1)S(1)} %get-tuple-element.34), channel_id=1, source_target_pairs={{0,192},{32,224},{1,193},{33,225},{2,194},{34,226},{3,195},{35,227... | collective-permute-start | bytes 264200 | tf_op jit(solution)/shard_map/ppermute | solution.py:316
  49.8 1.3 %collective-permute-start.8 = (bf16[344,128]{1,0:T(8,128)(2,1)S(1)}, bf16[344,128]{1,0:T(8,128)(2,1)S(1)}, u32[]{:S(2)}, u32[]{:S(2)}) collective-permute-start(bf16[344,128]{1,0:T(8,128)(2,1)S(1)} %get-tuple-element.34), channel_id=1, source_target_pairs={{0,224},{1,225},{2,226},{3,227},{4,228},{5,229},{6,230},{7,231},{8... | collective-permute-start | bytes 264200 | tf_op jit(solution)/shard_map/ppermute | solution.py:316
  51.1 2.9 %collective-permute-done.6.refs_4_ = bf16[344,128]{1,0:T(8,128)(2,1)S(1)} collective-permute-done((bf16[344,128]{1,0:T(8,128)(2,1)S(1)}, bf16[344,128]{1,0:T(8,128)(2,1)S(1)}, u32[]{:S(2)}, u32[]{:S(2)}) %collective-permute-start.6) | collective-permute-done | bytes 88096 | tf_op jit(solution)/shard_map/ppermute | solution.py:316
  54.0 1.1 %collective-permute-done.7.refs_5_ = bf16[344,128]{1,0:T(8,128)(2,1)S(1)} collective-permute-done((bf16[344,128]{1,0:T(8,128)(2,1)S(1)}, bf16[344,128]{1,0:T(8,128)(2,1)S(1)}, u32[]{:S(2)}, u32[]{:S(2)}) %collective-permute-start.7) | collective-permute-done | bytes 88096 | tf_op jit(solution)/shard_map/ppermute | solution.py:316
  55.1 0.9 %collective-permute-done.8.refs_6_ = bf16[344,128]{1,0:T(8,128)(2,1)S(1)} collective-permute-done((bf16[344,128]{1,0:T(8,128)(2,1)S(1)}, bf16[344,128]{1,0:T(8,128)(2,1)S(1)}, u32[]{:S(2)}, u32[]{:S(2)}) %collective-permute-start.8) | collective-permute-done | bytes 88096 | tf_op jit(solution)/shard_map/ppermute | solution.py:316
  56.1 1.3 %gate.1 = (bf16[320,512]{1,0:T(8,128)(2,1)S(1)}, bf16[320,512]{1,0:T(8,128)(2,1)S(1)}, bf16[320,512]{1,0:T(8,128)(2,1)S(1)}, bf16[320,512]{1,0:T(8,128)(2,1)S(1)}) custom-call(f32[320,2048]{1,0:T(8,128)S(1)} %within.1.out_ref, bf16[320,2048]{1,0:T(8,128)(2,1)S(1)} %bitcast.5, bf16[2048,128]{1,0:T(8,128)(2,1)S(1)} %get-tuple-element.29.c_ref, ...), custom_call_target="tpu_custom_call" | custom-call | tf_op jit(solution)/shard_map/gate/pallas_call | solution.py:335
  57.4 1.2 %collective-permute-start.10 = (bf16[320,512]{1,0:T(8,128)(2,1)S(1)}, bf16[320,512]{1,0:T(8,128)(2,1)S(1)}, u32[]{:S(2)}, u32[]{:S(2)}) collective-permute-start(bf16[320,512]{1,0:T(8,128)(2,1)S(1)} %get-tuple-element.37), channel_id=1, source_target_pairs={{0,4},{1,17},{2,6},{3,19},{4,0},{5,21},{6,2},{7,23},{8,12},{9,25},... | collective-permute-start | bytes 983048 | tf_op jit(solution)/shard_map/ppermute | solution.py:273
  58.6 3.2 %collective-permute-start.9 = (bf16[320,512]{1,0:T(8,128)(2,1)S(1)}, bf16[320,512]{1,0:T(8,128)(2,1)S(1)}, u32[]{:S(2)}, u32[]{:S(2)}) collective-permute-start(bf16[320,512]{1,0:T(8,128)(2,1)S(1)} %get-tuple-element.36), channel_id=1, source_target_pairs={{0,2},{1,9},{2,4},{3,11},{4,6},{5,13},{6,0},{7,15},{8,10},{9,17},{... | collective-permute-start | bytes 983048 | tf_op jit(solution)/shard_map/ppermute | solution.py:273
  61.9 4.3 %collective-permute-done.10.refs_2_ = bf16[320,512]{1,0:T(8,128)(2,1)S(1)} collective-permute-done((bf16[320,512]{1,0:T(8,128)(2,1)S(1)}, bf16[320,512]{1,0:T(8,128)(2,1)S(1)}, u32[]{:S(2)}, u32[]{:S(2)}) %collective-permute-start.10) | collective-permute-done | bytes 327712 | tf_op jit(solution)/shard_map/ppermute | solution.py:273
  66.2 3.4 %collective-permute-done.11.refs_3_ = bf16[320,512]{1,0:T(8,128)(2,1)S(1)} collective-permute-done((bf16[320,512]{1,0:T(8,128)(2,1)S(1)}, bf16[320,512]{1,0:T(8,128)(2,1)S(1)}, u32[]{:S(2)}, u32[]{:S(2)}) %collective-permute-start.11) | collective-permute-done | bytes 327712 | tf_op jit(solution)/shard_map/ppermute | solution.py:273
  69.6 1.2 %opposite.1 = (bf16[136,1280]{1,0:T(8,128)(2,1)S(1)}, bf16[128,1280]{1,0:T(8,128)(2,1)S(1)}) custom-call(f32[40,128]{1,0:T(8,128)S(1)} %bitcast.6, bf16[320,512]{1,0:T(8,128)(2,1)S(1)} %get-tuple-element.35.refs_0_, bf16[320,512]{1,0:T(8,128)(2,1)S(1)} %collective-permute-done.9.refs_1_, bf16[320,512]{1,0:T(8,128)(2,1)S(1)} %collective-permute-done.10.refs_2_, ...), custom_call_target="tpu_custom_call" | custom-call | tf_op jit(solution)/shard_map/opposite/pallas_call | solution.py:349
  71.4 3.0 %collective-permute-start.15 = (bf16[128,1280]{1,0:T(8,128)(2,1)S(1)}, bf16[128,1280]{1,0:T(8,128)(2,1)S(1)}, u32[]{:S(2)}, u32[]{:S(2)}) collective-permute-start(bf16[128,1280]{1,0:T(8,128)(2,1)S(1)} %get-tuple-element.46), channel_id=1, source_target_pairs={{0,24},{1,7},{2,26},{3,1},{4,28},{5,3},{6,30},{7,5},{8,0},{9,15},{... | collective-permute-start | bytes 983048 | tf_op jit(solution)/shard_map/ppermute | solution.py:273
  74.3 2.9 %project.1 = (bf16[136,1280]{1,0:T(8,128)(2,1)S(1)}, bf16[128,1280]{1,0:T(8,128)(2,1)S(1)}, bf16[136,1280]{1,0:T(8,128)(2,1)S(1)}, bf16[128,1280]{1,0:T(8,128)(2...) custom-call(f32[40,128]{1,0:T(8,128)S(1)} %bitcast.7, bf16[320,512]{1,0:T(8,128)(2,1)S(1)} %get-tuple-element.35.refs_0_, ...), custom_call_target="tpu_custom_call" | custom-call | tf_op jit(solution)/shard_map/project/pallas_call | solution.py:360
  77.9 1.1 %collective-permute-done.15.got_second = bf16[128,1280]{1,0:T(8,128)(2,1)S(1)} collective-permute-done((bf16[128,1280]{1,0:T(8,128)(2,1)S(1)}, bf16[128,1280]{1,0:T(8,128)(2,1)S(1)}, u32[]{:S(2)}, u32[]{:S(2)}) %collective-permute-start.15) | collective-permute-done | bytes 327712 | tf_op jit(solution)/shard_map/ppermute | solution.py:273
  80.2 1.5 %collective-permute-start.17 = (bf16[128,1280]{1,0:T(8,128)(2,1)S(1)}, bf16[128,1280]{1,0:T(8,128)(2,1)S(1)}, u32[]{:S(2)}, u32[]{:S(2)}) collective-permute-start(bf16[128,1280]{1,0:T(8,128)(2,1)S(1)} %get-tuple-element.48), channel_id=1, source_target_pairs={{0,8},{1,3},{2,10},{3,5},{4,12},{5,7},{6,14},{7,1},{8,16},{9,11},{... | collective-permute-start | bytes 983048 | tf_op jit(solution)/shard_map/ppermute | solution.py:273
  81.6 1.8 %collective-permute-start.19 = (bf16[128,1280]{1,0:T(8,128)(2,1)S(1)}, bf16[128,1280]{1,0:T(8,128)(2,1)S(1)}, u32[]{:S(2)}, u32[]{:S(2)}) collective-permute-start(bf16[128,1280]{1,0:T(8,128)(2,1)S(1)} %get-tuple-element.50), channel_id=1, source_target_pairs={{0,24},{1,7},{2,26},{3,1},{4,28},{5,3},{6,30},{7,5},{8,0},{9,15},{... | collective-permute-start | bytes 983048 | tf_op jit(solution)/shard_map/ppermute | solution.py:273
  83.4 8.5 %collective-permute-done.17.refs_3_ = bf16[128,1280]{1,0:T(8,128)(2,1)S(1)} collective-permute-done((bf16[128,1280]{1,0:T(8,128)(2,1)S(1)}, bf16[128,1280]{1,0:T(8,128)(2,1)S(1)}, u32[]{:S(2)}, u32[]{:S(2)}) %collective-permute-start.17) | collective-permute-done | bytes 327712 | tf_op jit(solution)/shard_map/ppermute | solution.py:273
  91.9 1.2 %finish.1 = bf16[128,2560]{1,0:T(8,128)(2,1)} custom-call(f32[128,2560]{1,0:T(8,128)S(1)} %get-tuple-element.41.refs_0_, f32[8,128]{1,0:T(8,128)S(1)} %get-tuple-element.42.refs_1_, bf16[136,1280]{1,0:T(8,128)(2,1)S(1)} %collective-permute-done.16.refs_2_, bf16[128,1280]{1,0:T(8,128)(2,1)S(1)} %collective-permute-done.17.refs_3_, ...), custom_call_target="tpu_custom_call" | custom-call | tf_op jit(solution)/shard_map/finish/pallas_call | solution.py:382
  (31 shorter events, 2.7 us)
Async XLA Ops:
  0.0 21.3 %collective-permute-start = (bf16[320,2560]{1,0:T(8,128)(2,1)}, bf16[320,2560]{1,0:T(8,128)(2,1)S(1)}, u32[]{:S(2)}, u32[]{:S(2)}) collective-permute-start(bf16[320,2560]{1,0:T(8,128)(2,1)} %refs_4_.3), channel_id=1, source_target_pairs={{0,2},{1,9},{2,4},{3,11},{4,6},{5,13},{6,0},{7,15},{8,10},{9,17},{... | collective-permute-start | bytes 4915208 | tf_op jit(solution)/shard_map/ppermute | solution.py:273
  2.2 22.5 %collective-permute-start.1 = (bf16[320,2560]{1,0:T(8,128)(2,1)}, bf16[320,2560]{1,0:T(8,128)(2,1)S(1)}, u32[]{:S(2)}, u32[]{:S(2)}) collective-permute-start(bf16[320,2560]{1,0:T(8,128)(2,1)} %refs_4_.3), channel_id=1, source_target_pairs={{0,6},{1,25},{2,0},{3,27},{4,2},{5,29},{6,4},{7,31},{8,14},{9,1},{... | collective-permute-start | bytes 4915208 | tf_op jit(solution)/shard_map/ppermute | solution.py:273
  2.2 1.3 %copy-start.1 = (bf16[2048,320]{0,1:T(8,128)(2,1)S(1)}, bf16[2048,320]{0,1:T(8,128)(2,1)}, u32[]{:S(2)}) copy-start(bf16[2048,320]{0,1:T(8,128)(2,1)} %param.9) | copy-start | bytes 3932164
  3.5 0.8 copy-start.3
  4.3 0.8 copy-start.5
  5.2 1.7 %copy-start.6 = (f32[5]{0:T(128)S(1)}, f32[5]{0:T(128)}, u32[]{:S(2)}) copy-start(f32[5]{0:T(128)} %skip_ref.1) | copy-start | bytes 64
  11.1 44.9 %copy-start.2 = (bf16[2048,320]{0,1:T(8,128)(2,1)S(1)}, bf16[2048,320]{0,1:T(8,128)(2,1)}, u32[]{:S(2)}) copy-start(bf16[2048,320]{0,1:T(8,128)(2,1)} %param.10) | copy-start | bytes 3932164
  24.8 44.8 %collective-permute-start.12 = (bf16[160,2560]{1,0:T(8,128)(2,1)S(1)}, bf16[160,2560]{1,0:T(8,128)(2,1)S(1)}, u32[]{:S(2)}, u32[]{:S(2)}) collective-permute-start(bf16[160,2560]{1,0:T(8,128)(2,1)S(1)} %slice.6), channel_id=1, source_target_pairs={{0,2},{1,9},{2,4},{3,11},{4,6},{5,13},{6,0},{7,15},{8,10},{9,17},{... | collective-permute-start | bytes 2457608 | tf_op jit(solution)/shard_map/ppermute | solution.py:273
  24.9 44.6 %collective-permute-start.13 = (bf16[160,2560]{1,0:T(8,128)(2,1)S(1)}, bf16[160,2560]{1,0:T(8,128)(2,1)S(1)}, u32[]{:S(2)}, u32[]{:S(2)}) collective-permute-start(bf16[160,2560]{1,0:T(8,128)(2,1)S(1)} %slice.7), channel_id=1, source_target_pairs={{0,6},{1,25},{2,0},{3,27},{4,2},{5,29},{6,4},{7,31},{8,14},{9,1},{... | collective-permute-start | bytes 2457608 | tf_op jit(solution)/shard_map/ppermute | solution.py:273
  27.0 13.3 %collective-permute-start.2 = (bf16[344,128]{1,0:T(8,128)(2,1)S(1)}, bf16[344,128]{1,0:T(8,128)(2,1)S(1)}, u32[]{:S(2)}, u32[]{:S(2)}) collective-permute-start(bf16[344,128]{1,0:T(8,128)(2,1)S(1)} %get-tuple-element.34), channel_id=1, source_target_pairs={{0,32},{32,64},{64,96},{96,128},{128,160},{160,192},{192,224},{1,3... | collective-permute-start | bytes 264200 | tf_op jit(solution)/shard_map/ppermute | solution.py:316
  29.1 13.5 %collective-permute-start.3 = (bf16[344,128]{1,0:T(8,128)(2,1)S(1)}, bf16[344,128]{1,0:T(8,128)(2,1)S(1)}, u32[]{:S(2)}, u32[]{:S(2)}) collective-permute-start(bf16[344,128]{1,0:T(8,128)(2,1)S(1)} %get-tuple-element.34), channel_id=1, source_target_pairs={{0,64},{32,96},{64,128},{96,160},{128,192},{160,224},{1,65},{33,97... | collective-permute-start | bytes 264200 | tf_op jit(solution)/shard_map/ppermute | solution.py:316
  34.3 13.3 %collective-permute-start.4 = (bf16[344,128]{1,0:T(8,128)(2,1)S(1)}, bf16[344,128]{1,0:T(8,128)(2,1)S(1)}, u32[]{:S(2)}, u32[]{:S(2)}) collective-permute-start(bf16[344,128]{1,0:T(8,128)(2,1)S(1)} %get-tuple-element.34), channel_id=1, source_target_pairs={{0,96},{32,128},{64,160},{96,192},{128,224},{1,97},{33,129},{65,16... | collective-permute-start | bytes 264200 | tf_op jit(solution)/shard_map/ppermute | solution.py:316
  40.3 9.5 %collective-permute-start.5 = (bf16[344,128]{1,0:T(8,128)(2,1)S(1)}, bf16[344,128]{1,0:T(8,128)(2,1)S(1)}, u32[]{:S(2)}, u32[]{:S(2)}) collective-permute-start(bf16[344,128]{1,0:T(8,128)(2,1)S(1)} %get-tuple-element.34), channel_id=1, source_target_pairs={{0,128},{32,160},{64,192},{96,224},{1,129},{33,161},{65,193},{97,2... | collective-permute-start | bytes 264200 | tf_op jit(solution)/shard_map/ppermute | solution.py:316
  42.7 11.3 %collective-permute-start.6 = (bf16[344,128]{1,0:T(8,128)(2,1)S(1)}, bf16[344,128]{1,0:T(8,128)(2,1)S(1)}, u32[]{:S(2)}, u32[]{:S(2)}) collective-permute-start(bf16[344,128]{1,0:T(8,128)(2,1)S(1)} %get-tuple-element.34), channel_id=1, source_target_pairs={{0,160},{32,192},{64,224},{1,161},{33,193},{65,225},{2,162},{34,19... | collective-permute-start | bytes 264200 | tf_op jit(solution)/shard_map/ppermute | solution.py:316
  47.7 7.4 %collective-permute-start.7 = (bf16[344,128]{1,0:T(8,128)(2,1)S(1)}, bf16[344,128]{1,0:T(8,128)(2,1)S(1)}, u32[]{:S(2)}, u32[]{:S(2)}) collective-permute-start(bf16[344,128]{1,0:T(8,128)(2,1)S(1)} %get-tuple-element.34), channel_id=1, source_target_pairs={{0,192},{32,224},{1,193},{33,225},{2,194},{34,226},{3,195},{35,227... | collective-permute-start | bytes 264200 | tf_op jit(solution)/shard_map/ppermute | solution.py:316
  49.8 6.2 %collective-permute-start.8 = (bf16[344,128]{1,0:T(8,128)(2,1)S(1)}, bf16[344,128]{1,0:T(8,128)(2,1)S(1)}, u32[]{:S(2)}, u32[]{:S(2)}) collective-permute-start(bf16[344,128]{1,0:T(8,128)(2,1)S(1)} %get-tuple-element.34), channel_id=1, source_target_pairs={{0,224},{1,225},{2,226},{3,227},{4,228},{5,229},{6,230},{7,231},{8... | collective-permute-start | bytes 264200 | tf_op jit(solution)/shard_map/ppermute | solution.py:316
  56.0 13.5 %copy-start = (bf16[320,2560]{1,0:T(8,128)(2,1)S(1)}, bf16[320,2560]{1,0:T(8,128)(2,1)}, u32[]{:S(2)}) copy-start(bf16[320,2560]{1,0:T(8,128)(2,1)} %refs_4_.3) | copy-start | bytes 4915204
  56.0 13.5 %copy-start.4 = (f32[5120]{0:T(1024)S(1)}, f32[5120]{0:T(1024)}, u32[]{:S(2)}) copy-start(f32[5120]{0:T(1024)} %param.16) | copy-start | bytes 61444
  57.4 8.8 %collective-permute-start.10 = (bf16[320,512]{1,0:T(8,128)(2,1)S(1)}, bf16[320,512]{1,0:T(8,128)(2,1)S(1)}, u32[]{:S(2)}, u32[]{:S(2)}) collective-permute-start(bf16[320,512]{1,0:T(8,128)(2,1)S(1)} %get-tuple-element.37), channel_id=1, source_target_pairs={{0,4},{1,17},{2,6},{3,19},{4,0},{5,21},{6,2},{7,23},{8,12},{9,25},... | collective-permute-start | bytes 983048 | tf_op jit(solution)/shard_map/ppermute | solution.py:273
  58.6 10.9 %collective-permute-start.11 = (bf16[320,512]{1,0:T(8,128)(2,1)S(1)}, bf16[320,512]{1,0:T(8,128)(2,1)S(1)}, u32[]{:S(2)}, u32[]{:S(2)}) collective-permute-start(bf16[320,512]{1,0:T(8,128)(2,1)S(1)} %get-tuple-element.38), channel_id=1, source_target_pairs={{0,6},{1,25},{2,0},{3,27},{4,2},{5,29},{6,4},{7,31},{8,14},{9,1},{... | collective-permute-start | bytes 983048 | tf_op jit(solution)/shard_map/ppermute | solution.py:273
  58.6 10.9 %collective-permute-start.9 = (bf16[320,512]{1,0:T(8,128)(2,1)S(1)}, bf16[320,512]{1,0:T(8,128)(2,1)S(1)}, u32[]{:S(2)}, u32[]{:S(2)}) collective-permute-start(bf16[320,512]{1,0:T(8,128)(2,1)S(1)} %get-tuple-element.36), channel_id=1, source_target_pairs={{0,2},{1,9},{2,4},{3,11},{4,6},{5,13},{6,0},{7,15},{8,10},{9,17},{... | collective-permute-start | bytes 983048 | tf_op jit(solution)/shard_map/ppermute | solution.py:273
  70.8 8.8 %collective-permute-start.14 = (bf16[136,1280]{1,0:T(8,128)(2,1)S(1)}, bf16[136,1280]{1,0:T(8,128)(2,1)S(1)}, u32[]{:S(2)}, u32[]{:S(2)}) collective-permute-start(bf16[136,1280]{1,0:T(8,128)(2,1)S(1)} %get-tuple-element.45), channel_id=1, source_target_pairs={{0,8},{1,3},{2,10},{3,5},{4,12},{5,7},{6,14},{7,1},{8,16},{9,11},{... | collective-permute-start | bytes 1044488 | tf_op jit(solution)/shard_map/ppermute | solution.py:273
  71.4 7.6 %collective-permute-start.15 = (bf16[128,1280]{1,0:T(8,128)(2,1)S(1)}, bf16[128,1280]{1,0:T(8,128)(2,1)S(1)}, u32[]{:S(2)}, u32[]{:S(2)}) collective-permute-start(bf16[128,1280]{1,0:T(8,128)(2,1)S(1)} %get-tuple-element.46), channel_id=1, source_target_pairs={{0,24},{1,7},{2,26},{3,1},{4,28},{5,3},{6,30},{7,5},{8,0},{9,15},{... | collective-permute-start | bytes 983048 | tf_op jit(solution)/shard_map/ppermute | solution.py:273
  77.2 14.7 %collective-permute-start.18 = (bf16[136,1280]{1,0:T(8,128)(2,1)S(1)}, bf16[136,1280]{1,0:T(8,128)(2,1)S(1)}, u32[]{:S(2)}, u32[]{:S(2)}) collective-permute-start(bf16[136,1280]{1,0:T(8,128)(2,1)S(1)} %get-tuple-element.49), channel_id=1, source_target_pairs={{0,24},{1,7},{2,26},{3,1},{4,28},{5,3},{6,30},{7,5},{8,0},{9,15},{... | collective-permute-start | bytes 1044488 | tf_op jit(solution)/shard_map/ppermute | solution.py:273
  79.8 12.1 %collective-permute-start.16 = (bf16[136,1280]{1,0:T(8,128)(2,1)S(1)}, bf16[136,1280]{1,0:T(8,128)(2,1)S(1)}, u32[]{:S(2)}, u32[]{:S(2)}) collective-permute-start(bf16[136,1280]{1,0:T(8,128)(2,1)S(1)} %get-tuple-element.47), channel_id=1, source_target_pairs={{0,8},{1,3},{2,10},{3,5},{4,12},{5,7},{6,14},{7,1},{8,16},{9,11},{... | collective-permute-start | bytes 1044488 | tf_op jit(solution)/shard_map/ppermute | solution.py:273
  80.2 11.7 %collective-permute-start.17 = (bf16[128,1280]{1,0:T(8,128)(2,1)S(1)}, bf16[128,1280]{1,0:T(8,128)(2,1)S(1)}, u32[]{:S(2)}, u32[]{:S(2)}) collective-permute-start(bf16[128,1280]{1,0:T(8,128)(2,1)S(1)} %get-tuple-element.48), channel_id=1, source_target_pairs={{0,8},{1,3},{2,10},{3,5},{4,12},{5,7},{6,14},{7,1},{8,16},{9,11},{... | collective-permute-start | bytes 983048 | tf_op jit(solution)/shard_map/ppermute | solution.py:273
  81.6 10.2 %collective-permute-start.19 = (bf16[128,1280]{1,0:T(8,128)(2,1)S(1)}, bf16[128,1280]{1,0:T(8,128)(2,1)S(1)}, u32[]{:S(2)}, u32[]{:S(2)}) collective-permute-start(bf16[128,1280]{1,0:T(8,128)(2,1)S(1)} %get-tuple-element.50), channel_id=1, source_target_pairs={{0,24},{1,7},{2,26},{3,1},{4,28},{5,3},{6,30},{7,5},{8,0},{9,15},{... | collective-permute-start | bytes 983048 | tf_op jit(solution)/shard_map/ppermute | solution.py:273
where the time goes:
time: 93.4 us; the launch traced here: 93.1 us
  starting transfers between devices  40.6 us (43%)
  waiting for transfers between devices  36.4 us (39%)
  Pallas kernels  12.7 us (14%)
  local copies, waits for them, and re-layouts  3.12 us (3%)
    ppermute x13, waiting for transfers between devices, ring(): return lax.ppermute(value, ('head', 'batch'), ring_pairs(shift, gather))  31.5 us
    ppermute x7, starting transfers between devices, body(): lax.ppermute(total, 'seq', [(k, k + s) for k in range(seq_count - s)])  24 us
    ppermute x13, starting transfers between devices, ring(): return lax.ppermute(value, ('head', 'batch'), ring_pairs(shift, gather))  16.6 us
    ppermute x7, waiting for transfers between devices, body(): lax.ppermute(total, 'seq', [(k, k + s) for k in range(seq_count - s)])  4.91 us
    pallas_call x1, Pallas kernels, body(): pl.pallas_call(within_kernel, in_specs=[pl.BlockSpec(memory_space=pltpu.S...  4.21 us
    unnamed x14, local copies, waits for them, and re-layouts  3.01 us
    pallas_call x1, Pallas kernels, body(): pl.pallas_call(project_kernel, in_specs=[near] * len(operands), out_specs...  2.87 us
  transfers between devices with their start and end apart: 20, of which 10 were waited for; matrix products, arithmetic and copies ran while one was open for 0% of the time, Pallas kernels for 11%

commit v1 on v0

--- a/solution.py
+++ b/solution.py
@@ -47,15 +47,19 @@
     )
 
 
-def state_kernel(x_ref, b_hbm, c_hbm, step_ref, decay_ref, prefix_ref, total_ref, cum_ref, factor_ref, b_ref, c_ref, sems):
+def state_kernel(
+    x_hbm, b_hbm, c_hbm, step_hbm, decay_hbm, prefix_ref, total_ref, cum_ref, factor_ref, x_ref, b_ref, c_ref, step_ref, decay_ref, sems
+):
     heads, tokens = step_ref.shape
     blocks = tokens // BLOCK
     group = lax.axis_index("head") * heads * GROUPS // HEAD_COUNT
     columns = pl.ds(pl.multiple_of(group * STATE, STATE), STATE)
-    fetch_b = pltpu.make_async_copy(b_hbm.at[:, columns], b_ref, sems.at[0])
-    fetch_c = pltpu.make_async_copy(c_hbm.at[:, columns], c_ref, sems.at[1])
-    fetch_b.start()
-    fetch_c.start()
+    sources = (decay_hbm, step_hbm, x_hbm, b_hbm.at[:, columns], c_hbm.at[:, columns])
+    targets = (decay_ref, step_ref, x_ref, b_ref, c_ref)
+    fetches = [pltpu.make_async_copy(sources[k], targets[k], sems.at[k]) for k in range(5)]
+    for fetch in fetches:
+        fetch.start()
+    fetches[0].wait()
     fill = jnp.zeros((PAD - heads, BLOCK), f32)
     decay = jnp.concatenate(
         [piece for c in range(blocks) for piece in (decay_ref[:, c * BLOCK : (c + 1) * BLOCK], fill)], axis=0
@@ -71,7 +75,8 @@
         cum_ref[:, span] = cumulative
         factor_ref[:, span] = jnp.exp(cumulative + offset)
         offset = offset + cumulative[:, BLOCK - 1 :]
-    fetch_b.wait()
+    for fetch in fetches[1:4]:
+        fetch.wait()
     state = jnp.zeros((heads * HEAD_DIM, STATE), f32)
     for c in range(blocks):
         span = slice(c * BLOCK, (c + 1) * BLOCK)
@@ -91,12 +96,21 @@
     total_ref[0 : heads * HEAD_DIM, :] = state.astype(bf16)
     parts = split3(jnp.broadcast_to(offset, (PAD, STATE)))
     total_ref[heads * HEAD_DIM :, :] = jnp.concatenate(parts, axis=0)
-    fetch_c.wait()
-
-
-def within_kernel(skip_ref, x_ref, b_ref, c_ref, cum_ref, step_ref, prefix_ref, out_ref):
-    heads = step_ref.shape[0]
+    fetches[4].wait()
+
+
+def pair_kernel(total_ref, before_ref, pair_ref):
+    channels = total_ref.shape[0] - 3 * PAD
+    heads = channels // HEAD_DIM
+    logs = join3(total_ref[channels:, :], PAD)
+    decayed = per_head(jnp.exp(logs), heads, STATE) * before_ref[0:channels, :].astype(f32)
+    pair_ref[0:channels, :] = (total_ref[0:channels, :].astype(f32) + decayed).astype(bf16)
+    pair_ref[channels:, :] = jnp.concatenate(split3(logs + join3(before_ref[channels:, :], PAD)), axis=0)
+
+
+def within_kernel(first_head, last_head, skip_ref, x_ref, b_ref, c_ref, cum_ref, step_ref, prefix_ref, out_ref):
     half = BLOCK // 2
+    chosen = slice(first_head * HEAD_DIM, last_head * HEAD_DIM)
     causal = triangle(half, f32).T > 0
     for k in range(step_ref.shape[1] // BLOCK):
         span = slice(k * BLOCK, (k + 1) * BLOCK)
@@ -104,13 +118,13 @@
         b_block = b_ref[span, :]
         scores_first = lax.dot_general(c_block[:half], b_block[:half], TT, preferred_element_type=f32)
         scores_second = lax.dot_general(c_block[half:], b_block, TT, preferred_element_type=f32)
-        across = lax.dot_general(prefix_ref[k], c_block, TT, preferred_element_type=f32)
+        across = lax.dot_general(prefix_ref[k, chosen], c_block, TT, preferred_element_type=f32)
         cumulative = cum_ref[:, span]
         factor = jnp.exp(cumulative)
         columns = cumulative.T
-        for h in range(heads):
-            channels = slice(h * HEAD_DIM, (h + 1) * HEAD_DIM)
-            x_head = x_ref[channels, span]
+        for h in range(first_head, last_head):
+            channels = slice((h - first_head) * HEAD_DIM, (h - first_head + 1) * HEAD_DIM)
+            x_head = x_ref[h * HEAD_DIM : (h + 1) * HEAD_DIM, span]
             row = cumulative[h : h + 1]
             step = step_ref[h : h + 1, span]
             differ = columns[:half, h : h + 1] - row[:, :half]
@@ -143,10 +157,11 @@
     return jnp.where(core == 0, v * RING + u, u * RING + v)
 
 
-def gate_kernel(out_ref, gate_ref, c_ref, factor_ref, *refs):
+def gate_kernel(out_first, out_last, gate_ref, c_ref, factor_ref, *refs):
     totals, results = refs[:-RING], refs[-RING:]
-    channels = out_ref.shape[0]
+    channels = gate_ref.shape[0]
     heads = channels // HEAD_DIM
+    split = out_first.shape[0]
     incoming = jnp.zeros((channels, STATE), f32)
     log_sum = jnp.zeros((PAD, STATE), f32)
     for total in totals:
@@ -163,7 +178,11 @@
             for h in range(heads):
                 rows = slice(h * HEAD_DIM, (h + 1) * HEAD_DIM)
                 gate = gate_ref[rows, span].astype(f32)
-                output = out_ref[rows, span] + across[rows] * factor[h : h + 1]
+                if rows.start < split:
+                    local = out_first[rows, span]
+                else:
+                    local = out_last[rows.start - split : rows.stop - split, span]
+                output = local + across[rows] * factor[h : h + 1]
                 gated = output * (gate / (1.0 + jnp.exp(-gate)))
                 results[su][rows, sv * SUB : (sv + 1) * SUB] = gated.astype(bf16)
 
@@ -277,6 +296,7 @@
     ssm_input, gate_input, b_proj, c_proj, step_size, log_decay, skip_gain, norm_gain, out_weight
 ):
     tokens, channels = ssm_input.shape
+    heads = step_size.shape[0]
     width = out_weight.shape[1]
     blocks = tokens // BLOCK
     seq_count = lax.axis_size("seq")
@@ -295,37 +315,53 @@
 
     payload = channels + 3 * PAD
     ssm_columns, gate_columns = ssm_input.T, gate_input.T
-    prefix, total, cum, factor, b_own, c_own = pl.pallas_call(
+    prefix, total, cum, factor, x_own, b_own, c_own, step_own = pl.pallas_call(
         state_kernel,
-        in_specs=[near, pl.BlockSpec(memory_space=pltpu.HBM), pl.BlockSpec(memory_space=pltpu.HBM), near, near],
-        out_specs=[near] * 6,
+        in_specs=[pl.BlockSpec(memory_space=pltpu.HBM)] * 5,
+        out_specs=[near] * 8,
         out_shape=[
             pltpu.VMEM((blocks, channels, STATE), bf16),
             pltpu.VMEM((payload, STATE), bf16),
             pltpu.VMEM((PAD, tokens), f32),
             pltpu.VMEM((PAD, tokens), f32),
+            pltpu.VMEM((channels, tokens), bf16),
             pltpu.VMEM((tokens, STATE), bf16),
             pltpu.VMEM((tokens, STATE), bf16),
+            pltpu.VMEM((heads, tokens), f32),
         ],
-        scratch_shapes=[pltpu.SemaphoreType.DMA((2,))],
+        scratch_shapes=[pltpu.VMEM((heads, tokens), f32), pltpu.SemaphoreType.DMA((5,))],
         compiler_params=params,
         name="state",
-    )(*hold(ssm_columns), far(b_proj), far(c_proj), *hold(step_size, log_decay))
-
-    totals = [
-        lax.ppermute(total, "seq", [(k, k + s) for k in range(seq_count - s)]) for s in range(1, seq_count)
-    ]
-
-    local = pl.pallas_call(
-        within_kernel,
-        in_specs=[pl.BlockSpec(memory_space=pltpu.SMEM)] + [near] * 6,
+    )(*[far(value) for value in (ssm_columns, b_proj, c_proj, step_size, log_decay)])
+
+    def along(value, shift):
+        return lax.ppermute(value, "seq", [(k, k + shift) for k in range(seq_count - shift)])
+
+    def within(first_head, last_head):
+        return pl.pallas_call(
+            lambda *refs: within_kernel(first_head, last_head, *refs),
+            in_specs=[pl.BlockSpec(memory_space=pltpu.SMEM)] + [near] * 6,
+            out_specs=near,
+            out_shape=pltpu.VMEM(((last_head - first_head) * HEAD_DIM, tokens), f32),
+            compiler_params=params,
+        )(skip_gain, *hold(x_own, b_own, c_own, cum, step_own, prefix))
+
+    split = heads // 2 + 1
+    before = along(total, 1)
+    local_first = within(0, split)
+    before, local_first = lax.optimization_barrier((before, local_first))
+    pair = pl.pallas_call(
+        pair_kernel,
+        in_specs=[near] * 2,
         out_specs=near,
-        out_shape=pltpu.VMEM((channels, tokens), f32),
-        compiler_params=params,
-        name="within",
-    )(skip_gain, *hold(ssm_columns, b_own, c_own, cum, step_size, prefix))
-
-    local, weight_before, weight_after = lax.optimization_barrier((local, weight_before, weight_after))
+        out_shape=pltpu.VMEM((payload, STATE), bf16),
+        compiler_params=params,
+        name="pair",
+    )(*hold(total, before))
+    totals = [along(pair, shift) for shift in range(1, seq_count, 2)]
+    local_last = within(split, heads)
+
+    local_last, weight_before, weight_after = lax.optimization_barrier((local_last, weight_before, weight_after))
     middle = channels // 2
     upper, lower = weight_before[:middle], weight_after[middle:]
     upper, lower = ring(upper, 1, True), ring(lower, following, True)
@@ -334,12 +370,12 @@
     quarter = tokens // RING
     gated = pl.pallas_call(
         gate_kernel,
-        in_specs=[near] * (4 + seq_count - 1),
+        in_specs=[near] * (5 + len(totals)),
         out_specs=[near] * RING,
         out_shape=[pltpu.VMEM((channels, quarter), bf16)] * RING,
         compiler_params=params,
         name="gate",
-    )(*hold(local, gate_columns, c_own, factor, *totals))
+    )(*hold(local_first, local_last, gate_columns, c_own, factor, *totals))
 
     rows = [gated[0]] + [ring(gated[s], s, True) for s in range(1, RING)]
 

time: 93.4 us -> 89.6 us (0.959)
  the two profiles are of different devices: /device:TPU:6 before, /device:TPU:2 now
where the time goes in v1:
time: 89.6 us; the launch traced here: 89.4 us
  waiting for transfers between devices  38 us (42%)
  starting transfers between devices  35.9 us (40%)
  Pallas kernels  15.2 us (17%)
    ppermute x13, waiting for transfers between devices, ring(): return lax.ppermute(value, ('head', 'batch'), ring_pairs(shift, gather))  33.9 us
    ppermute x5, starting transfers between devices, along(): lax.ppermute(value, 'seq', [(k, k + shift) for k in range(seq_count - shi...  18.7 us
    ppermute x13, starting transfers between devices, ring(): return lax.ppermute(value, ('head', 'batch'), ring_pairs(shift, gather))  17.2 us
    pallas_call x2, Pallas kernels, within(): pl.pallas_call(lambda *refs: within_kernel(first_head, last_head, *refs),...  6.2 us
    ppermute x5, waiting for transfers between devices, along(): lax.ppermute(value, 'seq', [(k, k + shift) for k in range(seq_count - shi...  4.12 us
    pallas_call x1, Pallas kernels, body(): pl.pallas_call(project_kernel, in_specs=[near] * len(operands), out_specs...  2.85 us
    pallas_call x1, Pallas kernels, body(): pl.pallas_call(state_kernel, in_specs=[pl.BlockSpec(memory_space=pltpu.HB...  2.16 us
  transfers between devices with their start and end apart: 18, of which 10 were waited for; matrix products, arithmetic and copies ran while one was open for 0% of the time, Pallas kernels for 14%

profile of v1, /device:TPU:2, one launch (start us, length us, event | category | flops | bytes accessed | tf_op | source)
XLA Modules:
  0.0 89.4 jit_solution(648531969503189803)
XLA Ops:
  0.0 1.5 %collective-permute-start.1 = (bf16[320,2560]{1,0:T(8,128)(2,1)}, bf16[320,2560]{1,0:T(8,128)(2,1)S(1)}, u32[]{:S(2)}, u32[]{:S(2)}) collective-permute-start(bf16[320,2560]{1,0:T(8,128)(2,1)} %refs_4_.3), channel_id=1, source_target_pairs={{0,2},{1,9},{2,4},{3,11},{4,6},{5,13},{6,0},{7,15},{8,10},{9,17},{... | collective-permute-start | bytes 4915208 | tf_op jit(solution)/shard_map/ppermute | solution.py:292
  1.5 0.8 collective-permute-start.2
  2.2 2.2 %state.1 = (bf16[8,320,128]{2,1,0:T(8,128)(2,1)S(1)}, bf16[344,128]{1,0:T(8,128)(2,1)S(1)}, f32[8,2048]{1,0:T(8,128)S(1)}, f32[8,2048]{1,0:T(8,128)S(1)}, bf16[3...) custom-call(bf16[320,2048]{1,0:T(8,128)(2,1)} %bitcast.6, ...), custom_call_target="tpu_custom_call" | custom-call | tf_op jit(solution)/shard_map/state/pallas_call | solution.py:318
  4.4 3.1 %shard_map.92.out_last = f32[128,2048]{1,0:T(8,128)S(1)} custom-call(f32[5]{0:T(128)S(1)} %copy-done.3, bf16[320,2048]{1,0:T(8,128)(2,1)S(1)} %get-tuple-element.33.refs_1_, bf16[2048,128]{1,0:T(8,128)(2,1)S(1)} %get-tuple-element.34.refs_2_, bf16[2048,128]{1,0:T(8,128)(2,1)S(1)} %get-tuple-element.35.refs_3_.c_ref, ...), custom_call_target="tpu_custom_call" | custom-call | tf_op jit(solution)/shard_map/pallas_call | solution.py:341
  7.5 14.0 %collective-permute-done.1.refs_5_ = bf16[320,2560]{1,0:T(8,128)(2,1)S(1)} collective-permute-done((bf16[320,2560]{1,0:T(8,128)(2,1)}, bf16[320,2560]{1,0:T(8,128)(2,1)S(1)}, u32[]{:S(2)}, u32[]{:S(2)}) %collective-permute-start.1) | collective-permute-done | bytes 1638432 | tf_op jit(solution)/shard_map/ppermute | solution.py:292
  21.5 1.3 %collective-permute-done.2.refs_8_ = bf16[320,2560]{1,0:T(8,128)(2,1)S(1)} collective-permute-done((bf16[320,2560]{1,0:T(8,128)(2,1)}, bf16[320,2560]{1,0:T(8,128)(2,1)S(1)}, u32[]{:S(2)}, u32[]{:S(2)}) %collective-permute-start.2) | collective-permute-done | bytes 1638432 | tf_op jit(solution)/shard_map/ppermute | solution.py:292
  22.9 1.5 %collective-permute-start.10 = (bf16[160,2560]{1,0:T(8,128)(2,1)S(1)}, bf16[160,2560]{1,0:T(8,128)(2,1)S(1)}, u32[]{:S(2)}, u32[]{:S(2)}) collective-permute-start(bf16[160,2560]{1,0:T(8,128)(2,1)S(1)} %slice.6), channel_id=1, source_target_pairs={{0,2},{1,9},{2,4},{3,11},{4,6},{5,13},{6,0},{7,15},{8,10},{9,17},{... | collective-permute-start | bytes 2457608 | tf_op jit(solution)/shard_map/ppermute | solution.py:292
  24.4 0.7 collective-permute-start.11
  25.1 3.9 %collective-permute-start = (bf16[344,128]{1,0:T(8,128)(2,1)S(1)}, bf16[344,128]{1,0:T(8,128)(2,1)S(1)}, u32[]{:S(2)}, u32[]{:S(2)}) collective-permute-start(bf16[344,128]{1,0:T(8,128)(2,1)S(1)} %get-tuple-element.32.total_ref), channel_id=1, source_target_pairs={{0,32},{32,64},{64,96},{96,128},{128,160},{160,192},{192,224},{1,3... | collective-permute-start | bytes 264200 | tf_op jit(solution)/shard_map/ppermute | solution.py:338
  29.1 3.1 %shard_map.91.out_first = f32[192,2048]{1,0:T(8,128)S(1)} custom-call(f32[5]{0:T(128)S(1)} %copy-done.3, bf16[320,2048]{1,0:T(8,128)(2,1)S(1)} %get-tuple-element.33.refs_1_, bf16[2048,128]{1,0:T(8,128)(2,1)S(1)} %get-tuple-element.34.refs_2_, bf16[2048,128]{1,0:T(8,128)(2,1)S(1)} %get-tuple-element.35.refs_3_.c_ref, ...), custom_call_target="tpu_custom_call" | custom-call | tf_op jit(solution)/shard_map/pallas_call | solution.py:341
  32.3 3.8 %collective-permute-start.3 = (bf16[344,128]{1,0:T(8,128)(2,1)S(1)}, bf16[344,128]{1,0:T(8,128)(2,1)S(1)}, u32[]{:S(2)}, u32[]{:S(2)}) collective-permute-start(bf16[344,128]{1,0:T(8,128)(2,1)S(1)} %pair.1), channel_id=1, source_target_pairs={{0,32},{32,64},{64,96},{96,128},{128,160},{160,192},{192,224},{1,3... | collective-permute-start | bytes 264200 | tf_op jit(solution)/shard_map/ppermute | solution.py:338
  36.1 8.4 %collective-permute-start.4 = (bf16[344,128]{1,0:T(8,128)(2,1)S(1)}, bf16[344,128]{1,0:T(8,128)(2,1)S(1)}, u32[]{:S(2)}, u32[]{:S(2)}) collective-permute-start(bf16[344,128]{1,0:T(8,128)(2,1)S(1)} %pair.1), channel_id=1, source_target_pairs={{0,96},{32,128},{64,160},{96,192},{128,224},{1,97},{33,129},{65,16... | collective-permute-start | bytes 264200 | tf_op jit(solution)/shard_map/ppermute | solution.py:338
  44.5 1.3 %collective-permute-start.5 = (bf16[344,128]{1,0:T(8,128)(2,1)S(1)}, bf16[344,128]{1,0:T(8,128)(2,1)S(1)}, u32[]{:S(2)}, u32[]{:S(2)}) collective-permute-start(bf16[344,128]{1,0:T(8,128)(2,1)S(1)} %pair.1), channel_id=1, source_target_pairs={{0,160},{32,192},{64,224},{1,161},{33,193},{65,225},{2,162},{34,19... | collective-permute-start | bytes 264200 | tf_op jit(solution)/shard_map/ppermute | solution.py:338
  45.8 1.3 %collective-permute-start.6 = (bf16[344,128]{1,0:T(8,128)(2,1)S(1)}, bf16[344,128]{1,0:T(8,128)(2,1)S(1)}, u32[]{:S(2)}, u32[]{:S(2)}) collective-permute-start(bf16[344,128]{1,0:T(8,128)(2,1)S(1)} %pair.1), channel_id=1, source_target_pairs={{0,224},{1,225},{2,226},{3,227},{4,228},{5,229},{6,230},{7,231},{8... | collective-permute-start | bytes 264200 | tf_op jit(solution)/shard_map/ppermute | solution.py:338
  47.1 3.0 %collective-permute-done.5.refs_2_ = bf16[344,128]{1,0:T(8,128)(2,1)S(1)} collective-permute-done((bf16[344,128]{1,0:T(8,128)(2,1)S(1)}, bf16[344,128]{1,0:T(8,128)(2,1)S(1)}, u32[]{:S(2)}, u32[]{:S(2)}) %collective-permute-start.5) | collective-permute-done | bytes 88096 | tf_op jit(solution)/shard_map/ppermute | solution.py:338
  50.1 1.2 %collective-permute-done.6.refs_3_ = bf16[344,128]{1,0:T(8,128)(2,1)S(1)} collective-permute-done((bf16[344,128]{1,0:T(8,128)(2,1)S(1)}, bf16[344,128]{1,0:T(8,128)(2,1)S(1)}, u32[]{:S(2)}, u32[]{:S(2)}) %collective-permute-start.6) | collective-permute-done | bytes 88096 | tf_op jit(solution)/shard_map/ppermute | solution.py:338
  51.3 1.3 %gate.1 = (bf16[320,512]{1,0:T(8,128)(2,1)S(1)}, bf16[320,512]{1,0:T(8,128)(2,1)S(1)}, bf16[320,512]{1,0:T(8,128)(2,1)S(1)}, bf16[320,512]{1,0:T(8,128)(2,1)S(1)}) custom-call(f32[192,2048]{1,0:T(8,128)S(1)} %shard_map.91.out_first, f32[128,2048]{1,0:T(8,128)S(1)} %shard_map.92.out_last, bf16[320,2048]{1,0:T(8,128)(2,1)S(1)} %bitcast.3, ...), custom_call_target="tpu_custom_call" | custom-call | tf_op jit(solution)/shard_map/gate/pallas_call | solution.py:371
  52.6 1.6 %collective-permute-start.7 = (bf16[320,512]{1,0:T(8,128)(2,1)S(1)}, bf16[320,512]{1,0:T(8,128)(2,1)S(1)}, u32[]{:S(2)}, u32[]{:S(2)}) collective-permute-start(bf16[320,512]{1,0:T(8,128)(2,1)S(1)} %get-tuple-element.44), channel_id=1, source_target_pairs={{0,2},{1,9},{2,4},{3,11},{4,6},{5,13},{6,0},{7,15},{8,10},{9,17},{... | collective-permute-start | bytes 983048 | tf_op jit(solution)/shard_map/ppermute | solution.py:292
  54.1 1.3 %collective-permute-start.8 = (bf16[320,512]{1,0:T(8,128)(2,1)S(1)}, bf16[320,512]{1,0:T(8,128)(2,1)S(1)}, u32[]{:S(2)}, u32[]{:S(2)}) collective-permute-start(bf16[320,512]{1,0:T(8,128)(2,1)S(1)} %get-tuple-element.45), channel_id=1, source_target_pairs={{0,4},{1,17},{2,6},{3,19},{4,0},{5,21},{6,2},{7,23},{8,12},{9,25},... | collective-permute-start | bytes 983048 | tf_op jit(solution)/shard_map/ppermute | solution.py:292
  55.5 2.2 %collective-permute-start.9 = (bf16[320,512]{1,0:T(8,128)(2,1)S(1)}, bf16[320,512]{1,0:T(8,128)(2,1)S(1)}, u32[]{:S(2)}, u32[]{:S(2)}) collective-permute-start(bf16[320,512]{1,0:T(8,128)(2,1)S(1)} %get-tuple-element.46), channel_id=1, source_target_pairs={{0,6},{1,25},{2,0},{3,27},{4,2},{5,29},{6,4},{7,31},{8,14},{9,1},{... | collective-permute-start | bytes 983048 | tf_op jit(solution)/shard_map/ppermute | solution.py:292
  57.6 2.1 %collective-permute-done.7.refs_1_ = bf16[320,512]{1,0:T(8,128)(2,1)S(1)} collective-permute-done((bf16[320,512]{1,0:T(8,128)(2,1)S(1)}, bf16[320,512]{1,0:T(8,128)(2,1)S(1)}, u32[]{:S(2)}, u32[]{:S(2)}) %collective-permute-start.7) | collective-permute-done | bytes 327712 | tf_op jit(solution)/shard_map/ppermute | solution.py:292
  59.7 3.1 %collective-permute-done.8.refs_2_ = bf16[320,512]{1,0:T(8,128)(2,1)S(1)} collective-permute-done((bf16[320,512]{1,0:T(8,128)(2,1)S(1)}, bf16[320,512]{1,0:T(8,128)(2,1)S(1)}, u32[]{:S(2)}, u32[]{:S(2)}) %collective-permute-start.8) | collective-permute-done | bytes 327712 | tf_op jit(solution)/shard_map/ppermute | solution.py:292
  62.8 3.2 %collective-permute-done.9.refs_3_ = bf16[320,512]{1,0:T(8,128)(2,1)S(1)} collective-permute-done((bf16[320,512]{1,0:T(8,128)(2,1)S(1)}, bf16[320,512]{1,0:T(8,128)(2,1)S(1)}, u32[]{:S(2)}, u32[]{:S(2)}) %collective-permute-start.9) | collective-permute-done | bytes 327712 | tf_op jit(solution)/shard_map/ppermute | solution.py:292
  66.1 1.2 %opposite.1 = (bf16[136,1280]{1,0:T(8,128)(2,1)S(1)}, bf16[128,1280]{1,0:T(8,128)(2,1)S(1)}) custom-call(f32[40,128]{1,0:T(8,128)S(1)} %bitcast.4, bf16[320,512]{1,0:T(8,128)(2,1)S(1)} %get-tuple-element.43.refs_0_, bf16[320,512]{1,0:T(8,128)(2,1)S(1)} %collective-permute-done.7.refs_1_, bf16[320,512]{1,0:T(8,128)(2,1)S(1)} %collective-permute-done.8.refs_2_, ...), custom_call_target="tpu_custom_call" | custom-call | tf_op jit(solution)/shard_map/opposite/pallas_call | solution.py:385
  67.9 2.7 %collective-permute-start.13 = (bf16[128,1280]{1,0:T(8,128)(2,1)S(1)}, bf16[128,1280]{1,0:T(8,128)(2,1)S(1)}, u32[]{:S(2)}, u32[]{:S(2)}) collective-permute-start(bf16[128,1280]{1,0:T(8,128)(2,1)S(1)} %get-tuple-element.54), channel_id=1, source_target_pairs={{0,24},{1,7},{2,26},{3,1},{4,28},{5,3},{6,30},{7,5},{8,0},{9,15},{... | collective-permute-start | bytes 983048 | tf_op jit(solution)/shard_map/ppermute | solution.py:292
  70.6 2.9 %project.1 = (bf16[136,1280]{1,0:T(8,128)(2,1)S(1)}, bf16[128,1280]{1,0:T(8,128)(2,1)S(1)}, bf16[136,1280]{1,0:T(8,128)(2,1)S(1)}, bf16[128,1280]{1,0:T(8,128)(2...) custom-call(f32[40,128]{1,0:T(8,128)S(1)} %bitcast.5, bf16[320,512]{1,0:T(8,128)(2,1)S(1)} %get-tuple-element.43.refs_0_, ...), custom_call_target="tpu_custom_call" | custom-call | tf_op jit(solution)/shard_map/project/pallas_call | solution.py:396
  74.1 1.1 %collective-permute-done.13.got_second = bf16[128,1280]{1,0:T(8,128)(2,1)S(1)} collective-permute-done((bf16[128,1280]{1,0:T(8,128)(2,1)S(1)}, bf16[128,1280]{1,0:T(8,128)(2,1)S(1)}, u32[]{:S(2)}, u32[]{:S(2)}) %collective-permute-start.13) | collective-permute-done | bytes 327712 | tf_op jit(solution)/shard_map/ppermute | solution.py:292
  75.2 0.7 collective-permute-done.12.got_first
  76.6 1.3 %collective-permute-start.15 = (bf16[128,1280]{1,0:T(8,128)(2,1)S(1)}, bf16[128,1280]{1,0:T(8,128)(2,1)S(1)}, u32[]{:S(2)}, u32[]{:S(2)}) collective-permute-start(bf16[128,1280]{1,0:T(8,128)(2,1)S(1)} %get-tuple-element.56), channel_id=1, source_target_pairs={{0,8},{1,3},{2,10},{3,5},{4,12},{5,7},{6,14},{7,1},{8,16},{9,11},{... | collective-permute-start | bytes 983048 | tf_op jit(solution)/shard_map/ppermute | solution.py:292
  77.9 2.0 %collective-permute-start.17 = (bf16[128,1280]{1,0:T(8,128)(2,1)S(1)}, bf16[128,1280]{1,0:T(8,128)(2,1)S(1)}, u32[]{:S(2)}, u32[]{:S(2)}) collective-permute-start(bf16[128,1280]{1,0:T(8,128)(2,1)S(1)} %get-tuple-element.58), channel_id=1, source_target_pairs={{0,24},{1,7},{2,26},{3,1},{4,28},{5,3},{6,30},{7,5},{8,0},{9,15},{... | collective-permute-start | bytes 983048 | tf_op jit(solution)/shard_map/ppermute | solution.py:292
  79.8 8.3 %collective-permute-done.15.refs_3_ = bf16[128,1280]{1,0:T(8,128)(2,1)S(1)} collective-permute-done((bf16[128,1280]{1,0:T(8,128)(2,1)S(1)}, bf16[128,1280]{1,0:T(8,128)(2,1)S(1)}, u32[]{:S(2)}, u32[]{:S(2)}) %collective-permute-start.15) | collective-permute-done | bytes 327712 | tf_op jit(solution)/shard_map/ppermute | solution.py:292
  88.2 1.2 %finish.1 = bf16[128,2560]{1,0:T(8,128)(2,1)} custom-call(f32[128,2560]{1,0:T(8,128)S(1)} %get-tuple-element.49.refs_0_, f32[8,128]{1,0:T(8,128)S(1)} %get-tuple-element.50.refs_1_, bf16[136,1280]{1,0:T(8,128)(2,1)S(1)} %collective-permute-done.14.refs_2_, bf16[128,1280]{1,0:T(8,128)(2,1)S(1)} %collective-permute-done.15.refs_3_, ...), custom_call_target="tpu_custom_call" | custom-call | tf_op jit(solution)/shard_map/finish/pallas_call | solution.py:418
  (23 shorter events, 2.1 us)
Async XLA Ops:
  0.0 21.5 %collective-permute-start.1 = (bf16[320,2560]{1,0:T(8,128)(2,1)}, bf16[320,2560]{1,0:T(8,128)(2,1)S(1)}, u32[]{:S(2)}, u32[]{:S(2)}) collective-permute-start(bf16[320,2560]{1,0:T(8,128)(2,1)} %refs_4_.3), channel_id=1, source_target_pairs={{0,2},{1,9},{2,4},{3,11},{4,6},{5,13},{6,0},{7,15},{8,10},{9,17},{... | collective-permute-start | bytes 4915208 | tf_op jit(solution)/shard_map/ppermute | solution.py:292
  1.5 21.3 %collective-permute-start.2 = (bf16[320,2560]{1,0:T(8,128)(2,1)}, bf16[320,2560]{1,0:T(8,128)(2,1)S(1)}, u32[]{:S(2)}, u32[]{:S(2)}) collective-permute-start(bf16[320,2560]{1,0:T(8,128)(2,1)} %refs_4_.3), channel_id=1, source_target_pairs={{0,6},{1,25},{2,0},{3,27},{4,2},{5,29},{6,4},{7,31},{8,14},{9,1},{... | collective-permute-start | bytes 4915208 | tf_op jit(solution)/shard_map/ppermute | solution.py:292
  2.2 2.2 %copy-start.3 = (f32[5]{0:T(128)S(1)}, f32[5]{0:T(128)}, u32[]{:S(2)}) copy-start(f32[5]{0:T(128)} %refs_0_.3) | copy-start | bytes 64
  22.9 43.2 %collective-permute-start.10 = (bf16[160,2560]{1,0:T(8,128)(2,1)S(1)}, bf16[160,2560]{1,0:T(8,128)(2,1)S(1)}, u32[]{:S(2)}, u32[]{:S(2)}) collective-permute-start(bf16[160,2560]{1,0:T(8,128)(2,1)S(1)} %slice.6), channel_id=1, source_target_pairs={{0,2},{1,9},{2,4},{3,11},{4,6},{5,13},{6,0},{7,15},{8,10},{9,17},{... | collective-permute-start | bytes 2457608 | tf_op jit(solution)/shard_map/ppermute | solution.py:292
  24.4 41.7 %collective-permute-start.11 = (bf16[160,2560]{1,0:T(8,128)(2,1)S(1)}, bf16[160,2560]{1,0:T(8,128)(2,1)S(1)}, u32[]{:S(2)}, u32[]{:S(2)}) collective-permute-start(bf16[160,2560]{1,0:T(8,128)(2,1)S(1)} %slice.7), channel_id=1, source_target_pairs={{0,6},{1,25},{2,0},{3,27},{4,2},{5,29},{6,4},{7,31},{8,14},{9,1},{... | collective-permute-start | bytes 2457608 | tf_op jit(solution)/shard_map/ppermute | solution.py:292
  25.1 26.1 %copy-start.1 = (bf16[2048,320]{0,1:T(8,128)(2,1)S(1)}, bf16[2048,320]{0,1:T(8,128)(2,1)}, u32[]{:S(2)}) copy-start(bf16[2048,320]{0,1:T(8,128)(2,1)} %param.10) | copy-start | bytes 3932164
  25.1 7.1 %collective-permute-start = (bf16[344,128]{1,0:T(8,128)(2,1)S(1)}, bf16[344,128]{1,0:T(8,128)(2,1)S(1)}, u32[]{:S(2)}, u32[]{:S(2)}) collective-permute-start(bf16[344,128]{1,0:T(8,128)(2,1)S(1)} %get-tuple-element.32.total_ref), channel_id=1, source_target_pairs={{0,32},{32,64},{64,96},{96,128},{128,160},{160,192},{192,224},{1,3... | collective-permute-start | bytes 264200 | tf_op jit(solution)/shard_map/ppermute | solution.py:338
  32.3 13.5 %collective-permute-start.3 = (bf16[344,128]{1,0:T(8,128)(2,1)S(1)}, bf16[344,128]{1,0:T(8,128)(2,1)S(1)}, u32[]{:S(2)}, u32[]{:S(2)}) collective-permute-start(bf16[344,128]{1,0:T(8,128)(2,1)S(1)} %pair.1), channel_id=1, source_target_pairs={{0,32},{32,64},{64,96},{96,128},{128,160},{160,192},{192,224},{1,3... | collective-permute-start | bytes 264200 | tf_op jit(solution)/shard_map/ppermute | solution.py:338
  36.1 11.0 %collective-permute-start.4 = (bf16[344,128]{1,0:T(8,128)(2,1)S(1)}, bf16[344,128]{1,0:T(8,128)(2,1)S(1)}, u32[]{:S(2)}, u32[]{:S(2)}) collective-permute-start(bf16[344,128]{1,0:T(8,128)(2,1)S(1)} %pair.1), channel_id=1, source_target_pairs={{0,96},{32,128},{64,160},{96,192},{128,224},{1,97},{33,129},{65,16... | collective-permute-start | bytes 264200 | tf_op jit(solution)/shard_map/ppermute | solution.py:338
  44.5 5.6 %collective-permute-start.5 = (bf16[344,128]{1,0:T(8,128)(2,1)S(1)}, bf16[344,128]{1,0:T(8,128)(2,1)S(1)}, u32[]{:S(2)}, u32[]{:S(2)}) collective-permute-start(bf16[344,128]{1,0:T(8,128)(2,1)S(1)} %pair.1), channel_id=1, source_target_pairs={{0,160},{32,192},{64,224},{1,161},{33,193},{65,225},{2,162},{34,19... | collective-permute-start | bytes 264200 | tf_op jit(solution)/shard_map/ppermute | solution.py:338
  45.8 5.4 %collective-permute-start.6 = (bf16[344,128]{1,0:T(8,128)(2,1)S(1)}, bf16[344,128]{1,0:T(8,128)(2,1)S(1)}, u32[]{:S(2)}, u32[]{:S(2)}) collective-permute-start(bf16[344,128]{1,0:T(8,128)(2,1)S(1)} %pair.1), channel_id=1, source_target_pairs={{0,224},{1,225},{2,226},{3,227},{4,228},{5,229},{6,230},{7,231},{8... | collective-permute-start | bytes 264200 | tf_op jit(solution)/shard_map/ppermute | solution.py:338
  51.3 14.8 %copy-start = (bf16[320,2560]{1,0:T(8,128)(2,1)S(1)}, bf16[320,2560]{1,0:T(8,128)(2,1)}, u32[]{:S(2)}) copy-start(bf16[320,2560]{1,0:T(8,128)(2,1)} %refs_4_.3) | copy-start | bytes 4915204
  51.3 14.8 %copy-start.2 = (f32[5120]{0:T(1024)S(1)}, f32[5120]{0:T(1024)}, u32[]{:S(2)}) copy-start(f32[5120]{0:T(1024)} %param.16) | copy-start | bytes 61444
  52.6 7.2 %collective-permute-start.7 = (bf16[320,512]{1,0:T(8,128)(2,1)S(1)}, bf16[320,512]{1,0:T(8,128)(2,1)S(1)}, u32[]{:S(2)}, u32[]{:S(2)}) collective-permute-start(bf16[320,512]{1,0:T(8,128)(2,1)S(1)} %get-tuple-element.44), channel_id=1, source_target_pairs={{0,2},{1,9},{2,4},{3,11},{4,6},{5,13},{6,0},{7,15},{8,10},{9,17},{... | collective-permute-start | bytes 983048 | tf_op jit(solution)/shard_map/ppermute | solution.py:292
  54.1 8.7 %collective-permute-start.8 = (bf16[320,512]{1,0:T(8,128)(2,1)S(1)}, bf16[320,512]{1,0:T(8,128)(2,1)S(1)}, u32[]{:S(2)}, u32[]{:S(2)}) collective-permute-start(bf16[320,512]{1,0:T(8,128)(2,1)S(1)} %get-tuple-element.45), channel_id=1, source_target_pairs={{0,4},{1,17},{2,6},{3,19},{4,0},{5,21},{6,2},{7,23},{8,12},{9,25},... | collective-permute-start | bytes 983048 | tf_op jit(solution)/shard_map/ppermute | solution.py:292
  55.5 10.6 %collective-permute-start.9 = (bf16[320,512]{1,0:T(8,128)(2,1)S(1)}, bf16[320,512]{1,0:T(8,128)(2,1)S(1)}, u32[]{:S(2)}, u32[]{:S(2)}) collective-permute-start(bf16[320,512]{1,0:T(8,128)(2,1)S(1)} %get-tuple-element.46), channel_id=1, source_target_pairs={{0,6},{1,25},{2,0},{3,27},{4,2},{5,29},{6,4},{7,31},{8,14},{9,1},{... | collective-permute-start | bytes 983048 | tf_op jit(solution)/shard_map/ppermute | solution.py:292
  67.3 8.6 %collective-permute-start.12 = (bf16[136,1280]{1,0:T(8,128)(2,1)S(1)}, bf16[136,1280]{1,0:T(8,128)(2,1)S(1)}, u32[]{:S(2)}, u32[]{:S(2)}) collective-permute-start(bf16[136,1280]{1,0:T(8,128)(2,1)S(1)} %get-tuple-element.53), channel_id=1, source_target_pairs={{0,8},{1,3},{2,10},{3,5},{4,12},{5,7},{6,14},{7,1},{8,16},{9,11},{... | collective-permute-start | bytes 1044488 | tf_op jit(solution)/shard_map/ppermute | solution.py:292
  67.9 7.3 %collective-permute-start.13 = (bf16[128,1280]{1,0:T(8,128)(2,1)S(1)}, bf16[128,1280]{1,0:T(8,128)(2,1)S(1)}, u32[]{:S(2)}, u32[]{:S(2)}) collective-permute-start(bf16[128,1280]{1,0:T(8,128)(2,1)S(1)} %get-tuple-element.54), channel_id=1, source_target_pairs={{0,24},{1,7},{2,26},{3,1},{4,28},{5,3},{6,30},{7,5},{8,0},{9,15},{... | collective-permute-start | bytes 983048 | tf_op jit(solution)/shard_map/ppermute | solution.py:292
  73.5 14.7 %collective-permute-start.16 = (bf16[136,1280]{1,0:T(8,128)(2,1)S(1)}, bf16[136,1280]{1,0:T(8,128)(2,1)S(1)}, u32[]{:S(2)}, u32[]{:S(2)}) collective-permute-start(bf16[136,1280]{1,0:T(8,128)(2,1)S(1)} %get-tuple-element.57), channel_id=1, source_target_pairs={{0,24},{1,7},{2,26},{3,1},{4,28},{5,3},{6,30},{7,5},{8,0},{9,15},{... | collective-permute-start | bytes 1044488 | tf_op jit(solution)/shard_map/ppermute | solution.py:292
  76.1 12.1 %collective-permute-start.14 = (bf16[136,1280]{1,0:T(8,128)(2,1)S(1)}, bf16[136,1280]{1,0:T(8,128)(2,1)S(1)}, u32[]{:S(2)}, u32[]{:S(2)}) collective-permute-start(bf16[136,1280]{1,0:T(8,128)(2,1)S(1)} %get-tuple-element.55), channel_id=1, source_target_pairs={{0,8},{1,3},{2,10},{3,5},{4,12},{5,7},{6,14},{7,1},{8,16},{9,11},{... | collective-permute-start | bytes 1044488 | tf_op jit(solution)/shard_map/ppermute | solution.py:292
  76.6 11.6 %collective-permute-start.15 = (bf16[128,1280]{1,0:T(8,128)(2,1)S(1)}, bf16[128,1280]{1,0:T(8,128)(2,1)S(1)}, u32[]{:S(2)}, u32[]{:S(2)}) collective-permute-start(bf16[128,1280]{1,0:T(8,128)(2,1)S(1)} %get-tuple-element.56), channel_id=1, source_target_pairs={{0,8},{1,3},{2,10},{3,5},{4,12},{5,7},{6,14},{7,1},{8,16},{9,11},{... | collective-permute-start | bytes 983048 | tf_op jit(solution)/shard_map/ppermute | solution.py:292
  77.9 10.3 %collective-permute-start.17 = (bf16[128,1280]{1,0:T(8,128)(2,1)S(1)}, bf16[128,1280]{1,0:T(8,128)(2,1)S(1)}, u32[]{:S(2)}, u32[]{:S(2)}) collective-permute-start(bf16[128,1280]{1,0:T(8,128)(2,1)S(1)} %get-tuple-element.58), channel_id=1, source_target_pairs={{0,24},{1,7},{2,26},{3,1},{4,28},{5,3},{6,30},{7,5},{8,0},{9,15},{... | collective-permute-start | bytes 983048 | tf_op jit(solution)/shard_map/ppermute | solution.py:292

commit v2 on v1

--- a/solution.py
+++ b/solution.py
@@ -108,9 +108,9 @@
     pair_ref[channels:, :] = jnp.concatenate(split3(logs + join3(before_ref[channels:, :], PAD)), axis=0)
 
 
-def within_kernel(first_head, last_head, skip_ref, x_ref, b_ref, c_ref, cum_ref, step_ref, prefix_ref, out_ref):
+def within_kernel(skip_ref, x_ref, b_ref, c_ref, cum_ref, step_ref, prefix_ref, out_ref):
+    heads = step_ref.shape[0]
     half = BLOCK // 2
-    chosen = slice(first_head * HEAD_DIM, last_head * HEAD_DIM)
     causal = triangle(half, f32).T > 0
     for k in range(step_ref.shape[1] // BLOCK):
         span = slice(k * BLOCK, (k + 1) * BLOCK)
@@ -118,13 +118,13 @@
         b_block = b_ref[span, :]
         scores_first = lax.dot_general(c_block[:half], b_block[:half], TT, preferred_element_type=f32)
         scores_second = lax.dot_general(c_block[half:], b_block, TT, preferred_element_type=f32)
-        across = lax.dot_general(prefix_ref[k, chosen], c_block, TT, preferred_element_type=f32)
+        across = lax.dot_general(prefix_ref[k], c_block, TT, preferred_element_type=f32)
         cumulative = cum_ref[:, span]
         factor = jnp.exp(cumulative)
         columns = cumulative.T
-        for h in range(first_head, last_head):
-            channels = slice((h - first_head) * HEAD_DIM, (h - first_head + 1) * HEAD_DIM)
-            x_head = x_ref[h * HEAD_DIM : (h + 1) * HEAD_DIM, span]
+        for h in range(heads):
+            channels = slice(h * HEAD_DIM, (h + 1) * HEAD_DIM)
+            x_head = x_ref[channels, span]
             row = cumulative[h : h + 1]
             step = step_ref[h : h + 1, span]
             differ = columns[:half, h : h + 1] - row[:, :half]
@@ -157,11 +157,10 @@
     return jnp.where(core == 0, v * RING + u, u * RING + v)
 
 
-def gate_kernel(out_first, out_last, gate_ref, c_ref, factor_ref, *refs):
+def gate_kernel(out_ref, gate_ref, c_ref, factor_ref, *refs):
     totals, results = refs[:-RING], refs[-RING:]
     channels = gate_ref.shape[0]
     heads = channels // HEAD_DIM
-    split = out_first.shape[0]
     incoming = jnp.zeros((channels, STATE), f32)
     log_sum = jnp.zeros((PAD, STATE), f32)
     for total in totals:
@@ -178,11 +177,7 @@
             for h in range(heads):
                 rows = slice(h * HEAD_DIM, (h + 1) * HEAD_DIM)
                 gate = gate_ref[rows, span].astype(f32)
-                if rows.start < split:
-                    local = out_first[rows, span]
-                else:
-                    local = out_last[rows.start - split : rows.stop - split, span]
-                output = local + across[rows] * factor[h : h + 1]
+                output = out_ref[rows, span] + across[rows] * factor[h : h + 1]
                 gated = output * (gate / (1.0 + jnp.exp(-gate)))
                 results[su][rows, sv * SUB : (sv + 1) * SUB] = gated.astype(bf16)
 
@@ -337,19 +332,16 @@
     def along(value, shift):
         return lax.ppermute(value, "seq", [(k, k + shift) for k in range(seq_count - shift)])
 
-    def within(first_head, last_head):
-        return pl.pallas_call(
-            lambda *refs: within_kernel(first_head, last_head, *refs),
-            in_specs=[pl.BlockSpec(memory_space=pltpu.SMEM)] + [near] * 6,
-            out_specs=near,
-            out_shape=pltpu.VMEM(((last_head - first_head) * HEAD_DIM, tokens), f32),
-            compiler_params=params,
-        )(skip_gain, *hold(x_own, b_own, c_own, cum, step_own, prefix))
-
-    split = heads // 2 + 1
     before = along(total, 1)
-    local_first = within(0, split)
-    before, local_first = lax.optimization_barrier((before, local_first))
+    local = pl.pallas_call(
+        within_kernel,
+        in_specs=[pl.BlockSpec(memory_space=pltpu.SMEM)] + [near] * 6,
+        out_specs=near,
+        out_shape=pltpu.VMEM((channels, tokens), f32),
+        compiler_params=params,
+        name="within",
+    )(skip_gain, *hold(x_own, b_own, c_own, cum, step_own, prefix))
+    before, local = lax.optimization_barrier((before, local))
     pair = pl.pallas_call(
         pair_kernel,
         in_specs=[near] * 2,
@@ -359,9 +351,8 @@
         name="pair",
     )(*hold(total, before))
     totals = [along(pair, shift) for shift in range(1, seq_count, 2)]
-    local_last = within(split, heads)
-
-    local_last, weight_before, weight_after = lax.optimization_barrier((local_last, weight_before, weight_after))
+
+    weight_before, weight_after, pair = lax.optimization_barrier((weight_before, weight_after, pair))
     middle = channels // 2
     upper, lower = weight_before[:middle], weight_after[middle:]
     upper, lower = ring(upper, 1, True), ring(lower, following, True)
@@ -370,12 +361,12 @@
     quarter = tokens // RING
     gated = pl.pallas_call(
         gate_kernel,
-        in_specs=[near] * (5 + len(totals)),
+        in_specs=[near] * (4 + len(totals)),
         out_specs=[near] * RING,
         out_shape=[pltpu.VMEM((channels, quarter), bf16)] * RING,
         compiler_params=params,
         name="gate",
-    )(*hold(local_first, local_last, gate_columns, c_own, factor, *totals))
+    )(*hold(local, gate_columns, c_own, factor, *totals))
 
     rows = [gated[0]] + [ring(gated[s], s, True) for s in range(1, RING)]
 

time: 89.6 us -> 83 us (0.926)
  waiting for transfers between devices: 38 us -> 34.2 us
  Pallas kernels: 15.2 us -> 13.3 us
    ppermute x13, waiting for transfers between devices: 33.9 us -> 28.7 us  [ring(): return lax.ppermute(value, ('head', 'batch'), ring_pairs(shift, gather))]
    pallas_call x3 -> x2, Pallas kernels: 7.49 us -> 5.61 us  [the longest x1 4.27 us: body(): pl.pallas_call(within_kernel, in_specs=[pl.BlockSpec(memory_space=pltpu.S...]
    ppermute x5, waiting for transfers between devices: 4.12 us -> 5.48 us  [along(): lax.ppermute(value, 'seq', [(k, k + shift) for k in range(seq_count - shi...]
    ppermute x5, starting transfers between devices: 18.7 us -> 17.8 us  [along(): lax.ppermute(value, 'seq', [(k, k + shift) for k in range(seq_count - shi...]
  transfers between devices with their start and end apart: 18 -> 18, of which waited for: 10 -> 10; matrix products, arithmetic and copies ran while one was open for 0% -> 0% of each run, Pallas kernels for 14% -> 13%
where the time goes in v2:
time: 83 us; the launch traced here: 82.8 us
  starting transfers between devices  35.1 us (42%)
  waiting for transfers between devices  34.2 us (41%)
  Pallas kernels  13.3 us (16%)
    ppermute x13, waiting for transfers between devices, ring(): return lax.ppermute(value, ('head', 'batch'), ring_pairs(shift, gather))  28.7 us
    ppermute x5, starting transfers between devices, along(): lax.ppermute(value, 'seq', [(k, k + shift) for k in range(seq_count - shi...  17.8 us
    ppermute x13, starting transfers between devices, ring(): return lax.ppermute(value, ('head', 'batch'), ring_pairs(shift, gather))  17.3 us
    ppermute x5, waiting for transfers between devices, along(): lax.ppermute(value, 'seq', [(k, k + shift) for k in range(seq_count - shi...  5.48 us
    pallas_call x1, Pallas kernels, body(): pl.pallas_call(within_kernel, in_specs=[pl.BlockSpec(memory_space=pltpu.S...  4.27 us
    pallas_call x1, Pallas kernels, body(): pl.pallas_call(project_kernel, in_specs=[near] * len(operands), out_specs...  2.86 us
    pallas_call x1, Pallas kernels, body(): pl.pallas_call(state_kernel, in_specs=[pl.BlockSpec(memory_space=pltpu.HB...  2.17 us
  transfers between devices with their start and end apart: 18, of which 10 were waited for; matrix products, arithmetic and copies ran while one was open for 0% of the time, Pallas kernels for 13%

profile of v2, /device:TPU:2, one launch (start us, length us, event | category | flops | bytes accessed | tf_op | source)
XLA Modules:
  0.0 82.8 jit_solution(2514862748179986892)
XLA Ops:
  0.0 1.5 %collective-permute-start.8 = (bf16[320,2560]{1,0:T(8,128)(2,1)}, bf16[320,2560]{1,0:T(8,128)(2,1)S(1)}, u32[]{:S(2)}, u32[]{:S(2)}) collective-permute-start(bf16[320,2560]{1,0:T(8,128)(2,1)} %refs_4_.3), channel_id=1, source_target_pairs={{0,2},{1,9},{2,4},{3,11},{4,6},{5,13},{6,0},{7,15},{8,10},{9,17},{... | collective-permute-start | bytes 4915208 | tf_op jit(solution)/shard_map/ppermute | solution.py:287
  1.5 0.8 collective-permute-start.9
  2.2 2.2 %state.1 = (bf16[8,320,128]{2,1,0:T(8,128)(2,1)S(1)}, bf16[344,128]{1,0:T(8,128)(2,1)S(1)}, f32[8,2048]{1,0:T(8,128)S(1)}, f32[8,2048]{1,0:T(8,128)S(1)}, bf16[3...) custom-call(bf16[320,2048]{1,0:T(8,128)(2,1)} %bitcast.6, ...), custom_call_target="tpu_custom_call" | custom-call | tf_op jit(solution)/shard_map/state/pallas_call | solution.py:313
  4.4 3.6 %collective-permute-start = (bf16[344,128]{1,0:T(8,128)(2,1)S(1)}, bf16[344,128]{1,0:T(8,128)(2,1)S(1)}, u32[]{:S(2)}, u32[]{:S(2)}) collective-permute-start(bf16[344,128]{1,0:T(8,128)(2,1)S(1)} %get-tuple-element.31.total_ref), channel_id=1, source_target_pairs={{0,32},{32,64},{64,96},{96,128},{128,160},{160,192},{192,224},{1,3... | collective-permute-start | bytes 264200 | tf_op jit(solution)/shard_map/ppermute | solution.py:333
  8.1 4.3 %within.1.out_ref = f32[320,2048]{1,0:T(8,128)S(1)} custom-call(f32[5]{0:T(128)S(1)} %copy-done.3, bf16[320,2048]{1,0:T(8,128)(2,1)S(1)} %get-tuple-element.32.x_ref, bf16[2048,128]{1,0:T(8,128)(2,1)S(1)} %get-tuple-element.33.b_ref, bf16[2048,128]{1,0:T(8,128)(2,1)S(1)} %get-tuple-element.34.c_ref, f32[8,2048]{1,0:T(8,128)S(1)} %get-tuple-element.35.cum_ref, ...), custom_call_target="tpu_custom_call" | custom-call | tf_op jit(solution)/shard_map/within/pallas_call | solution.py:336
  12.4 9.1 %collective-permute-done.8.refs_5_ = bf16[320,2560]{1,0:T(8,128)(2,1)S(1)} collective-permute-done((bf16[320,2560]{1,0:T(8,128)(2,1)}, bf16[320,2560]{1,0:T(8,128)(2,1)S(1)}, u32[]{:S(2)}, u32[]{:S(2)}) %collective-permute-start.8) | collective-permute-done | bytes 1638432 | tf_op jit(solution)/shard_map/ppermute | solution.py:287
  21.5 1.3 %collective-permute-done.9.refs_8_ = bf16[320,2560]{1,0:T(8,128)(2,1)S(1)} collective-permute-done((bf16[320,2560]{1,0:T(8,128)(2,1)}, bf16[320,2560]{1,0:T(8,128)(2,1)S(1)}, u32[]{:S(2)}, u32[]{:S(2)}) %collective-permute-start.9) | collective-permute-done | bytes 1638432 | tf_op jit(solution)/shard_map/ppermute | solution.py:287
  22.9 1.5 %collective-permute-start.10 = (bf16[160,2560]{1,0:T(8,128)(2,1)S(1)}, bf16[160,2560]{1,0:T(8,128)(2,1)S(1)}, u32[]{:S(2)}, u32[]{:S(2)}) collective-permute-start(bf16[160,2560]{1,0:T(8,128)(2,1)S(1)} %slice.6), channel_id=1, source_target_pairs={{0,2},{1,9},{2,4},{3,11},{4,6},{5,13},{6,0},{7,15},{8,10},{9,17},{... | collective-permute-start | bytes 2457608 | tf_op jit(solution)/shard_map/ppermute | solution.py:287
  24.4 0.7 collective-permute-start.11
  25.1 3.8 %collective-permute-start.1 = (bf16[344,128]{1,0:T(8,128)(2,1)S(1)}, bf16[344,128]{1,0:T(8,128)(2,1)S(1)}, u32[]{:S(2)}, u32[]{:S(2)}) collective-permute-start(bf16[344,128]{1,0:T(8,128)(2,1)S(1)} %pair.1), channel_id=1, source_target_pairs={{0,32},{32,64},{64,96},{96,128},{128,160},{160,192},{192,224},{1,3... | collective-permute-start | bytes 264200 | tf_op jit(solution)/shard_map/ppermute | solution.py:333
  28.9 7.7 %collective-permute-start.2 = (bf16[344,128]{1,0:T(8,128)(2,1)S(1)}, bf16[344,128]{1,0:T(8,128)(2,1)S(1)}, u32[]{:S(2)}, u32[]{:S(2)}) collective-permute-start(bf16[344,128]{1,0:T(8,128)(2,1)S(1)} %pair.1), channel_id=1, source_target_pairs={{0,96},{32,128},{64,160},{96,192},{128,224},{1,97},{33,129},{65,16... | collective-permute-start | bytes 264200 | tf_op jit(solution)/shard_map/ppermute | solution.py:333
  36.7 1.3 %collective-permute-start.3 = (bf16[344,128]{1,0:T(8,128)(2,1)S(1)}, bf16[344,128]{1,0:T(8,128)(2,1)S(1)}, u32[]{:S(2)}, u32[]{:S(2)}) collective-permute-start(bf16[344,128]{1,0:T(8,128)(2,1)S(1)} %pair.1), channel_id=1, source_target_pairs={{0,160},{32,192},{64,224},{1,161},{33,193},{65,225},{2,162},{34,19... | collective-permute-start | bytes 264200 | tf_op jit(solution)/shard_map/ppermute | solution.py:333
  38.0 1.3 %collective-permute-start.4 = (bf16[344,128]{1,0:T(8,128)(2,1)S(1)}, bf16[344,128]{1,0:T(8,128)(2,1)S(1)}, u32[]{:S(2)}, u32[]{:S(2)}) collective-permute-start(bf16[344,128]{1,0:T(8,128)(2,1)S(1)} %pair.1), channel_id=1, source_target_pairs={{0,224},{1,225},{2,226},{3,227},{4,228},{5,229},{6,230},{7,231},{8... | collective-permute-start | bytes 264200 | tf_op jit(solution)/shard_map/ppermute | solution.py:333
  39.3 4.1 %collective-permute-done.3.refs_2_ = bf16[344,128]{1,0:T(8,128)(2,1)S(1)} collective-permute-done((bf16[344,128]{1,0:T(8,128)(2,1)S(1)}, bf16[344,128]{1,0:T(8,128)(2,1)S(1)}, u32[]{:S(2)}, u32[]{:S(2)}) %collective-permute-start.3) | collective-permute-done | bytes 88096 | tf_op jit(solution)/shard_map/ppermute | solution.py:333
  43.5 1.3 %collective-permute-done.4.refs_3_ = bf16[344,128]{1,0:T(8,128)(2,1)S(1)} collective-permute-done((bf16[344,128]{1,0:T(8,128)(2,1)S(1)}, bf16[344,128]{1,0:T(8,128)(2,1)S(1)}, u32[]{:S(2)}, u32[]{:S(2)}) %collective-permute-start.4) | collective-permute-done | bytes 88096 | tf_op jit(solution)/shard_map/ppermute | solution.py:333
  44.8 1.3 %gate.1 = (bf16[320,512]{1,0:T(8,128)(2,1)S(1)}, bf16[320,512]{1,0:T(8,128)(2,1)S(1)}, bf16[320,512]{1,0:T(8,128)(2,1)S(1)}, bf16[320,512]{1,0:T(8,128)(2,1)S(1)}) custom-call(f32[320,2048]{1,0:T(8,128)S(1)} %within.1.out_ref, bf16[320,2048]{1,0:T(8,128)(2,1)S(1)} %bitcast.3, bf16[2048,128]{1,0:T(8,128)(2,1)S(1)} %get-tuple-element.34.c_ref, ...), custom_call_target="tpu_custom_call" | custom-call | tf_op jit(solution)/shard_map/gate/pallas_call | solution.py:362
  46.1 1.5 %collective-permute-start.5 = (bf16[320,512]{1,0:T(8,128)(2,1)S(1)}, bf16[320,512]{1,0:T(8,128)(2,1)S(1)}, u32[]{:S(2)}, u32[]{:S(2)}) collective-permute-start(bf16[320,512]{1,0:T(8,128)(2,1)S(1)} %get-tuple-element.42), channel_id=1, source_target_pairs={{0,2},{1,9},{2,4},{3,11},{4,6},{5,13},{6,0},{7,15},{8,10},{9,17},{... | collective-permute-start | bytes 983048 | tf_op jit(solution)/shard_map/ppermute | solution.py:287
  47.7 1.1 %collective-permute-start.6 = (bf16[320,512]{1,0:T(8,128)(2,1)S(1)}, bf16[320,512]{1,0:T(8,128)(2,1)S(1)}, u32[]{:S(2)}, u32[]{:S(2)}) collective-permute-start(bf16[320,512]{1,0:T(8,128)(2,1)S(1)} %get-tuple-element.43), channel_id=1, source_target_pairs={{0,4},{1,17},{2,6},{3,19},{4,0},{5,21},{6,2},{7,23},{8,12},{9,25},... | collective-permute-start | bytes 983048 | tf_op jit(solution)/shard_map/ppermute | solution.py:287
  48.8 2.1 %collective-permute-start.7 = (bf16[320,512]{1,0:T(8,128)(2,1)S(1)}, bf16[320,512]{1,0:T(8,128)(2,1)S(1)}, u32[]{:S(2)}, u32[]{:S(2)}) collective-permute-start(bf16[320,512]{1,0:T(8,128)(2,1)S(1)} %get-tuple-element.44), channel_id=1, source_target_pairs={{0,6},{1,25},{2,0},{3,27},{4,2},{5,29},{6,4},{7,31},{8,14},{9,1},{... | collective-permute-start | bytes 983048 | tf_op jit(solution)/shard_map/ppermute | solution.py:287
  50.9 2.4 %collective-permute-done.5.refs_1_ = bf16[320,512]{1,0:T(8,128)(2,1)S(1)} collective-permute-done((bf16[320,512]{1,0:T(8,128)(2,1)S(1)}, bf16[320,512]{1,0:T(8,128)(2,1)S(1)}, u32[]{:S(2)}, u32[]{:S(2)}) %collective-permute-start.5) | collective-permute-done | bytes 327712 | tf_op jit(solution)/shard_map/ppermute | solution.py:287
  53.3 3.1 %collective-permute-done.6.refs_2_ = bf16[320,512]{1,0:T(8,128)(2,1)S(1)} collective-permute-done((bf16[320,512]{1,0:T(8,128)(2,1)S(1)}, bf16[320,512]{1,0:T(8,128)(2,1)S(1)}, u32[]{:S(2)}, u32[]{:S(2)}) %collective-permute-start.6) | collective-permute-done | bytes 327712 | tf_op jit(solution)/shard_map/ppermute | solution.py:287
  56.4 3.0 %collective-permute-done.7.refs_3_ = bf16[320,512]{1,0:T(8,128)(2,1)S(1)} collective-permute-done((bf16[320,512]{1,0:T(8,128)(2,1)S(1)}, bf16[320,512]{1,0:T(8,128)(2,1)S(1)}, u32[]{:S(2)}, u32[]{:S(2)}) %collective-permute-start.7) | collective-permute-done | bytes 327712 | tf_op jit(solution)/shard_map/ppermute | solution.py:287
  59.4 1.2 %opposite.1 = (bf16[136,1280]{1,0:T(8,128)(2,1)S(1)}, bf16[128,1280]{1,0:T(8,128)(2,1)S(1)}) custom-call(f32[40,128]{1,0:T(8,128)S(1)} %bitcast.4, bf16[320,512]{1,0:T(8,128)(2,1)S(1)} %get-tuple-element.41.refs_0_, bf16[320,512]{1,0:T(8,128)(2,1)S(1)} %collective-permute-done.5.refs_1_, bf16[320,512]{1,0:T(8,128)(2,1)S(1)} %collective-permute-done.6.refs_2_, ...), custom_call_target="tpu_custom_call" | custom-call | tf_op jit(solution)/shard_map/opposite/pallas_call | solution.py:376
  60.6 1.0 %collective-permute-start.12 = (bf16[136,1280]{1,0:T(8,128)(2,1)S(1)}, bf16[136,1280]{1,0:T(8,128)(2,1)S(1)}, u32[]{:S(2)}, u32[]{:S(2)}) collective-permute-start(bf16[136,1280]{1,0:T(8,128)(2,1)S(1)} %get-tuple-element.51), channel_id=1, source_target_pairs={{0,8},{1,3},{2,10},{3,5},{4,12},{5,7},{6,14},{7,1},{8,16},{9,11},{... | collective-permute-start | bytes 1044488 | tf_op jit(solution)/shard_map/ppermute | solution.py:287
  61.6 2.5 %collective-permute-start.13 = (bf16[128,1280]{1,0:T(8,128)(2,1)S(1)}, bf16[128,1280]{1,0:T(8,128)(2,1)S(1)}, u32[]{:S(2)}, u32[]{:S(2)}) collective-permute-start(bf16[128,1280]{1,0:T(8,128)(2,1)S(1)} %get-tuple-element.52), channel_id=1, source_target_pairs={{0,24},{1,7},{2,26},{3,1},{4,28},{5,3},{6,30},{7,5},{8,0},{9,15},{... | collective-permute-start | bytes 983048 | tf_op jit(solution)/shard_map/ppermute | solution.py:287
  64.1 2.9 %project.1 = (bf16[136,1280]{1,0:T(8,128)(2,1)S(1)}, bf16[128,1280]{1,0:T(8,128)(2,1)S(1)}, bf16[136,1280]{1,0:T(8,128)(2,1)S(1)}, bf16[128,1280]{1,0:T(8,128)(2...) custom-call(f32[40,128]{1,0:T(8,128)S(1)} %bitcast.5, bf16[320,512]{1,0:T(8,128)(2,1)S(1)} %get-tuple-element.41.refs_0_, ...), custom_call_target="tpu_custom_call" | custom-call | tf_op jit(solution)/shard_map/project/pallas_call | solution.py:387
  67.7 1.0 %collective-permute-done.13.got_second = bf16[128,1280]{1,0:T(8,128)(2,1)S(1)} collective-permute-done((bf16[128,1280]{1,0:T(8,128)(2,1)S(1)}, bf16[128,1280]{1,0:T(8,128)(2,1)S(1)}, u32[]{:S(2)}, u32[]{:S(2)}) %collective-permute-start.13) | collective-permute-done | bytes 327712 | tf_op jit(solution)/shard_map/ppermute | solution.py:287
  69.6 0.7 collective-permute-start.14
  70.3 1.2 %collective-permute-start.15 = (bf16[128,1280]{1,0:T(8,128)(2,1)S(1)}, bf16[128,1280]{1,0:T(8,128)(2,1)S(1)}, u32[]{:S(2)}, u32[]{:S(2)}) collective-permute-start(bf16[128,1280]{1,0:T(8,128)(2,1)S(1)} %get-tuple-element.54), channel_id=1, source_target_pairs={{0,8},{1,3},{2,10},{3,5},{4,12},{5,7},{6,14},{7,1},{8,16},{9,11},{... | collective-permute-start | bytes 983048 | tf_op jit(solution)/shard_map/ppermute | solution.py:287
  71.5 2.0 %collective-permute-start.17 = (bf16[128,1280]{1,0:T(8,128)(2,1)S(1)}, bf16[128,1280]{1,0:T(8,128)(2,1)S(1)}, u32[]{:S(2)}, u32[]{:S(2)}) collective-permute-start(bf16[128,1280]{1,0:T(8,128)(2,1)S(1)} %get-tuple-element.56), channel_id=1, source_target_pairs={{0,24},{1,7},{2,26},{3,1},{4,28},{5,3},{6,30},{7,5},{8,0},{9,15},{... | collective-permute-start | bytes 983048 | tf_op jit(solution)/shard_map/ppermute | solution.py:287
  73.5 8.2 %collective-permute-done.15.refs_3_ = bf16[128,1280]{1,0:T(8,128)(2,1)S(1)} collective-permute-done((bf16[128,1280]{1,0:T(8,128)(2,1)S(1)}, bf16[128,1280]{1,0:T(8,128)(2,1)S(1)}, u32[]{:S(2)}, u32[]{:S(2)}) %collective-permute-start.15) | collective-permute-done | bytes 327712 | tf_op jit(solution)/shard_map/ppermute | solution.py:287
  81.7 1.2 %finish.1 = bf16[128,2560]{1,0:T(8,128)(2,1)} custom-call(f32[128,2560]{1,0:T(8,128)S(1)} %get-tuple-element.47.refs_0_, f32[8,128]{1,0:T(8,128)S(1)} %get-tuple-element.48.refs_1_, bf16[136,1280]{1,0:T(8,128)(2,1)S(1)} %collective-permute-done.14.refs_2_, bf16[128,1280]{1,0:T(8,128)(2,1)S(1)} %collective-permute-done.15.refs_3_, ...), custom_call_target="tpu_custom_call" | custom-call | tf_op jit(solution)/shard_map/finish/pallas_call | solution.py:409
  (22 shorter events, 1.7 us)
Async XLA Ops:
  0.0 21.5 %collective-permute-start.8 = (bf16[320,2560]{1,0:T(8,128)(2,1)}, bf16[320,2560]{1,0:T(8,128)(2,1)S(1)}, u32[]{:S(2)}, u32[]{:S(2)}) collective-permute-start(bf16[320,2560]{1,0:T(8,128)(2,1)} %refs_4_.3), channel_id=1, source_target_pairs={{0,2},{1,9},{2,4},{3,11},{4,6},{5,13},{6,0},{7,15},{8,10},{9,17},{... | collective-permute-start | bytes 4915208 | tf_op jit(solution)/shard_map/ppermute | solution.py:287
  1.5 21.3 %collective-permute-start.9 = (bf16[320,2560]{1,0:T(8,128)(2,1)}, bf16[320,2560]{1,0:T(8,128)(2,1)S(1)}, u32[]{:S(2)}, u32[]{:S(2)}) collective-permute-start(bf16[320,2560]{1,0:T(8,128)(2,1)} %refs_4_.3), channel_id=1, source_target_pairs={{0,6},{1,25},{2,0},{3,27},{4,2},{5,29},{6,4},{7,31},{8,14},{9,1},{... | collective-permute-start | bytes 4915208 | tf_op jit(solution)/shard_map/ppermute | solution.py:287
  2.2 5.8 %copy-start.3 = (f32[5]{0:T(128)S(1)}, f32[5]{0:T(128)}, u32[]{:S(2)}) copy-start(f32[5]{0:T(128)} %skip_ref.1) | copy-start | bytes 64
  4.4 7.9 %collective-permute-start = (bf16[344,128]{1,0:T(8,128)(2,1)S(1)}, bf16[344,128]{1,0:T(8,128)(2,1)S(1)}, u32[]{:S(2)}, u32[]{:S(2)}) collective-permute-start(bf16[344,128]{1,0:T(8,128)(2,1)S(1)} %get-tuple-element.31.total_ref), channel_id=1, source_target_pairs={{0,32},{32,64},{64,96},{96,128},{128,160},{160,192},{192,224},{1,3... | collective-permute-start | bytes 264200 | tf_op jit(solution)/shard_map/ppermute | solution.py:333
  12.4 32.4 %copy-start.1 = (bf16[2048,320]{0,1:T(8,128)(2,1)S(1)}, bf16[2048,320]{0,1:T(8,128)(2,1)}, u32[]{:S(2)}) copy-start(bf16[2048,320]{0,1:T(8,128)(2,1)} %param.10) | copy-start | bytes 3932164
  22.9 36.5 %collective-permute-start.10 = (bf16[160,2560]{1,0:T(8,128)(2,1)S(1)}, bf16[160,2560]{1,0:T(8,128)(2,1)S(1)}, u32[]{:S(2)}, u32[]{:S(2)}) collective-permute-start(bf16[160,2560]{1,0:T(8,128)(2,1)S(1)} %slice.6), channel_id=1, source_target_pairs={{0,2},{1,9},{2,4},{3,11},{4,6},{5,13},{6,0},{7,15},{8,10},{9,17},{... | collective-permute-start | bytes 2457608 | tf_op jit(solution)/shard_map/ppermute | solution.py:287
  24.4 35.0 %collective-permute-start.11 = (bf16[160,2560]{1,0:T(8,128)(2,1)S(1)}, bf16[160,2560]{1,0:T(8,128)(2,1)S(1)}, u32[]{:S(2)}, u32[]{:S(2)}) collective-permute-start(bf16[160,2560]{1,0:T(8,128)(2,1)S(1)} %slice.7), channel_id=1, source_target_pairs={{0,6},{1,25},{2,0},{3,27},{4,2},{5,29},{6,4},{7,31},{8,14},{9,1},{... | collective-permute-start | bytes 2457608 | tf_op jit(solution)/shard_map/ppermute | solution.py:287
  25.1 12.9 %collective-permute-start.1 = (bf16[344,128]{1,0:T(8,128)(2,1)S(1)}, bf16[344,128]{1,0:T(8,128)(2,1)S(1)}, u32[]{:S(2)}, u32[]{:S(2)}) collective-permute-start(bf16[344,128]{1,0:T(8,128)(2,1)S(1)} %pair.1), channel_id=1, source_target_pairs={{0,32},{32,64},{64,96},{96,128},{128,160},{160,192},{192,224},{1,3... | collective-permute-start | bytes 264200 | tf_op jit(solution)/shard_map/ppermute | solution.py:333
  28.9 10.4 %collective-permute-start.2 = (bf16[344,128]{1,0:T(8,128)(2,1)S(1)}, bf16[344,128]{1,0:T(8,128)(2,1)S(1)}, u32[]{:S(2)}, u32[]{:S(2)}) collective-permute-start(bf16[344,128]{1,0:T(8,128)(2,1)S(1)} %pair.1), channel_id=1, source_target_pairs={{0,96},{32,128},{64,160},{96,192},{128,224},{1,97},{33,129},{65,16... | collective-permute-start | bytes 264200 | tf_op jit(solution)/shard_map/ppermute | solution.py:333
  36.7 6.8 %collective-permute-start.3 = (bf16[344,128]{1,0:T(8,128)(2,1)S(1)}, bf16[344,128]{1,0:T(8,128)(2,1)S(1)}, u32[]{:S(2)}, u32[]{:S(2)}) collective-permute-start(bf16[344,128]{1,0:T(8,128)(2,1)S(1)} %pair.1), channel_id=1, source_target_pairs={{0,160},{32,192},{64,224},{1,161},{33,193},{65,225},{2,162},{34,19... | collective-permute-start | bytes 264200 | tf_op jit(solution)/shard_map/ppermute | solution.py:333
  38.0 6.8 %collective-permute-start.4 = (bf16[344,128]{1,0:T(8,128)(2,1)S(1)}, bf16[344,128]{1,0:T(8,128)(2,1)S(1)}, u32[]{:S(2)}, u32[]{:S(2)}) collective-permute-start(bf16[344,128]{1,0:T(8,128)(2,1)S(1)} %pair.1), channel_id=1, source_target_pairs={{0,224},{1,225},{2,226},{3,227},{4,228},{5,229},{6,230},{7,231},{8... | collective-permute-start | bytes 264200 | tf_op jit(solution)/shard_map/ppermute | solution.py:333
  44.8 14.6 %copy-start = (bf16[320,2560]{1,0:T(8,128)(2,1)S(1)}, bf16[320,2560]{1,0:T(8,128)(2,1)}, u32[]{:S(2)}) copy-start(bf16[320,2560]{1,0:T(8,128)(2,1)} %refs_4_.3) | copy-start | bytes 4915204
  44.8 14.6 %copy-start.2 = (f32[5120]{0:T(1024)S(1)}, f32[5120]{0:T(1024)}, u32[]{:S(2)}) copy-start(f32[5120]{0:T(1024)} %param.16) | copy-start | bytes 61444
  46.1 7.2 %collective-permute-start.5 = (bf16[320,512]{1,0:T(8,128)(2,1)S(1)}, bf16[320,512]{1,0:T(8,128)(2,1)S(1)}, u32[]{:S(2)}, u32[]{:S(2)}) collective-permute-start(bf16[320,512]{1,0:T(8,128)(2,1)S(1)} %get-tuple-element.42), channel_id=1, source_target_pairs={{0,2},{1,9},{2,4},{3,11},{4,6},{5,13},{6,0},{7,15},{8,10},{9,17},{... | collective-permute-start | bytes 983048 | tf_op jit(solution)/shard_map/ppermute | solution.py:287
  47.7 8.7 %collective-permute-start.6 = (bf16[320,512]{1,0:T(8,128)(2,1)S(1)}, bf16[320,512]{1,0:T(8,128)(2,1)S(1)}, u32[]{:S(2)}, u32[]{:S(2)}) collective-permute-start(bf16[320,512]{1,0:T(8,128)(2,1)S(1)} %get-tuple-element.43), channel_id=1, source_target_pairs={{0,4},{1,17},{2,6},{3,19},{4,0},{5,21},{6,2},{7,23},{8,12},{9,25},... | collective-permute-start | bytes 983048 | tf_op jit(solution)/shard_map/ppermute | solution.py:287
  48.8 10.6 %collective-permute-start.7 = (bf16[320,512]{1,0:T(8,128)(2,1)S(1)}, bf16[320,512]{1,0:T(8,128)(2,1)S(1)}, u32[]{:S(2)}, u32[]{:S(2)}) collective-permute-start(bf16[320,512]{1,0:T(8,128)(2,1)S(1)} %get-tuple-element.44), channel_id=1, source_target_pairs={{0,6},{1,25},{2,0},{3,27},{4,2},{5,29},{6,4},{7,31},{8,14},{9,1},{... | collective-permute-start | bytes 983048 | tf_op jit(solution)/shard_map/ppermute | solution.py:287
  60.6 8.8 %collective-permute-start.12 = (bf16[136,1280]{1,0:T(8,128)(2,1)S(1)}, bf16[136,1280]{1,0:T(8,128)(2,1)S(1)}, u32[]{:S(2)}, u32[]{:S(2)}) collective-permute-start(bf16[136,1280]{1,0:T(8,128)(2,1)S(1)} %get-tuple-element.51), channel_id=1, source_target_pairs={{0,8},{1,3},{2,10},{3,5},{4,12},{5,7},{6,14},{7,1},{8,16},{9,11},{... | collective-permute-start | bytes 1044488 | tf_op jit(solution)/shard_map/ppermute | solution.py:287
  61.6 7.1 %collective-permute-start.13 = (bf16[128,1280]{1,0:T(8,128)(2,1)S(1)}, bf16[128,1280]{1,0:T(8,128)(2,1)S(1)}, u32[]{:S(2)}, u32[]{:S(2)}) collective-permute-start(bf16[128,1280]{1,0:T(8,128)(2,1)S(1)} %get-tuple-element.52), channel_id=1, source_target_pairs={{0,24},{1,7},{2,26},{3,1},{4,28},{5,3},{6,30},{7,5},{8,0},{9,15},{... | collective-permute-start | bytes 983048 | tf_op jit(solution)/shard_map/ppermute | solution.py:287
  67.0 14.7 %collective-permute-start.16 = (bf16[136,1280]{1,0:T(8,128)(2,1)S(1)}, bf16[136,1280]{1,0:T(8,128)(2,1)S(1)}, u32[]{:S(2)}, u32[]{:S(2)}) collective-permute-start(bf16[136,1280]{1,0:T(8,128)(2,1)S(1)} %get-tuple-element.55), channel_id=1, source_target_pairs={{0,24},{1,7},{2,26},{3,1},{4,28},{5,3},{6,30},{7,5},{8,0},{9,15},{... | collective-permute-start | bytes 1044488 | tf_op jit(solution)/shard_map/ppermute | solution.py:287
  69.6 12.1 %collective-permute-start.14 = (bf16[136,1280]{1,0:T(8,128)(2,1)S(1)}, bf16[136,1280]{1,0:T(8,128)(2,1)S(1)}, u32[]{:S(2)}, u32[]{:S(2)}) collective-permute-start(bf16[136,1280]{1,0:T(8,128)(2,1)S(1)} %get-tuple-element.53), channel_id=1, source_target_pairs={{0,8},{1,3},{2,10},{3,5},{4,12},{5,7},{6,14},{7,1},{8,16},{9,11},{... | collective-permute-start | bytes 1044488 | tf_op jit(solution)/shard_map/ppermute | solution.py:287
  70.3 11.4 %collective-permute-start.15 = (bf16[128,1280]{1,0:T(8,128)(2,1)S(1)}, bf16[128,1280]{1,0:T(8,128)(2,1)S(1)}, u32[]{:S(2)}, u32[]{:S(2)}) collective-permute-start(bf16[128,1280]{1,0:T(8,128)(2,1)S(1)} %get-tuple-element.54), channel_id=1, source_target_pairs={{0,8},{1,3},{2,10},{3,5},{4,12},{5,7},{6,14},{7,1},{8,16},{9,11},{... | collective-permute-start | bytes 983048 | tf_op jit(solution)/shard_map/ppermute | solution.py:287
  71.5 10.2 %collective-permute-start.17 = (bf16[128,1280]{1,0:T(8,128)(2,1)S(1)}, bf16[128,1280]{1,0:T(8,128)(2,1)S(1)}, u32[]{:S(2)}, u32[]{:S(2)}) collective-permute-start(bf16[128,1280]{1,0:T(8,128)(2,1)S(1)} %get-tuple-element.56), channel_id=1, source_target_pairs={{0,24},{1,7},{2,26},{3,1},{4,28},{5,3},{6,30},{7,5},{8,0},{9,15},{... | collective-permute-start | bytes 983048 | tf_op jit(solution)/shard_map/ppermute | solution.py:287

commit v3 on v2

--- a/solution.py
+++ b/solution.py
@@ -297,7 +297,9 @@
     seq_count = lax.axis_size("seq")
     core, u, v = ring_place()
     following = RING - 1
-    weight_before, weight_after = ring(out_weight, 1, True), ring(out_weight, following, True)
+    middle = channels // 2
+    own_upper, own_lower = out_weight[:middle], out_weight[middle:]
+    before_upper, after_lower = ring(own_upper, 1, True), ring(own_lower, following, True)
 
     params = pltpu.CompilerParams(vmem_limit_bytes=24 * 1024 * 1024)
     near = pl.BlockSpec(memory_space=pltpu.VMEM)
@@ -333,6 +335,7 @@
         return lax.ppermute(value, "seq", [(k, k + shift) for k in range(seq_count - shift)])
 
     before = along(total, 1)
+    before_lower, after_upper = ring(own_lower, 1, True), ring(own_upper, following, True)
     local = pl.pallas_call(
         within_kernel,
         in_specs=[pl.BlockSpec(memory_space=pltpu.SMEM)] + [near] * 6,
@@ -341,7 +344,9 @@
         compiler_params=params,
         name="within",
     )(skip_gain, *hold(x_own, b_own, c_own, cum, step_own, prefix))
-    before, local = lax.optimization_barrier((before, local))
+    before, local, upper, lower = lax.optimization_barrier((before, local, before_upper, after_lower))
+    upper, lower = ring(upper, 1, True), ring(lower, following, True)
+    weights = [own_upper, own_lower, before_upper, before_lower, upper, lower, after_upper, after_lower]
     pair = pl.pallas_call(
         pair_kernel,
         in_specs=[near] * 2,
@@ -351,12 +356,6 @@
         name="pair",
     )(*hold(total, before))
     totals = [along(pair, shift) for shift in range(1, seq_count, 2)]
-
-    weight_before, weight_after, pair = lax.optimization_barrier((weight_before, weight_after, pair))
-    middle = channels // 2
-    upper, lower = weight_before[:middle], weight_after[middle:]
-    upper, lower = ring(upper, 1, True), ring(lower, following, True)
-    weights = [out_weight, weight_before, upper, lower, weight_after]
 
     quarter = tokens // RING
     gated = pl.pallas_call(

time: 83 us -> 97.1 us (1.17)
  the two profiles are of different devices: /device:TPU:2 before, /device:TPU:6 now
where the time goes in v3:
time: 97.1 us; the launch traced here: 96.9 us
  starting transfers between devices  53.2 us (55%)
  waiting for transfers between devices  28.9 us (30%)
  Pallas kernels  13.2 us (14%)
  local copies, waits for them, and re-layouts  1.51 us (2%)
    ppermute x5, starting transfers between devices, along(): lax.ppermute(value, 'seq', [(k, k + shift) for k in range(seq_count - shi...  29.4 us
    ppermute x15, starting transfers between devices, ring(): return lax.ppermute(value, ('head', 'batch'), ring_pairs(shift, gather))  23.7 us
    ppermute x15, waiting for transfers between devices, ring(): return lax.ppermute(value, ('head', 'batch'), ring_pairs(shift, gather))  19.8 us
    ppermute x5, waiting for transfers between devices, along(): lax.ppermute(value, 'seq', [(k, k + shift) for k in range(seq_count - shi...  9.04 us
    pallas_call x1, Pallas kernels, body(): pl.pallas_call(within_kernel, in_specs=[pl.BlockSpec(memory_space=pltpu.S...  4.27 us
    pallas_call x1, Pallas kernels, body(): pl.pallas_call(project_kernel, in_specs=[near] * len(operands), out_specs...  2.85 us
    pallas_call x1, Pallas kernels, body(): pl.pallas_call(state_kernel, in_specs=[pl.BlockSpec(memory_space=pltpu.HB...  2.16 us
  transfers between devices with their start and end apart: 20, of which 10 were waited for; matrix products, arithmetic and copies ran while one was open for 0% of the time, Pallas kernels for 11%

profile of v3, /device:TPU:6, one launch (start us, length us, event | category | flops | bytes accessed | tf_op | source)
XLA Modules:
  0.0 96.9 jit_solution(14910729006979745051)
XLA Ops:
  0.0 1.5 %fusion = (bf16[160,2560]{1,0:T(8,128)(2,1)S(1)}, bf16[160,2560]{1,0:T(8,128)(2,1)S(1)}) fusion(bf16[320,2560]{1,0:T(8,128)(2,1)} %param.17), kind=kLoop, calls=%fused_computation | loop fusion | bytes 3276800 | tf_op jit(solution)/shard_map/slice | solution.py:301
  1.5 2.3 %collective-permute-start.1 = (bf16[160,2560]{1,0:T(8,128)(2,1)S(1)}, bf16[160,2560]{1,0:T(8,128)(2,1)S(1)}, u32[]{:S(2)}, u32[]{:S(2)}) collective-permute-start(bf16[160,2560]{1,0:T(8,128)(2,1)S(1)} %get-tuple-element.58.refs_4_), channel_id=1, source_target_pairs={{0,2},{1,9},{2,4},{3,11},{4,6},{5,13},{6,0},{7,15},{8,10},{9,17},{... | collective-permute-start | bytes 2457608 | tf_op jit(solution)/shard_map/ppermute | solution.py:287
  3.8 3.2 %collective-permute-start.10 = (bf16[160,2560]{1,0:T(8,128)(2,1)S(1)}, bf16[160,2560]{1,0:T(8,128)(2,1)S(1)}, u32[]{:S(2)}, u32[]{:S(2)}) collective-permute-start(bf16[160,2560]{1,0:T(8,128)(2,1)S(1)} %get-tuple-element.57.refs_5_), channel_id=1, source_target_pairs={{0,2},{1,9},{2,4},{3,11},{4,6},{5,13},{6,0},{7,15},{8,10},{9,17},{... | collective-permute-start | bytes 2457608 | tf_op jit(solution)/shard_map/ppermute | solution.py:287
  7.0 2.2 %state.1 = (bf16[8,320,128]{2,1,0:T(8,128)(2,1)S(1)}, bf16[344,128]{1,0:T(8,128)(2,1)S(1)}, f32[8,2048]{1,0:T(8,128)S(1)}, f32[8,2048]{1,0:T(8,128)S(1)}, bf16[3...) custom-call(bf16[320,2048]{1,0:T(8,128)(2,1)} %bitcast.6, ...), custom_call_target="tpu_custom_call" | custom-call | tf_op jit(solution)/shard_map/state/pallas_call | solution.py:315
  9.2 2.5 %collective-permute-start = (bf16[344,128]{1,0:T(8,128)(2,1)S(1)}, bf16[344,128]{1,0:T(8,128)(2,1)S(1)}, u32[]{:S(2)}, u32[]{:S(2)}) collective-permute-start(bf16[344,128]{1,0:T(8,128)(2,1)S(1)} %get-tuple-element.31.total_ref), channel_id=1, source_target_pairs={{0,32},{32,64},{64,96},{96,128},{128,160},{160,192},{192,224},{1,3... | collective-permute-start | bytes 264200 | tf_op jit(solution)/shard_map/ppermute | solution.py:335
  11.7 4.3 %within.1.out_ref = f32[320,2048]{1,0:T(8,128)S(1)} custom-call(f32[5]{0:T(128)S(1)} %copy-done.2, bf16[320,2048]{1,0:T(8,128)(2,1)S(1)} %get-tuple-element.32.x_ref, bf16[2048,128]{1,0:T(8,128)(2,1)S(1)} %get-tuple-element.33.b_ref, bf16[2048,128]{1,0:T(8,128)(2,1)S(1)} %get-tuple-element.34.c_ref, f32[8,2048]{1,0:T(8,128)S(1)} %get-tuple-element.35.cum_ref, ...), custom_call_target="tpu_custom_call" | custom-call | tf_op jit(solution)/shard_map/within/pallas_call | solution.py:339
  16.0 1.4 %collective-permute-done.2.refs_11_ = bf16[160,2560]{1,0:T(8,128)(2,1)S(1)} collective-permute-done((bf16[160,2560]{1,0:T(8,128)(2,1)S(1)}, bf16[160,2560]{1,0:T(8,128)(2,1)S(1)}, u32[]{:S(2)}, u32[]{:S(2)}) %collective-permute-start.2) | collective-permute-done | bytes 819232 | tf_op jit(solution)/shard_map/ppermute | solution.py:287
  17.3 1.6 %collective-permute-start.11 = (bf16[160,2560]{1,0:T(8,128)(2,1)S(1)}, bf16[160,2560]{1,0:T(8,128)(2,1)S(1)}, u32[]{:S(2)}, u32[]{:S(2)}) collective-permute-start(bf16[160,2560]{1,0:T(8,128)(2,1)S(1)} %collective-permute-done.1.refs_6_), channel_id=1, source_target_pairs={{0,2},{1,9},{2,4},{3,11},{4,6},{5,13},{6,0},{7,15},{8,10},{9,17},{... | collective-permute-start | bytes 2457608 | tf_op jit(solution)/shard_map/ppermute | solution.py:287
  18.9 0.4 collective-permute-start.12
  19.4 3.4 %collective-permute-start.3 = (bf16[344,128]{1,0:T(8,128)(2,1)S(1)}, bf16[344,128]{1,0:T(8,128)(2,1)S(1)}, u32[]{:S(2)}, u32[]{:S(2)}) collective-permute-start(bf16[344,128]{1,0:T(8,128)(2,1)S(1)} %pair.1), channel_id=1, source_target_pairs={{0,32},{32,64},{64,96},{96,128},{128,160},{160,192},{192,224},{1,3... | collective-permute-start | bytes 264200 | tf_op jit(solution)/shard_map/ppermute | solution.py:335
  22.9 2.8 %collective-permute-done.3.refs_0_ = bf16[344,128]{1,0:T(8,128)(2,1)S(1)} collective-permute-done((bf16[344,128]{1,0:T(8,128)(2,1)S(1)}, bf16[344,128]{1,0:T(8,128)(2,1)S(1)}, u32[]{:S(2)}, u32[]{:S(2)}) %collective-permute-start.3) | collective-permute-done | bytes 88096 | tf_op jit(solution)/shard_map/ppermute | solution.py:335
  25.6 8.3 %collective-permute-start.4 = (bf16[344,128]{1,0:T(8,128)(2,1)S(1)}, bf16[344,128]{1,0:T(8,128)(2,1)S(1)}, u32[]{:S(2)}, u32[]{:S(2)}) collective-permute-start(bf16[344,128]{1,0:T(8,128)(2,1)S(1)} %pair.1), channel_id=1, source_target_pairs={{0,96},{32,128},{64,160},{96,192},{128,224},{1,97},{33,129},{65,16... | collective-permute-start | bytes 264200 | tf_op jit(solution)/shard_map/ppermute | solution.py:335
  33.9 2.1 %collective-permute-done.4.refs_1_ = bf16[344,128]{1,0:T(8,128)(2,1)S(1)} collective-permute-done((bf16[344,128]{1,0:T(8,128)(2,1)S(1)}, bf16[344,128]{1,0:T(8,128)(2,1)S(1)}, u32[]{:S(2)}, u32[]{:S(2)}) %collective-permute-start.4) | collective-permute-done | bytes 88096 | tf_op jit(solution)/shard_map/ppermute | solution.py:335
  36.0 11.0 %collective-permute-start.5 = (bf16[344,128]{1,0:T(8,128)(2,1)S(1)}, bf16[344,128]{1,0:T(8,128)(2,1)S(1)}, u32[]{:S(2)}, u32[]{:S(2)}) collective-permute-start(bf16[344,128]{1,0:T(8,128)(2,1)S(1)} %pair.1), channel_id=1, source_target_pairs={{0,160},{32,192},{64,224},{1,161},{33,193},{65,225},{2,162},{34,19... | collective-permute-start | bytes 264200 | tf_op jit(solution)/shard_map/ppermute | solution.py:335
  47.0 2.1 %collective-permute-done.5.refs_2_ = bf16[344,128]{1,0:T(8,128)(2,1)S(1)} collective-permute-done((bf16[344,128]{1,0:T(8,128)(2,1)S(1)}, bf16[344,128]{1,0:T(8,128)(2,1)S(1)}, u32[]{:S(2)}, u32[]{:S(2)}) %collective-permute-start.5) | collective-permute-done | bytes 88096 | tf_op jit(solution)/shard_map/ppermute | solution.py:335
  49.1 4.3 %collective-permute-start.6 = (bf16[344,128]{1,0:T(8,128)(2,1)S(1)}, bf16[344,128]{1,0:T(8,128)(2,1)S(1)}, u32[]{:S(2)}, u32[]{:S(2)}) collective-permute-start(bf16[344,128]{1,0:T(8,128)(2,1)S(1)} %pair.1), channel_id=1, source_target_pairs={{0,224},{1,225},{2,226},{3,227},{4,228},{5,229},{6,230},{7,231},{8... | collective-permute-start | bytes 264200 | tf_op jit(solution)/shard_map/ppermute | solution.py:335
  53.4 2.1 %collective-permute-done.6.refs_3_ = bf16[344,128]{1,0:T(8,128)(2,1)S(1)} collective-permute-done((bf16[344,128]{1,0:T(8,128)(2,1)S(1)}, bf16[344,128]{1,0:T(8,128)(2,1)S(1)}, u32[]{:S(2)}, u32[]{:S(2)}) %collective-permute-start.6) | collective-permute-done | bytes 88096 | tf_op jit(solution)/shard_map/ppermute | solution.py:335
  55.5 1.3 %gate.1 = (bf16[320,512]{1,0:T(8,128)(2,1)S(1)}, bf16[320,512]{1,0:T(8,128)(2,1)S(1)}, bf16[320,512]{1,0:T(8,128)(2,1)S(1)}, bf16[320,512]{1,0:T(8,128)(2,1)S(1)}) custom-call(f32[320,2048]{1,0:T(8,128)S(1)} %within.1.out_ref, bf16[320,2048]{1,0:T(8,128)(2,1)S(1)} %bitcast.3, bf16[2048,128]{1,0:T(8,128)(2,1)S(1)} %get-tuple-element.34.c_ref, ...), custom_call_target="tpu_custom_call" | custom-call | tf_op jit(solution)/shard_map/gate/pallas_call | solution.py:361
  56.9 2.7 %collective-permute-start.8 = (bf16[320,512]{1,0:T(8,128)(2,1)S(1)}, bf16[320,512]{1,0:T(8,128)(2,1)S(1)}, u32[]{:S(2)}, u32[]{:S(2)}) collective-permute-start(bf16[320,512]{1,0:T(8,128)(2,1)S(1)} %get-tuple-element.43), channel_id=1, source_target_pairs={{0,4},{1,17},{2,6},{3,19},{4,0},{5,21},{6,2},{7,23},{8,12},{9,25},... | collective-permute-start | bytes 983048 | tf_op jit(solution)/shard_map/ppermute | solution.py:287
  59.5 4.4 %collective-permute-done.7.refs_1_ = bf16[320,512]{1,0:T(8,128)(2,1)S(1)} collective-permute-done((bf16[320,512]{1,0:T(8,128)(2,1)S(1)}, bf16[320,512]{1,0:T(8,128)(2,1)S(1)}, u32[]{:S(2)}, u32[]{:S(2)}) %collective-permute-start.7) | collective-permute-done | bytes 327712 | tf_op jit(solution)/shard_map/ppermute | solution.py:287
  63.9 1.7 %collective-permute-done.8.refs_2_ = bf16[320,512]{1,0:T(8,128)(2,1)S(1)} collective-permute-done((bf16[320,512]{1,0:T(8,128)(2,1)S(1)}, bf16[320,512]{1,0:T(8,128)(2,1)S(1)}, u32[]{:S(2)}, u32[]{:S(2)}) %collective-permute-start.8) | collective-permute-done | bytes 327712 | tf_op jit(solution)/shard_map/ppermute | solution.py:287
  65.6 4.2 %collective-permute-done.9.refs_3_ = bf16[320,512]{1,0:T(8,128)(2,1)S(1)} collective-permute-done((bf16[320,512]{1,0:T(8,128)(2,1)S(1)}, bf16[320,512]{1,0:T(8,128)(2,1)S(1)}, u32[]{:S(2)}, u32[]{:S(2)}) %collective-permute-start.9) | collective-permute-done | bytes 327712 | tf_op jit(solution)/shard_map/ppermute | solution.py:287
  69.8 1.2 %opposite.1 = (bf16[136,1280]{1,0:T(8,128)(2,1)S(1)}, bf16[128,1280]{1,0:T(8,128)(2,1)S(1)}) custom-call(f32[40,128]{1,0:T(8,128)S(1)} %bitcast.4, bf16[320,512]{1,0:T(8,128)(2,1)S(1)} %get-tuple-element.41.refs_0_, bf16[320,512]{1,0:T(8,128)(2,1)S(1)} %collective-permute-done.7.refs_1_, bf16[320,512]{1,0:T(8,128)(2,1)S(1)} %collective-permute-done.8.refs_2_, ...), custom_call_target="tpu_custom_call" | custom-call | tf_op jit(solution)/shard_map/opposite/pallas_call | solution.py:375
  71.1 1.9 %collective-permute-start.14 = (bf16[136,1280]{1,0:T(8,128)(2,1)S(1)}, bf16[136,1280]{1,0:T(8,128)(2,1)S(1)}, u32[]{:S(2)}, u32[]{:S(2)}) collective-permute-start(bf16[136,1280]{1,0:T(8,128)(2,1)S(1)} %get-tuple-element.51), channel_id=1, source_target_pairs={{0,8},{1,3},{2,10},{3,5},{4,12},{5,7},{6,14},{7,1},{8,16},{9,11},{... | collective-permute-start | bytes 1044488 | tf_op jit(solution)/shard_map/ppermute | solution.py:287
  72.9 3.1 %collective-permute-start.15 = (bf16[128,1280]{1,0:T(8,128)(2,1)S(1)}, bf16[128,1280]{1,0:T(8,128)(2,1)S(1)}, u32[]{:S(2)}, u32[]{:S(2)}) collective-permute-start(bf16[128,1280]{1,0:T(8,128)(2,1)S(1)} %get-tuple-element.52), channel_id=1, source_target_pairs={{0,24},{1,7},{2,26},{3,1},{4,28},{5,3},{6,30},{7,5},{8,0},{9,15},{... | collective-permute-start | bytes 983048 | tf_op jit(solution)/shard_map/ppermute | solution.py:287
  76.1 2.9 %project.1 = (bf16[136,1280]{1,0:T(8,128)(2,1)S(1)}, bf16[128,1280]{1,0:T(8,128)(2,1)S(1)}, bf16[136,1280]{1,0:T(8,128)(2,1)S(1)}, bf16[128,1280]{1,0:T(8,128)(2...) custom-call(f32[40,128]{1,0:T(8,128)S(1)} %bitcast.5, bf16[320,512]{1,0:T(8,128)(2,1)S(1)} %get-tuple-element.41.refs_0_, ...), custom_call_target="tpu_custom_call" | custom-call | tf_op jit(solution)/shard_map/project/pallas_call | solution.py:386
  78.9 3.2 %collective-permute-start.18 = (bf16[136,1280]{1,0:T(8,128)(2,1)S(1)}, bf16[136,1280]{1,0:T(8,128)(2,1)S(1)}, u32[]{:S(2)}, u32[]{:S(2)}) collective-permute-start(bf16[136,1280]{1,0:T(8,128)(2,1)S(1)} %get-tuple-element.55), channel_id=1, source_target_pairs={{0,24},{1,7},{2,26},{3,1},{4,28},{5,3},{6,30},{7,5},{8,0},{9,15},{... | collective-permute-start | bytes 1044488 | tf_op jit(solution)/shard_map/ppermute | solution.py:287
  82.1 1.4 %collective-permute-done.15.got_second = bf16[128,1280]{1,0:T(8,128)(2,1)S(1)} collective-permute-done((bf16[128,1280]{1,0:T(8,128)(2,1)S(1)}, bf16[128,1280]{1,0:T(8,128)(2,1)S(1)}, u32[]{:S(2)}, u32[]{:S(2)}) %collective-permute-start.15) | collective-permute-done | bytes 327712 | tf_op jit(solution)/shard_map/ppermute | solution.py:287
  83.6 2.1 %collective-permute-start.16 = (bf16[136,1280]{1,0:T(8,128)(2,1)S(1)}, bf16[136,1280]{1,0:T(8,128)(2,1)S(1)}, u32[]{:S(2)}, u32[]{:S(2)}) collective-permute-start(bf16[136,1280]{1,0:T(8,128)(2,1)S(1)} %get-tuple-element.53), channel_id=1, source_target_pairs={{0,8},{1,3},{2,10},{3,5},{4,12},{5,7},{6,14},{7,1},{8,16},{9,11},{... | collective-permute-start | bytes 1044488 | tf_op jit(solution)/shard_map/ppermute | solution.py:287
  86.0 3.0 %collective-permute-start.19 = (bf16[128,1280]{1,0:T(8,128)(2,1)S(1)}, bf16[128,1280]{1,0:T(8,128)(2,1)S(1)}, u32[]{:S(2)}, u32[]{:S(2)}) collective-permute-start(bf16[128,1280]{1,0:T(8,128)(2,1)S(1)} %get-tuple-element.56), channel_id=1, source_target_pairs={{0,24},{1,7},{2,26},{3,1},{4,28},{5,3},{6,30},{7,5},{8,0},{9,15},{... | collective-permute-start | bytes 983048 | tf_op jit(solution)/shard_map/ppermute | solution.py:287
  89.0 6.8 %collective-permute-done.17.refs_3_ = bf16[128,1280]{1,0:T(8,128)(2,1)S(1)} collective-permute-done((bf16[128,1280]{1,0:T(8,128)(2,1)S(1)}, bf16[128,1280]{1,0:T(8,128)(2,1)S(1)}, u32[]{:S(2)}, u32[]{:S(2)}) %collective-permute-start.17) | collective-permute-done | bytes 327712 | tf_op jit(solution)/shard_map/ppermute | solution.py:287
  95.7 1.2 %finish.1 = bf16[128,2560]{1,0:T(8,128)(2,1)} custom-call(f32[128,2560]{1,0:T(8,128)S(1)} %get-tuple-element.47.refs_0_, f32[8,128]{1,0:T(8,128)S(1)} %get-tuple-element.48.refs_1_, bf16[136,1280]{1,0:T(8,128)(2,1)S(1)} %collective-permute-done.16.refs_2_, bf16[128,1280]{1,0:T(8,128)(2,1)S(1)} %collective-permute-done.17.refs_3_, ...), custom_call_target="tpu_custom_call" | custom-call | tf_op jit(solution)/shard_map/finish/pallas_call | solution.py:408
  (23 shorter events, 0.6 us)
Async XLA Ops:
  1.5 14.4 %collective-permute-start.1 = (bf16[160,2560]{1,0:T(8,128)(2,1)S(1)}, bf16[160,2560]{1,0:T(8,128)(2,1)S(1)}, u32[]{:S(2)}, u32[]{:S(2)}) collective-permute-start(bf16[160,2560]{1,0:T(8,128)(2,1)S(1)} %get-tuple-element.58.refs_4_), channel_id=1, source_target_pairs={{0,2},{1,9},{2,4},{3,11},{4,6},{5,13},{6,0},{7,15},{8,10},{9,17},{... | collective-permute-start | bytes 2457608 | tf_op jit(solution)/shard_map/ppermute | solution.py:287
  3.8 13.6 %collective-permute-start.2 = (bf16[160,2560]{1,0:T(8,128)(2,1)S(1)}, bf16[160,2560]{1,0:T(8,128)(2,1)S(1)}, u32[]{:S(2)}, u32[]{:S(2)}) collective-permute-start(bf16[160,2560]{1,0:T(8,128)(2,1)S(1)} %get-tuple-element.57.refs_5_), channel_id=1, source_target_pairs={{0,6},{1,25},{2,0},{3,27},{4,2},{5,29},{6,4},{7,31},{8,14},{9,1},{... | collective-permute-start | bytes 2457608 | tf_op jit(solution)/shard_map/ppermute | solution.py:287
  3.8 53.1 %collective-permute-start.10 = (bf16[160,2560]{1,0:T(8,128)(2,1)S(1)}, bf16[160,2560]{1,0:T(8,128)(2,1)S(1)}, u32[]{:S(2)}, u32[]{:S(2)}) collective-permute-start(bf16[160,2560]{1,0:T(8,128)(2,1)S(1)} %get-tuple-element.57.refs_5_), channel_id=1, source_target_pairs={{0,2},{1,9},{2,4},{3,11},{4,6},{5,13},{6,0},{7,15},{8,10},{9,17},{... | collective-permute-start | bytes 2457608 | tf_op jit(solution)/shard_map/ppermute | solution.py:287
  7.0 52.5 %collective-permute-start.13 = (bf16[160,2560]{1,0:T(8,128)(2,1)S(1)}, bf16[160,2560]{1,0:T(8,128)(2,1)S(1)}, u32[]{:S(2)}, u32[]{:S(2)}) collective-permute-start(bf16[160,2560]{1,0:T(8,128)(2,1)S(1)} %get-tuple-element.58.refs_4_), channel_id=1, source_target_pairs={{0,6},{1,25},{2,0},{3,27},{4,2},{5,29},{6,4},{7,31},{8,14},{9,1},{... | collective-permute-start | bytes 2457608 | tf_op jit(solution)/shard_map/ppermute | solution.py:287
  7.0 4.6 %copy-start.2 = (f32[5]{0:T(128)S(1)}, f32[5]{0:T(128)}, u32[]{:S(2)}) copy-start(f32[5]{0:T(128)} %skip_ref.1) | copy-start | bytes 64
  9.2 6.8 %collective-permute-start = (bf16[344,128]{1,0:T(8,128)(2,1)S(1)}, bf16[344,128]{1,0:T(8,128)(2,1)S(1)}, u32[]{:S(2)}, u32[]{:S(2)}) collective-permute-start(bf16[344,128]{1,0:T(8,128)(2,1)S(1)} %get-tuple-element.31.total_ref), channel_id=1, source_target_pairs={{0,32},{32,64},{64,96},{96,128},{128,160},{160,192},{192,224},{1,3... | collective-permute-start | bytes 264200 | tf_op jit(solution)/shard_map/ppermute | solution.py:335
  11.7 43.8 %copy-start = (bf16[2048,320]{0,1:T(8,128)(2,1)S(1)}, bf16[2048,320]{0,1:T(8,128)(2,1)}, u32[]{:S(2)}) copy-start(bf16[2048,320]{0,1:T(8,128)(2,1)} %param.10) | copy-start | bytes 3932164
  17.3 52.5 %collective-permute-start.11 = (bf16[160,2560]{1,0:T(8,128)(2,1)S(1)}, bf16[160,2560]{1,0:T(8,128)(2,1)S(1)}, u32[]{:S(2)}, u32[]{:S(2)}) collective-permute-start(bf16[160,2560]{1,0:T(8,128)(2,1)S(1)} %collective-permute-done.1.refs_6_), channel_id=1, source_target_pairs={{0,2},{1,9},{2,4},{3,11},{4,6},{5,13},{6,0},{7,15},{8,10},{9,17},{... | collective-permute-start | bytes 2457608 | tf_op jit(solution)/shard_map/ppermute | solution.py:287
  18.9 50.9 %collective-permute-start.12 = (bf16[160,2560]{1,0:T(8,128)(2,1)S(1)}, bf16[160,2560]{1,0:T(8,128)(2,1)S(1)}, u32[]{:S(2)}, u32[]{:S(2)}) collective-permute-start(bf16[160,2560]{1,0:T(8,128)(2,1)S(1)} %collective-permute-done.2.refs_11_), channel_id=1, source_target_pairs={{0,6},{1,25},{2,0},{3,27},{4,2},{5,29},{6,4},{7,31},{8,14},{9,1},{... | collective-permute-start | bytes 2457608 | tf_op jit(solution)/shard_map/ppermute | solution.py:287
  19.4 6.2 %collective-permute-start.3 = (bf16[344,128]{1,0:T(8,128)(2,1)S(1)}, bf16[344,128]{1,0:T(8,128)(2,1)S(1)}, u32[]{:S(2)}, u32[]{:S(2)}) collective-permute-start(bf16[344,128]{1,0:T(8,128)(2,1)S(1)} %pair.1), channel_id=1, source_target_pairs={{0,32},{32,64},{64,96},{96,128},{128,160},{160,192},{192,224},{1,3... | collective-permute-start | bytes 264200 | tf_op jit(solution)/shard_map/ppermute | solution.py:335
  25.6 10.4 %collective-permute-start.4 = (bf16[344,128]{1,0:T(8,128)(2,1)S(1)}, bf16[344,128]{1,0:T(8,128)(2,1)S(1)}, u32[]{:S(2)}, u32[]{:S(2)}) collective-permute-start(bf16[344,128]{1,0:T(8,128)(2,1)S(1)} %pair.1), channel_id=1, source_target_pairs={{0,96},{32,128},{64,160},{96,192},{128,224},{1,97},{33,129},{65,16... | collective-permute-start | bytes 264200 | tf_op jit(solution)/shard_map/ppermute | solution.py:335
  36.0 13.1 %collective-permute-start.5 = (bf16[344,128]{1,0:T(8,128)(2,1)S(1)}, bf16[344,128]{1,0:T(8,128)(2,1)S(1)}, u32[]{:S(2)}, u32[]{:S(2)}) collective-permute-start(bf16[344,128]{1,0:T(8,128)(2,1)S(1)} %pair.1), channel_id=1, source_target_pairs={{0,160},{32,192},{64,224},{1,161},{33,193},{65,225},{2,162},{34,19... | collective-permute-start | bytes 264200 | tf_op jit(solution)/shard_map/ppermute | solution.py:335
  49.1 6.4 %collective-permute-start.6 = (bf16[344,128]{1,0:T(8,128)(2,1)S(1)}, bf16[344,128]{1,0:T(8,128)(2,1)S(1)}, u32[]{:S(2)}, u32[]{:S(2)}) collective-permute-start(bf16[344,128]{1,0:T(8,128)(2,1)S(1)} %pair.1), channel_id=1, source_target_pairs={{0,224},{1,225},{2,226},{3,227},{4,228},{5,229},{6,230},{7,231},{8... | collective-permute-start | bytes 264200 | tf_op jit(solution)/shard_map/ppermute | solution.py:335
  55.5 14.4 %copy-start.1 = (f32[5120]{0:T(1024)S(1)}, f32[5120]{0:T(1024)}, u32[]{:S(2)}) copy-start(f32[5120]{0:T(1024)} %param.16) | copy-start | bytes 61444
  56.8 7.2 %collective-permute-start.7 = (bf16[320,512]{1,0:T(8,128)(2,1)S(1)}, bf16[320,512]{1,0:T(8,128)(2,1)S(1)}, u32[]{:S(2)}, u32[]{:S(2)}) collective-permute-start(bf16[320,512]{1,0:T(8,128)(2,1)S(1)} %get-tuple-element.42), channel_id=1, source_target_pairs={{0,2},{1,9},{2,4},{3,11},{4,6},{5,13},{6,0},{7,15},{8,10},{9,17},{... | collective-permute-start | bytes 983048 | tf_op jit(solution)/shard_map/ppermute | solution.py:287
  56.9 8.8 %collective-permute-start.8 = (bf16[320,512]{1,0:T(8,128)(2,1)S(1)}, bf16[320,512]{1,0:T(8,128)(2,1)S(1)}, u32[]{:S(2)}, u32[]{:S(2)}) collective-permute-start(bf16[320,512]{1,0:T(8,128)(2,1)S(1)} %get-tuple-element.43), channel_id=1, source_target_pairs={{0,4},{1,17},{2,6},{3,19},{4,0},{5,21},{6,2},{7,23},{8,12},{9,25},... | collective-permute-start | bytes 983048 | tf_op jit(solution)/shard_map/ppermute | solution.py:287
  59.5 10.3 %collective-permute-start.9 = (bf16[320,512]{1,0:T(8,128)(2,1)S(1)}, bf16[320,512]{1,0:T(8,128)(2,1)S(1)}, u32[]{:S(2)}, u32[]{:S(2)}) collective-permute-start(bf16[320,512]{1,0:T(8,128)(2,1)S(1)} %get-tuple-element.44), channel_id=1, source_target_pairs={{0,6},{1,25},{2,0},{3,27},{4,2},{5,29},{6,4},{7,31},{8,14},{9,1},{... | collective-permute-start | bytes 983048 | tf_op jit(solution)/shard_map/ppermute | solution.py:287
  71.1 12.4 %collective-permute-start.14 = (bf16[136,1280]{1,0:T(8,128)(2,1)S(1)}, bf16[136,1280]{1,0:T(8,128)(2,1)S(1)}, u32[]{:S(2)}, u32[]{:S(2)}) collective-permute-start(bf16[136,1280]{1,0:T(8,128)(2,1)S(1)} %get-tuple-element.51), channel_id=1, source_target_pairs={{0,8},{1,3},{2,10},{3,5},{4,12},{5,7},{6,14},{7,1},{8,16},{9,11},{... | collective-permute-start | bytes 1044488 | tf_op jit(solution)/shard_map/ppermute | solution.py:287
  72.9 10.5 %collective-permute-start.15 = (bf16[128,1280]{1,0:T(8,128)(2,1)S(1)}, bf16[128,1280]{1,0:T(8,128)(2,1)S(1)}, u32[]{:S(2)}, u32[]{:S(2)}) collective-permute-start(bf16[128,1280]{1,0:T(8,128)(2,1)S(1)} %get-tuple-element.52), channel_id=1, source_target_pairs={{0,24},{1,7},{2,26},{3,1},{4,28},{5,3},{6,30},{7,5},{8,0},{9,15},{... | collective-permute-start | bytes 983048 | tf_op jit(solution)/shard_map/ppermute | solution.py:287
  78.9 16.8 %collective-permute-start.18 = (bf16[136,1280]{1,0:T(8,128)(2,1)S(1)}, bf16[136,1280]{1,0:T(8,128)(2,1)S(1)}, u32[]{:S(2)}, u32[]{:S(2)}) collective-permute-start(bf16[136,1280]{1,0:T(8,128)(2,1)S(1)} %get-tuple-element.55), channel_id=1, source_target_pairs={{0,24},{1,7},{2,26},{3,1},{4,28},{5,3},{6,30},{7,5},{8,0},{9,15},{... | collective-permute-start | bytes 1044488 | tf_op jit(solution)/shard_map/ppermute | solution.py:287
  83.6 12.1 %collective-permute-start.16 = (bf16[136,1280]{1,0:T(8,128)(2,1)S(1)}, bf16[136,1280]{1,0:T(8,128)(2,1)S(1)}, u32[]{:S(2)}, u32[]{:S(2)}) collective-permute-start(bf16[136,1280]{1,0:T(8,128)(2,1)S(1)} %get-tuple-element.53), channel_id=1, source_target_pairs={{0,8},{1,3},{2,10},{3,5},{4,12},{5,7},{6,14},{7,1},{8,16},{9,11},{... | collective-permute-start | bytes 1044488 | tf_op jit(solution)/shard_map/ppermute | solution.py:287
  85.7 10.0 %collective-permute-start.17 = (bf16[128,1280]{1,0:T(8,128)(2,1)S(1)}, bf16[128,1280]{1,0:T(8,128)(2,1)S(1)}, u32[]{:S(2)}, u32[]{:S(2)}) collective-permute-start(bf16[128,1280]{1,0:T(8,128)(2,1)S(1)} %get-tuple-element.54), channel_id=1, source_target_pairs={{0,8},{1,3},{2,10},{3,5},{4,12},{5,7},{6,14},{7,1},{8,16},{9,11},{... | collective-permute-start | bytes 983048 | tf_op jit(solution)/shard_map/ppermute | solution.py:287
  86.0 9.8 %collective-permute-start.19 = (bf16[128,1280]{1,0:T(8,128)(2,1)S(1)}, bf16[128,1280]{1,0:T(8,128)(2,1)S(1)}, u32[]{:S(2)}, u32[]{:S(2)}) collective-permute-start(bf16[128,1280]{1,0:T(8,128)(2,1)S(1)} %get-tuple-element.56), channel_id=1, source_target_pairs={{0,24},{1,7},{2,26},{3,1},{4,28},{5,3},{6,30},{7,5},{8,0},{9,15},{... | collective-permute-start | bytes 983048 | tf_op jit(solution)/shard_map/ppermute | solution.py:287

commit v4 on v2

--- a/solution.py
+++ b/solution.py
@@ -190,7 +190,7 @@
     return jnp.where(first % SUB == 0, line, shifted)[:, :channels]
 
 
-def left_side(gain_ref, rows, blocks):
+def left_side(gain_ref, rows, sources, blocks):
     core, u, v = ring_place()
     channels = rows[0].shape[0]
     pick = [slice(k * SUB, (k + 1) * SUB) for k in blocks]
@@ -198,7 +198,7 @@
     wide = values.astype(f32)
     squares = jnp.sum(wide * wide, axis=0, keepdims=True)
     gains = jnp.concatenate(
-        [gain_row(gain_ref, head_at(core, (u - s + RING) % RING, v), channels) for s in range(RING)], axis=1
+        [gain_row(gain_ref, head_at(core, (u - s + RING) % RING, v), channels) for s in sources], axis=1
     )
     return (values.T.astype(f32) * gains).astype(bf16), squares
 
@@ -213,43 +213,60 @@
     return jnp.sum(part[SUB:, 0:SUB].astype(f32), axis=0, keepdims=True)
 
 
-def opposite_kernel(gain_ref, *refs):
-    rows, weights = refs[:RING], refs[RING:-3]
+def begin_kernel(gain_ref, *refs):
+    rows, weights = refs[:2], refs[2:-3]
+    product_ref, squares_ref, left = refs[-3:]
+    left[...], squares = left_side(gain_ref, rows, (0, 1), range(RING))
+    squares_ref[...] = jnp.broadcast_to(squares, squares_ref.shape)
+    tile = 256
+    for n in range(product_ref.shape[1] // tile):
+        span = slice(n * tile, (n + 1) * tile)
+        right = jnp.concatenate([w[:, span] for w in weights], axis=0)
+        product_ref[:, span] = jnp.dot(left[...], right, preferred_element_type=f32)
+
+
+def opposite_kernel(gain_ref, begun_ref, begun_squares, *refs):
+    rows, weights = refs[:2], refs[2:-3]
     first_ref, second_ref, left = refs[-3:]
     half = first_ref.shape[1]
-    left[...], squares = left_side(gain_ref, rows, (2,))
-    first_ref[SUB:, :] = tail_rows(squares, half)
+    block = slice(2 * SUB, 3 * SUB)
+    left[...], squares = left_side(gain_ref, rows, (2, 3), (2,))
+    first_ref[SUB:, :] = tail_rows(squares + begun_squares[0:1, block], half)
     tile = 256
     for n in range(2 * half // tile):
-        right = jnp.concatenate([w[:, n * tile : (n + 1) * tile] for w in weights], axis=0)
-        product = jnp.dot(left[...], right, preferred_element_type=f32).astype(bf16)
+        span = slice(n * tile, (n + 1) * tile)
+        right = jnp.concatenate([w[:, span] for w in weights], axis=0)
+        product = begun_ref[block, span] + jnp.dot(left[...], right, preferred_element_type=f32)
         if n * tile < half:
-            first_ref[0:SUB, n * tile : (n + 1) * tile] = product
+            first_ref[0:SUB, span] = product.astype(bf16)
         else:
-            second_ref[:, n * tile - half : (n + 1) * tile - half] = product
-
-
-def project_kernel(gain_ref, *refs):
-    rows, weights = refs[:RING], refs[RING:-7]
+            second_ref[:, n * tile - half : (n + 1) * tile - half] = product.astype(bf16)
+
+
+def project_kernel(gain_ref, begun_ref, begun_squares, *refs):
+    rows, weights = refs[:2], refs[2:-7]
     next_first, next_second, last_first, last_second, own_ref, own_squares, left = refs[-7:]
     half = next_first.shape[1]
-    left[...], squares = left_side(gain_ref, rows, (1, 3, 0))
-    next_first[SUB:, :] = tail_rows(squares[:, 0:SUB], half)
-    last_first[SUB:, :] = tail_rows(squares[:, SUB : 2 * SUB], half)
-    own_squares[...] = jnp.broadcast_to(squares[:, 2 * SUB :], own_squares.shape)
+    own, following, previous = slice(0, SUB), slice(SUB, 2 * SUB), slice(3 * SUB, 4 * SUB)
+    left[...], squares = left_side(gain_ref, rows, (2, 3), (1, 3, 0))
+    next_first[SUB:, :] = tail_rows(squares[:, 0:SUB] + begun_squares[0:1, following], half)
+    last_first[SUB:, :] = tail_rows(squares[:, SUB : 2 * SUB] + begun_squares[0:1, previous], half)
+    own_squares[...] = jnp.broadcast_to(squares[:, 2 * SUB :] + begun_squares[0:1, own], own_squares.shape)
     tile = 256
     for n in range(2 * half // tile):
         span = slice(n * tile, (n + 1) * tile)
         right = jnp.concatenate([w[:, span] for w in weights], axis=0)
         product = jnp.dot(left[...], right, preferred_element_type=f32)
-        own_ref[:, span] = product[2 * SUB :]
+        own_ref[:, span] = product[2 * SUB :] + begun_ref[own, span]
+        next_rows = (product[0:SUB] + begun_ref[following, span]).astype(bf16)
+        last_rows = (product[SUB : 2 * SUB] + begun_ref[previous, span]).astype(bf16)
         if n * tile < half:
-            next_first[0:SUB, span] = product[0:SUB].astype(bf16)
-            last_first[0:SUB, span] = product[SUB : 2 * SUB].astype(bf16)
+            next_first[0:SUB, span] = next_rows
+            last_first[0:SUB, span] = last_rows
         else:
             span = slice(n * tile - half, (n + 1) * tile - half)
-            next_second[:, span] = product[0:SUB].astype(bf16)
-            last_second[:, span] = product[SUB : 2 * SUB].astype(bf16)
+            next_second[:, span] = next_rows
+            last_second[:, span] = last_rows
 
 
 def merge_kernel(next_first, last_second, got_first, got_second, next_ref, last_ref):
@@ -333,6 +350,16 @@
         return lax.ppermute(value, "seq", [(k, k + shift) for k in range(seq_count - shift)])
 
     before = along(total, 1)
+    pair = pl.pallas_call(
+        pair_kernel,
+        in_specs=[near] * 2,
+        out_specs=near,
+        out_shape=pltpu.VMEM((payload, STATE), bf16),
+        compiler_params=params,
+        name="pair",
+    )(*hold(total, before))
+    totals = [along(pair, shift) for shift in range(1, seq_count, 2)]
+
     local = pl.pallas_call(
         within_kernel,
         in_specs=[pl.BlockSpec(memory_space=pltpu.SMEM)] + [near] * 6,
@@ -341,22 +368,10 @@
         compiler_params=params,
         name="within",
     )(skip_gain, *hold(x_own, b_own, c_own, cum, step_own, prefix))
-    before, local = lax.optimization_barrier((before, local))
-    pair = pl.pallas_call(
-        pair_kernel,
-        in_specs=[near] * 2,
-        out_specs=near,
-        out_shape=pltpu.VMEM((payload, STATE), bf16),
-        compiler_params=params,
-        name="pair",
-    )(*hold(total, before))
-    totals = [along(pair, shift) for shift in range(1, seq_count, 2)]
-
-    weight_before, weight_after, pair = lax.optimization_barrier((weight_before, weight_after, pair))
+    local, weight_before, weight_after = lax.optimization_barrier((local, weight_before, weight_after))
     middle = channels // 2
     upper, lower = weight_before[:middle], weight_after[middle:]
     upper, lower = ring(upper, 1, True), ring(lower, following, True)
-    weights = [out_weight, weight_before, upper, lower, weight_after]
 
     quarter = tokens // RING
     gated = pl.pallas_call(
@@ -368,16 +383,27 @@
         name="gate",
     )(*hold(local, gate_columns, c_own, factor, *totals))
 
-    rows = [gated[0]] + [ring(gated[s], s, True) for s in range(1, RING)]
+    rows_before = ring(gated[1], 1, True)
+    rows_later = [ring(gated[s], s, True) for s in range(2, RING)]
 
     half = width // 2
     with_tail, without = pltpu.VMEM((SUB + EXTRA, half), bf16), pltpu.VMEM((SUB, half), bf16)
-    operands = hold(norm_gain.reshape(-1, SUB), *rows, *weights)
+    gain_lines = norm_gain.reshape(-1, SUB)
+    begun, begun_squares = pl.pallas_call(
+        begin_kernel,
+        in_specs=[near] * 5,
+        out_specs=[near] * 2,
+        scratch_shapes=[pltpu.VMEM((quarter, 2 * channels), bf16)],
+        out_shape=[pltpu.VMEM((quarter, width), f32), pltpu.VMEM((PAD, quarter), f32)],
+        compiler_params=params,
+        name="begin",
+    )(*hold(gain_lines, gated[0], rows_before, out_weight, weight_before))
+    operands = hold(gain_lines, begun, begun_squares, *rows_later, upper, lower, weight_after)
     opposite_first, opposite_second = pl.pallas_call(
         opposite_kernel,
         in_specs=[near] * len(operands),
         out_specs=[near] * 2,
-        scratch_shapes=[pltpu.VMEM((SUB, RING * channels), bf16)],
+        scratch_shapes=[pltpu.VMEM((SUB, 2 * channels), bf16)],
         out_shape=[with_tail, without],
         compiler_params=params,
         name="opposite",
@@ -388,7 +414,7 @@
         project_kernel,
         in_specs=[near] * len(operands),
         out_specs=[near] * 6,
-        scratch_shapes=[pltpu.VMEM((3 * SUB, RING * channels), bf16)],
+        scratch_shapes=[pltpu.VMEM((3 * SUB, 2 * channels), bf16)],
         out_shape=[with_tail, without, with_tail, without, pltpu.VMEM((SUB, width), f32), pltpu.VMEM((PAD, SUB), f32)],
         compiler_params=params,
         name="project",

time: 83 us -> 88.8 us (1.070)
  starting transfers between devices: 35.1 us -> 38.8 us
  waiting for transfers between devices: 34.2 us -> 35.4 us
  Pallas kernels: 13.3 us -> 14.2 us
    pallas_call x0 -> x1, Pallas kernels: none -> 2.31 us  [body(): pl.pallas_call(begin_kernel, in_specs=[near] * 5, out_specs=[near] * 2, s...]
    ppermute x5, starting transfers between devices: 17.8 us -> 19.7 us  [along(): lax.ppermute(value, 'seq', [(k, k + shift) for k in range(seq_count - shi...]
    ppermute x13, starting transfers between devices: 17.3 us -> 19.2 us  [ring(): return lax.ppermute(value, ('head', 'batch'), ring_pairs(shift, gather))]
    pallas_call x1, Pallas kernels: 2.86 us -> 1.84 us  [body(): pl.pallas_call(project_kernel, in_specs=[near] * len(operands), out_specs...]
  transfers between devices with their start and end apart: 18 -> 18, of which waited for: 10 -> 11; matrix products, arithmetic and copies ran while one was open for 0% -> 0% of each run, Pallas kernels for 13% -> 14%
where the time goes in v4:
time: 88.8 us; the launch traced here: 88.6 us
  starting transfers between devices  38.8 us (44%)
  waiting for transfers between devices  35.4 us (40%)
  Pallas kernels  14.2 us (16%)
    ppermute x13, waiting for transfers between devices, ring(): return lax.ppermute(value, ('head', 'batch'), ring_pairs(shift, gather))  29.5 us
    ppermute x5, starting transfers between devices, along(): lax.ppermute(value, 'seq', [(k, k + shift) for k in range(seq_count - shi...  19.7 us
    ppermute x13, starting transfers between devices, ring(): return lax.ppermute(value, ('head', 'batch'), ring_pairs(shift, gather))  19.2 us
    ppermute x5, waiting for transfers between devices, along(): lax.ppermute(value, 'seq', [(k, k + shift) for k in range(seq_count - shi...  5.85 us
    pallas_call x1, Pallas kernels, body(): pl.pallas_call(within_kernel, in_specs=[pl.BlockSpec(memory_space=pltpu.S...  4.29 us
    pallas_call x1, Pallas kernels, body(): pl.pallas_call(begin_kernel, in_specs=[near] * 5, out_specs=[near] * 2, s...  2.31 us
    pallas_call x1, Pallas kernels, body(): pl.pallas_call(state_kernel, in_specs=[pl.BlockSpec(memory_space=pltpu.HB...  2.17 us
    pallas_call x1, Pallas kernels, body(): pl.pallas_call(project_kernel, in_specs=[near] * len(operands), out_specs...  1.84 us
  transfers between devices with their start and end apart: 18, of which 11 were waited for; matrix products, arithmetic and copies ran while one was open for 0% of the time, Pallas kernels for 14%

profile of v4, /device:TPU:2, one launch (start us, length us, event | category | flops | bytes accessed | tf_op | source)
XLA Modules:
  0.0 88.6 jit_solution(13681714091720766389)
XLA Ops:
  0.0 1.5 %collective-permute-start = (bf16[320,2560]{1,0:T(8,128)(2,1)}, bf16[320,2560]{1,0:T(8,128)(2,1)S(1)}, u32[]{:S(2)}, u32[]{:S(2)}) collective-permute-start(bf16[320,2560]{1,0:T(8,128)(2,1)} %refs_2_.1), channel_id=1, source_target_pairs={{0,2},{1,9},{2,4},{3,11},{4,6},{5,13},{6,0},{7,15},{8,10},{9,17},{... | collective-permute-start | bytes 4915208 | tf_op jit(solution)/shard_map/ppermute | solution.py:304
  2.2 2.2 %state.1 = (bf16[8,320,128]{2,1,0:T(8,128)(2,1)S(1)}, bf16[344,128]{1,0:T(8,128)(2,1)S(1)}, f32[8,2048]{1,0:T(8,128)S(1)}, f32[8,2048]{1,0:T(8,128)S(1)}, bf16[3...) custom-call(bf16[320,2048]{1,0:T(8,128)(2,1)} %bitcast.7, ...), custom_call_target="tpu_custom_call" | custom-call | tf_op jit(solution)/shard_map/state/pallas_call | solution.py:330
  4.4 4.3 %within.1.out_ref = f32[320,2048]{1,0:T(8,128)S(1)} custom-call(f32[5]{0:T(128)S(1)} %copy-done.3, bf16[320,2048]{1,0:T(8,128)(2,1)S(1)} %get-tuple-element.32.x_ref, bf16[2048,128]{1,0:T(8,128)(2,1)S(1)} %get-tuple-element.33.b_ref, bf16[2048,128]{1,0:T(8,128)(2,1)S(1)} %get-tuple-element.34.c_ref, f32[8,2048]{1,0:T(8,128)S(1)} %get-tuple-element.35.cum_ref, ...), custom_call_target="tpu_custom_call" | custom-call | tf_op jit(solution)/shard_map/within/pallas_call | solution.py:363
  8.7 12.8 %collective-permute-done.refs_3_ = bf16[320,2560]{1,0:T(8,128)(2,1)S(1)} collective-permute-done((bf16[320,2560]{1,0:T(8,128)(2,1)}, bf16[320,2560]{1,0:T(8,128)(2,1)S(1)}, u32[]{:S(2)}, u32[]{:S(2)}) %collective-permute-start) | collective-permute-done | bytes 1638432 | tf_op jit(solution)/shard_map/ppermute | solution.py:304
  21.5 1.3 %collective-permute-done.1.refs_4_ = bf16[320,2560]{1,0:T(8,128)(2,1)S(1)} collective-permute-done((bf16[320,2560]{1,0:T(8,128)(2,1)}, bf16[320,2560]{1,0:T(8,128)(2,1)S(1)}, u32[]{:S(2)}, u32[]{:S(2)}) %collective-permute-start.1) | collective-permute-done | bytes 1638432 | tf_op jit(solution)/shard_map/ppermute | solution.py:304
  22.9 2.0 %collective-permute-start.11 = (bf16[160,2560]{1,0:T(8,128)(2,1)S(1)}, bf16[160,2560]{1,0:T(8,128)(2,1)S(1)}, u32[]{:S(2)}, u32[]{:S(2)}) collective-permute-start(bf16[160,2560]{1,0:T(8,128)(2,1)S(1)} %slice.7), channel_id=1, source_target_pairs={{0,6},{1,25},{2,0},{3,27},{4,2},{5,29},{6,4},{7,31},{8,14},{9,1},{... | collective-permute-start | bytes 2457608 | tf_op jit(solution)/shard_map/ppermute | solution.py:304
  25.1 3.8 %collective-permute-start.2 = (bf16[344,128]{1,0:T(8,128)(2,1)S(1)}, bf16[344,128]{1,0:T(8,128)(2,1)S(1)}, u32[]{:S(2)}, u32[]{:S(2)}) collective-permute-start(bf16[344,128]{1,0:T(8,128)(2,1)S(1)} %get-tuple-element.40.total_ref), channel_id=1, source_target_pairs={{0,32},{32,64},{64,96},{96,128},{128,160},{160,192},{192,224},{1,3... | collective-permute-start | bytes 264200 | tf_op jit(solution)/shard_map/ppermute | solution.py:350
  28.9 2.1 %collective-permute-done.2.before_ref = bf16[344,128]{1,0:T(8,128)(2,1)S(1)} collective-permute-done((bf16[344,128]{1,0:T(8,128)(2,1)S(1)}, bf16[344,128]{1,0:T(8,128)(2,1)S(1)}, u32[]{:S(2)}, u32[]{:S(2)}) %collective-permute-start.2) | collective-permute-done | bytes 88096 | tf_op jit(solution)/shard_map/ppermute | solution.py:350
  31.1 4.3 %collective-permute-start.3 = (bf16[344,128]{1,0:T(8,128)(2,1)S(1)}, bf16[344,128]{1,0:T(8,128)(2,1)S(1)}, u32[]{:S(2)}, u32[]{:S(2)}) collective-permute-start(bf16[344,128]{1,0:T(8,128)(2,1)S(1)} %pair.1), channel_id=1, source_target_pairs={{0,32},{32,64},{64,96},{96,128},{128,160},{160,192},{192,224},{1,3... | collective-permute-start | bytes 264200 | tf_op jit(solution)/shard_map/ppermute | solution.py:350
  35.4 9.0 %collective-permute-start.4 = (bf16[344,128]{1,0:T(8,128)(2,1)S(1)}, bf16[344,128]{1,0:T(8,128)(2,1)S(1)}, u32[]{:S(2)}, u32[]{:S(2)}) collective-permute-start(bf16[344,128]{1,0:T(8,128)(2,1)S(1)} %pair.1), channel_id=1, source_target_pairs={{0,96},{32,128},{64,160},{96,192},{128,224},{1,97},{33,129},{65,16... | collective-permute-start | bytes 264200 | tf_op jit(solution)/shard_map/ppermute | solution.py:350
  44.4 1.3 %collective-permute-start.5 = (bf16[344,128]{1,0:T(8,128)(2,1)S(1)}, bf16[344,128]{1,0:T(8,128)(2,1)S(1)}, u32[]{:S(2)}, u32[]{:S(2)}) collective-permute-start(bf16[344,128]{1,0:T(8,128)(2,1)S(1)} %pair.1), channel_id=1, source_target_pairs={{0,160},{32,192},{64,224},{1,161},{33,193},{65,225},{2,162},{34,19... | collective-permute-start | bytes 264200 | tf_op jit(solution)/shard_map/ppermute | solution.py:350
  45.7 1.3 %collective-permute-start.6 = (bf16[344,128]{1,0:T(8,128)(2,1)S(1)}, bf16[344,128]{1,0:T(8,128)(2,1)S(1)}, u32[]{:S(2)}, u32[]{:S(2)}) collective-permute-start(bf16[344,128]{1,0:T(8,128)(2,1)S(1)} %pair.1), channel_id=1, source_target_pairs={{0,224},{1,225},{2,226},{3,227},{4,228},{5,229},{6,230},{7,231},{8... | collective-permute-start | bytes 264200 | tf_op jit(solution)/shard_map/ppermute | solution.py:350
  47.0 2.8 %collective-permute-done.5.refs_2_ = bf16[344,128]{1,0:T(8,128)(2,1)S(1)} collective-permute-done((bf16[344,128]{1,0:T(8,128)(2,1)S(1)}, bf16[344,128]{1,0:T(8,128)(2,1)S(1)}, u32[]{:S(2)}, u32[]{:S(2)}) %collective-permute-start.5) | collective-permute-done | bytes 88096 | tf_op jit(solution)/shard_map/ppermute | solution.py:350
  49.8 0.9 %collective-permute-done.6.refs_3_ = bf16[344,128]{1,0:T(8,128)(2,1)S(1)} collective-permute-done((bf16[344,128]{1,0:T(8,128)(2,1)S(1)}, bf16[344,128]{1,0:T(8,128)(2,1)S(1)}, u32[]{:S(2)}, u32[]{:S(2)}) %collective-permute-start.6) | collective-permute-done | bytes 88096 | tf_op jit(solution)/shard_map/ppermute | solution.py:350
  50.8 1.3 %gate.1 = (bf16[320,512]{1,0:T(8,128)(2,1)S(1)}, bf16[320,512]{1,0:T(8,128)(2,1)S(1)}, bf16[320,512]{1,0:T(8,128)(2,1)S(1)}, bf16[320,512]{1,0:T(8,128)(2,1)S(1)}) custom-call(f32[320,2048]{1,0:T(8,128)S(1)} %within.1.out_ref, bf16[320,2048]{1,0:T(8,128)(2,1)S(1)} %bitcast.3, bf16[2048,128]{1,0:T(8,128)(2,1)S(1)} %get-tuple-element.34.c_ref, ...), custom_call_target="tpu_custom_call" | custom-call | tf_op jit(solution)/shard_map/gate/pallas_call | solution.py:377
  52.1 1.6 %collective-permute-start.7 = (bf16[320,512]{1,0:T(8,128)(2,1)S(1)}, bf16[320,512]{1,0:T(8,128)(2,1)S(1)}, u32[]{:S(2)}, u32[]{:S(2)}) collective-permute-start(bf16[320,512]{1,0:T(8,128)(2,1)S(1)} %get-tuple-element.42), channel_id=1, source_target_pairs={{0,2},{1,9},{2,4},{3,11},{4,6},{5,13},{6,0},{7,15},{8,10},{9,17},{... | collective-permute-start | bytes 983048 | tf_op jit(solution)/shard_map/ppermute | solution.py:304
  53.7 1.6 %collective-permute-start.8 = (bf16[320,512]{1,0:T(8,128)(2,1)S(1)}, bf16[320,512]{1,0:T(8,128)(2,1)S(1)}, u32[]{:S(2)}, u32[]{:S(2)}) collective-permute-start(bf16[320,512]{1,0:T(8,128)(2,1)S(1)} %get-tuple-element.46), channel_id=1, source_target_pairs={{0,4},{1,17},{2,6},{3,19},{4,0},{5,21},{6,2},{7,23},{8,12},{9,25},... | collective-permute-start | bytes 983048 | tf_op jit(solution)/shard_map/ppermute | solution.py:304
  55.3 2.2 %collective-permute-start.9 = (bf16[320,512]{1,0:T(8,128)(2,1)S(1)}, bf16[320,512]{1,0:T(8,128)(2,1)S(1)}, u32[]{:S(2)}, u32[]{:S(2)}) collective-permute-start(bf16[320,512]{1,0:T(8,128)(2,1)S(1)} %get-tuple-element.47), channel_id=1, source_target_pairs={{0,6},{1,25},{2,0},{3,27},{4,2},{5,29},{6,4},{7,31},{8,14},{9,1},{... | collective-permute-start | bytes 983048 | tf_op jit(solution)/shard_map/ppermute | solution.py:304
  57.5 1.7 %collective-permute-done.7.refs_1_ = bf16[320,512]{1,0:T(8,128)(2,1)S(1)} collective-permute-done((bf16[320,512]{1,0:T(8,128)(2,1)S(1)}, bf16[320,512]{1,0:T(8,128)(2,1)S(1)}, u32[]{:S(2)}, u32[]{:S(2)}) %collective-permute-start.7) | collective-permute-done | bytes 327712 | tf_op jit(solution)/shard_map/ppermute | solution.py:304
  59.2 2.3 %begin.1 = (f32[512,2560]{1,0:T(8,128)S(1)}, f32[8,512]{1,0:T(8,128)S(1)}) custom-call(f32[40,128]{1,0:T(8,128)S(1)} %bitcast.4, bf16[320,512]{1,0:T(8,128)(2,1)S(1)} %get-tuple-element.41.refs_0_, bf16[320,512]{1,0:T(8,128)(2,1)S(1)} %collective-permute-done.7.refs_1_, bf16[320,2560]{1,0:T(8,128)(2,1)S(1)} %copy-done, ...), custom_call_target="tpu_custom_call" | custom-call | tf_op jit(solution)/shard_map/begin/pallas_call | solution.py:392
  61.6 0.8 collective-permute-done.8.refs_0_
  62.3 3.4 %collective-permute-done.9.refs_1_ = bf16[320,512]{1,0:T(8,128)(2,1)S(1)} collective-permute-done((bf16[320,512]{1,0:T(8,128)(2,1)S(1)}, bf16[320,512]{1,0:T(8,128)(2,1)S(1)}, u32[]{:S(2)}, u32[]{:S(2)}) %collective-permute-start.9) | collective-permute-done | bytes 327712 | tf_op jit(solution)/shard_map/ppermute | solution.py:304
  65.8 0.9 opposite.1
  67.3 2.6 %collective-permute-start.13 = (bf16[128,1280]{1,0:T(8,128)(2,1)S(1)}, bf16[128,1280]{1,0:T(8,128)(2,1)S(1)}, u32[]{:S(2)}, u32[]{:S(2)}) collective-permute-start(bf16[128,1280]{1,0:T(8,128)(2,1)S(1)} %get-tuple-element.54), channel_id=1, source_target_pairs={{0,24},{1,7},{2,26},{3,1},{4,28},{5,3},{6,30},{7,5},{8,0},{9,15},{... | collective-permute-start | bytes 983048 | tf_op jit(solution)/shard_map/ppermute | solution.py:304
  69.9 1.8 %project.1 = (bf16[136,1280]{1,0:T(8,128)(2,1)S(1)}, bf16[128,1280]{1,0:T(8,128)(2,1)S(1)}, bf16[136,1280]{1,0:T(8,128)(2,1)S(1)}, bf16[128,1280]{1,0:T(8,128)(2...) custom-call(f32[40,128]{1,0:T(8,128)S(1)} %bitcast.6, f32[512,2560]{1,0:T(8,128)S(1)} %get-tuple-element.44.begun_ref, ...), custom_call_target="tpu_custom_call" | custom-call | tf_op jit(solution)/shard_map/project/pallas_call | solution.py:413
  71.8 1.8 %collective-permute-start.16 = (bf16[136,1280]{1,0:T(8,128)(2,1)S(1)}, bf16[136,1280]{1,0:T(8,128)(2,1)S(1)}, u32[]{:S(2)}, u32[]{:S(2)}) collective-permute-start(bf16[136,1280]{1,0:T(8,128)(2,1)S(1)} %get-tuple-element.57), channel_id=1, source_target_pairs={{0,24},{1,7},{2,26},{3,1},{4,28},{5,3},{6,30},{7,5},{8,0},{9,15},{... | collective-permute-start | bytes 1044488 | tf_op jit(solution)/shard_map/ppermute | solution.py:304
  73.6 1.0 %collective-permute-done.13.got_second = bf16[128,1280]{1,0:T(8,128)(2,1)S(1)} collective-permute-done((bf16[128,1280]{1,0:T(8,128)(2,1)S(1)}, bf16[128,1280]{1,0:T(8,128)(2,1)S(1)}, u32[]{:S(2)}, u32[]{:S(2)}) %collective-permute-start.13) | collective-permute-done | bytes 327712 | tf_op jit(solution)/shard_map/ppermute | solution.py:304
  75.4 1.0 %collective-permute-start.14 = (bf16[136,1280]{1,0:T(8,128)(2,1)S(1)}, bf16[136,1280]{1,0:T(8,128)(2,1)S(1)}, u32[]{:S(2)}, u32[]{:S(2)}) collective-permute-start(bf16[136,1280]{1,0:T(8,128)(2,1)S(1)} %get-tuple-element.55), channel_id=1, source_target_pairs={{0,8},{1,3},{2,10},{3,5},{4,12},{5,7},{6,14},{7,1},{8,16},{9,11},{... | collective-permute-start | bytes 1044488 | tf_op jit(solution)/shard_map/ppermute | solution.py:304
  76.3 2.0 %collective-permute-start.15 = (bf16[128,1280]{1,0:T(8,128)(2,1)S(1)}, bf16[128,1280]{1,0:T(8,128)(2,1)S(1)}, u32[]{:S(2)}, u32[]{:S(2)}) collective-permute-start(bf16[128,1280]{1,0:T(8,128)(2,1)S(1)} %get-tuple-element.56), channel_id=1, source_target_pairs={{0,8},{1,3},{2,10},{3,5},{4,12},{5,7},{6,14},{7,1},{8,16},{9,11},{... | collective-permute-start | bytes 983048 | tf_op jit(solution)/shard_map/ppermute | solution.py:304
  78.4 1.2 %collective-permute-start.17 = (bf16[128,1280]{1,0:T(8,128)(2,1)S(1)}, bf16[128,1280]{1,0:T(8,128)(2,1)S(1)}, u32[]{:S(2)}, u32[]{:S(2)}) collective-permute-start(bf16[128,1280]{1,0:T(8,128)(2,1)S(1)} %get-tuple-element.58), channel_id=1, source_target_pairs={{0,24},{1,7},{2,26},{3,1},{4,28},{5,3},{6,30},{7,5},{8,0},{9,15},{... | collective-permute-start | bytes 983048 | tf_op jit(solution)/shard_map/ppermute | solution.py:304
  79.6 7.9 %collective-permute-done.15.refs_3_ = bf16[128,1280]{1,0:T(8,128)(2,1)S(1)} collective-permute-done((bf16[128,1280]{1,0:T(8,128)(2,1)S(1)}, bf16[128,1280]{1,0:T(8,128)(2,1)S(1)}, u32[]{:S(2)}, u32[]{:S(2)}) %collective-permute-start.15) | collective-permute-done | bytes 327712 | tf_op jit(solution)/shard_map/ppermute | solution.py:304
  87.5 1.2 %finish.1 = bf16[128,2560]{1,0:T(8,128)(2,1)} custom-call(f32[128,2560]{1,0:T(8,128)S(1)} %get-tuple-element.49.refs_0_, f32[8,128]{1,0:T(8,128)S(1)} %get-tuple-element.50.refs_1_, bf16[136,1280]{1,0:T(8,128)(2,1)S(1)} %collective-permute-done.14.refs_2_, bf16[128,1280]{1,0:T(8,128)(2,1)S(1)} %collective-permute-done.15.refs_3_, ...), custom_call_target="tpu_custom_call" | custom-call | tf_op jit(solution)/shard_map/finish/pallas_call | solution.py:435
  (23 shorter events, 2.7 us)
Async XLA Ops:
  0.0 21.5 %collective-permute-start = (bf16[320,2560]{1,0:T(8,128)(2,1)}, bf16[320,2560]{1,0:T(8,128)(2,1)S(1)}, u32[]{:S(2)}, u32[]{:S(2)}) collective-permute-start(bf16[320,2560]{1,0:T(8,128)(2,1)} %refs_2_.1), channel_id=1, source_target_pairs={{0,2},{1,9},{2,4},{3,11},{4,6},{5,13},{6,0},{7,15},{8,10},{9,17},{... | collective-permute-start | bytes 4915208 | tf_op jit(solution)/shard_map/ppermute | solution.py:304
  1.5 21.3 %collective-permute-start.1 = (bf16[320,2560]{1,0:T(8,128)(2,1)}, bf16[320,2560]{1,0:T(8,128)(2,1)S(1)}, u32[]{:S(2)}, u32[]{:S(2)}) collective-permute-start(bf16[320,2560]{1,0:T(8,128)(2,1)} %refs_2_.1), channel_id=1, source_target_pairs={{0,6},{1,25},{2,0},{3,27},{4,2},{5,29},{6,4},{7,31},{8,14},{9,1},{... | collective-permute-start | bytes 4915208 | tf_op jit(solution)/shard_map/ppermute | solution.py:304
  2.2 2.2 %copy-start.3 = (f32[5]{0:T(128)S(1)}, f32[5]{0:T(128)}, u32[]{:S(2)}) copy-start(f32[5]{0:T(128)} %skip_ref.1) | copy-start | bytes 64
  8.7 42.0 %copy-start.1 = (bf16[2048,320]{0,1:T(8,128)(2,1)S(1)}, bf16[2048,320]{0,1:T(8,128)(2,1)}, u32[]{:S(2)}) copy-start(bf16[2048,320]{0,1:T(8,128)(2,1)} %param.10) | copy-start | bytes 3932164
  22.9 42.9 %collective-permute-start.11 = (bf16[160,2560]{1,0:T(8,128)(2,1)S(1)}, bf16[160,2560]{1,0:T(8,128)(2,1)S(1)}, u32[]{:S(2)}, u32[]{:S(2)}) collective-permute-start(bf16[160,2560]{1,0:T(8,128)(2,1)S(1)} %slice.7), channel_id=1, source_target_pairs={{0,6},{1,25},{2,0},{3,27},{4,2},{5,29},{6,4},{7,31},{8,14},{9,1},{... | collective-permute-start | bytes 2457608 | tf_op jit(solution)/shard_map/ppermute | solution.py:304
  25.0 40.8 %collective-permute-start.10 = (bf16[160,2560]{1,0:T(8,128)(2,1)S(1)}, bf16[160,2560]{1,0:T(8,128)(2,1)S(1)}, u32[]{:S(2)}, u32[]{:S(2)}) collective-permute-start(bf16[160,2560]{1,0:T(8,128)(2,1)S(1)} %slice.6), channel_id=1, source_target_pairs={{0,2},{1,9},{2,4},{3,11},{4,6},{5,13},{6,0},{7,15},{8,10},{9,17},{... | collective-permute-start | bytes 2457608 | tf_op jit(solution)/shard_map/ppermute | solution.py:304
  25.1 5.9 %collective-permute-start.2 = (bf16[344,128]{1,0:T(8,128)(2,1)S(1)}, bf16[344,128]{1,0:T(8,128)(2,1)S(1)}, u32[]{:S(2)}, u32[]{:S(2)}) collective-permute-start(bf16[344,128]{1,0:T(8,128)(2,1)S(1)} %get-tuple-element.40.total_ref), channel_id=1, source_target_pairs={{0,32},{32,64},{64,96},{96,128},{128,160},{160,192},{192,224},{1,3... | collective-permute-start | bytes 264200 | tf_op jit(solution)/shard_map/ppermute | solution.py:350
  31.1 14.6 %collective-permute-start.3 = (bf16[344,128]{1,0:T(8,128)(2,1)S(1)}, bf16[344,128]{1,0:T(8,128)(2,1)S(1)}, u32[]{:S(2)}, u32[]{:S(2)}) collective-permute-start(bf16[344,128]{1,0:T(8,128)(2,1)S(1)} %pair.1), channel_id=1, source_target_pairs={{0,32},{32,64},{64,96},{96,128},{128,160},{160,192},{192,224},{1,3... | collective-permute-start | bytes 264200 | tf_op jit(solution)/shard_map/ppermute | solution.py:350
  35.4 11.6 %collective-permute-start.4 = (bf16[344,128]{1,0:T(8,128)(2,1)S(1)}, bf16[344,128]{1,0:T(8,128)(2,1)S(1)}, u32[]{:S(2)}, u32[]{:S(2)}) collective-permute-start(bf16[344,128]{1,0:T(8,128)(2,1)S(1)} %pair.1), channel_id=1, source_target_pairs={{0,96},{32,128},{64,160},{96,192},{128,224},{1,97},{33,129},{65,16... | collective-permute-start | bytes 264200 | tf_op jit(solution)/shard_map/ppermute | solution.py:350
  44.4 5.4 %collective-permute-start.5 = (bf16[344,128]{1,0:T(8,128)(2,1)S(1)}, bf16[344,128]{1,0:T(8,128)(2,1)S(1)}, u32[]{:S(2)}, u32[]{:S(2)}) collective-permute-start(bf16[344,128]{1,0:T(8,128)(2,1)S(1)} %pair.1), channel_id=1, source_target_pairs={{0,160},{32,192},{64,224},{1,161},{33,193},{65,225},{2,162},{34,19... | collective-permute-start | bytes 264200 | tf_op jit(solution)/shard_map/ppermute | solution.py:350
  45.7 5.1 %collective-permute-start.6 = (bf16[344,128]{1,0:T(8,128)(2,1)S(1)}, bf16[344,128]{1,0:T(8,128)(2,1)S(1)}, u32[]{:S(2)}, u32[]{:S(2)}) collective-permute-start(bf16[344,128]{1,0:T(8,128)(2,1)S(1)} %pair.1), channel_id=1, source_target_pairs={{0,224},{1,225},{2,226},{3,227},{4,228},{5,229},{6,230},{7,231},{8... | collective-permute-start | bytes 264200 | tf_op jit(solution)/shard_map/ppermute | solution.py:350
  50.8 8.5 %copy-start = (bf16[320,2560]{1,0:T(8,128)(2,1)S(1)}, bf16[320,2560]{1,0:T(8,128)(2,1)}, u32[]{:S(2)}) copy-start(bf16[320,2560]{1,0:T(8,128)(2,1)} %refs_2_.1) | copy-start | bytes 4915204
  50.8 8.5 %copy-start.2 = (f32[5120]{0:T(1024)S(1)}, f32[5120]{0:T(1024)}, u32[]{:S(2)}) copy-start(f32[5120]{0:T(1024)} %param.16) | copy-start | bytes 61444
  52.1 7.2 %collective-permute-start.7 = (bf16[320,512]{1,0:T(8,128)(2,1)S(1)}, bf16[320,512]{1,0:T(8,128)(2,1)S(1)}, u32[]{:S(2)}, u32[]{:S(2)}) collective-permute-start(bf16[320,512]{1,0:T(8,128)(2,1)S(1)} %get-tuple-element.42), channel_id=1, source_target_pairs={{0,2},{1,9},{2,4},{3,11},{4,6},{5,13},{6,0},{7,15},{8,10},{9,17},{... | collective-permute-start | bytes 983048 | tf_op jit(solution)/shard_map/ppermute | solution.py:304
  53.7 8.7 %collective-permute-start.8 = (bf16[320,512]{1,0:T(8,128)(2,1)S(1)}, bf16[320,512]{1,0:T(8,128)(2,1)S(1)}, u32[]{:S(2)}, u32[]{:S(2)}) collective-permute-start(bf16[320,512]{1,0:T(8,128)(2,1)S(1)} %get-tuple-element.46), channel_id=1, source_target_pairs={{0,4},{1,17},{2,6},{3,19},{4,0},{5,21},{6,2},{7,23},{8,12},{9,25},... | collective-permute-start | bytes 983048 | tf_op jit(solution)/shard_map/ppermute | solution.py:304
  55.3 10.4 %collective-permute-start.9 = (bf16[320,512]{1,0:T(8,128)(2,1)S(1)}, bf16[320,512]{1,0:T(8,128)(2,1)S(1)}, u32[]{:S(2)}, u32[]{:S(2)}) collective-permute-start(bf16[320,512]{1,0:T(8,128)(2,1)S(1)} %get-tuple-element.47), channel_id=1, source_target_pairs={{0,6},{1,25},{2,0},{3,27},{4,2},{5,29},{6,4},{7,31},{8,14},{9,1},{... | collective-permute-start | bytes 983048 | tf_op jit(solution)/shard_map/ppermute | solution.py:304
  66.6 8.6 %collective-permute-start.12 = (bf16[136,1280]{1,0:T(8,128)(2,1)S(1)}, bf16[136,1280]{1,0:T(8,128)(2,1)S(1)}, u32[]{:S(2)}, u32[]{:S(2)}) collective-permute-start(bf16[136,1280]{1,0:T(8,128)(2,1)S(1)} %get-tuple-element.53), channel_id=1, source_target_pairs={{0,8},{1,3},{2,10},{3,5},{4,12},{5,7},{6,14},{7,1},{8,16},{9,11},{... | collective-permute-start | bytes 1044488 | tf_op jit(solution)/shard_map/ppermute | solution.py:304
  67.3 7.2 %collective-permute-start.13 = (bf16[128,1280]{1,0:T(8,128)(2,1)S(1)}, bf16[128,1280]{1,0:T(8,128)(2,1)S(1)}, u32[]{:S(2)}, u32[]{:S(2)}) collective-permute-start(bf16[128,1280]{1,0:T(8,128)(2,1)S(1)} %get-tuple-element.54), channel_id=1, source_target_pairs={{0,24},{1,7},{2,26},{3,1},{4,28},{5,3},{6,30},{7,5},{8,0},{9,15},{... | collective-permute-start | bytes 983048 | tf_op jit(solution)/shard_map/ppermute | solution.py:304
  71.8 15.7 %collective-permute-start.16 = (bf16[136,1280]{1,0:T(8,128)(2,1)S(1)}, bf16[136,1280]{1,0:T(8,128)(2,1)S(1)}, u32[]{:S(2)}, u32[]{:S(2)}) collective-permute-start(bf16[136,1280]{1,0:T(8,128)(2,1)S(1)} %get-tuple-element.57), channel_id=1, source_target_pairs={{0,24},{1,7},{2,26},{3,1},{4,28},{5,3},{6,30},{7,5},{8,0},{9,15},{... | collective-permute-start | bytes 1044488 | tf_op jit(solution)/shard_map/ppermute | solution.py:304
  75.4 12.1 %collective-permute-start.14 = (bf16[136,1280]{1,0:T(8,128)(2,1)S(1)}, bf16[136,1280]{1,0:T(8,128)(2,1)S(1)}, u32[]{:S(2)}, u32[]{:S(2)}) collective-permute-start(bf16[136,1280]{1,0:T(8,128)(2,1)S(1)} %get-tuple-element.55), channel_id=1, source_target_pairs={{0,8},{1,3},{2,10},{3,5},{4,12},{5,7},{6,14},{7,1},{8,16},{9,11},{... | collective-permute-start | bytes 1044488 | tf_op jit(solution)/shard_map/ppermute | solution.py:304
  76.3 11.1 %collective-permute-start.15 = (bf16[128,1280]{1,0:T(8,128)(2,1)S(1)}, bf16[128,1280]{1,0:T(8,128)(2,1)S(1)}, u32[]{:S(2)}, u32[]{:S(2)}) collective-permute-start(bf16[128,1280]{1,0:T(8,128)(2,1)S(1)} %get-tuple-element.56), channel_id=1, source_target_pairs={{0,8},{1,3},{2,10},{3,5},{4,12},{5,7},{6,14},{7,1},{8,16},{9,11},{... | collective-permute-start | bytes 983048 | tf_op jit(solution)/shard_map/ppermute | solution.py:304
  78.4 9.1 %collective-permute-start.17 = (bf16[128,1280]{1,0:T(8,128)(2,1)S(1)}, bf16[128,1280]{1,0:T(8,128)(2,1)S(1)}, u32[]{:S(2)}, u32[]{:S(2)}) collective-permute-start(bf16[128,1280]{1,0:T(8,128)(2,1)S(1)} %get-tuple-element.58), channel_id=1, source_target_pairs={{0,24},{1,7},{2,26},{3,1},{4,28},{5,3},{6,30},{7,5},{8,0},{9,15},{... | collective-permute-start | bytes 983048 | tf_op jit(solution)/shard_map/ppermute | solution.py:304

commit v5 on v4

--- a/solution.py
+++ b/solution.py
@@ -216,7 +216,7 @@
 def begin_kernel(gain_ref, *refs):
     rows, weights = refs[:2], refs[2:-3]
     product_ref, squares_ref, left = refs[-3:]
-    left[...], squares = left_side(gain_ref, rows, (0, 1), range(RING))
+    left[...], squares = left_side(gain_ref, rows, (0, 2), range(RING))
     squares_ref[...] = jnp.broadcast_to(squares, squares_ref.shape)
     tile = 256
     for n in range(product_ref.shape[1] // tile):
@@ -230,7 +230,7 @@
     first_ref, second_ref, left = refs[-3:]
     half = first_ref.shape[1]
     block = slice(2 * SUB, 3 * SUB)
-    left[...], squares = left_side(gain_ref, rows, (2, 3), (2,))
+    left[...], squares = left_side(gain_ref, rows, (1, 3), (2,))
     first_ref[SUB:, :] = tail_rows(squares + begun_squares[0:1, block], half)
     tile = 256
     for n in range(2 * half // tile):
@@ -248,7 +248,7 @@
     next_first, next_second, last_first, last_second, own_ref, own_squares, left = refs[-7:]
     half = next_first.shape[1]
     own, following, previous = slice(0, SUB), slice(SUB, 2 * SUB), slice(3 * SUB, 4 * SUB)
-    left[...], squares = left_side(gain_ref, rows, (2, 3), (1, 3, 0))
+    left[...], squares = left_side(gain_ref, rows, (1, 3), (1, 3, 0))
     next_first[SUB:, :] = tail_rows(squares[:, 0:SUB] + begun_squares[0:1, following], half)
     last_first[SUB:, :] = tail_rows(squares[:, SUB : 2 * SUB] + begun_squares[0:1, previous], half)
     own_squares[...] = jnp.broadcast_to(squares[:, 2 * SUB :] + begun_squares[0:1, own], own_squares.shape)
@@ -350,6 +350,15 @@
         return lax.ppermute(value, "seq", [(k, k + shift) for k in range(seq_count - shift)])
 
     before = along(total, 1)
+    local = pl.pallas_call(
+        within_kernel,
+        in_specs=[pl.BlockSpec(memory_space=pltpu.SMEM)] + [near] * 6,
+        out_specs=near,
+        out_shape=pltpu.VMEM((channels, tokens), f32),
+        compiler_params=params,
+        name="within",
+    )(skip_gain, *hold(x_own, b_own, c_own, cum, step_own, prefix))
+    before, local = lax.optimization_barrier((before, local))
     pair = pl.pallas_call(
         pair_kernel,
         in_specs=[near] * 2,
@@ -360,15 +369,7 @@
     )(*hold(total, before))
     totals = [along(pair, shift) for shift in range(1, seq_count, 2)]
 
-    local = pl.pallas_call(
-        within_kernel,
-        in_specs=[pl.BlockSpec(memory_space=pltpu.SMEM)] + [near] * 6,
-        out_specs=near,
-        out_shape=pltpu.VMEM((channels, tokens), f32),
-        compiler_params=params,
-        name="within",
-    )(skip_gain, *hold(x_own, b_own, c_own, cum, step_own, prefix))
-    local, weight_before, weight_after = lax.optimization_barrier((local, weight_before, weight_after))
+    weight_before, weight_after, pair = lax.optimization_barrier((weight_before, weight_after, pair))
     middle = channels // 2
     upper, lower = weight_before[:middle], weight_after[middle:]
     upper, lower = ring(upper, 1, True), ring(lower, following, True)
@@ -383,22 +384,22 @@
         name="gate",
     )(*hold(local, gate_columns, c_own, factor, *totals))
 
-    rows_before = ring(gated[1], 1, True)
-    rows_later = [ring(gated[s], s, True) for s in range(2, RING)]
+    rows_opposite = ring(gated[2], 2, True)
+    rows_near = [ring(gated[s], s, True) for s in (1, following)]
 
     half = width // 2
     with_tail, without = pltpu.VMEM((SUB + EXTRA, half), bf16), pltpu.VMEM((SUB, half), bf16)
     gain_lines = norm_gain.reshape(-1, SUB)
     begun, begun_squares = pl.pallas_call(
         begin_kernel,
-        in_specs=[near] * 5,
+        in_specs=[near] * 6,
         out_specs=[near] * 2,
         scratch_shapes=[pltpu.VMEM((quarter, 2 * channels), bf16)],
         out_shape=[pltpu.VMEM((quarter, width), f32), pltpu.VMEM((PAD, quarter), f32)],
         compiler_params=params,
         name="begin",
-    )(*hold(gain_lines, gated[0], rows_before, out_weight, weight_before))
-    operands = hold(gain_lines, begun, begun_squares, *rows_later, upper, lower, weight_after)
+    )(*hold(gain_lines, gated[0], rows_opposite, out_weight, upper, lower))
+    operands = hold(gain_lines, begun, begun_squares, *rows_near, weight_before, weight_after)
     opposite_first, opposite_second = pl.pallas_call(
         opposite_kernel,
         in_specs=[near] * len(operands),

time: 88.8 us -> 81.4 us (0.917)
  starting transfers between devices: 38.8 us -> 33.6 us
  waiting for transfers between devices: 35.4 us -> 33.3 us
    ppermute x13, starting transfers between devices: 19.2 us -> 15.8 us  [ring(): return lax.ppermute(value, ('head', 'batch'), ring_pairs(shift, gather))]
    ppermute x5, starting transfers between devices: 19.7 us -> 17.8 us  [along(): lax.ppermute(value, 'seq', [(k, k + shift) for k in range(seq_count - shi...]
    ppermute x13, waiting for transfers between devices: 29.5 us -> 27.8 us  [ring(): return lax.ppermute(value, ('head', 'batch'), ring_pairs(shift, gather))]
  transfers between devices with their start and end apart: 18 -> 18, of which waited for: 11 -> 9; matrix products, arithmetic and copies ran while one was open for 0% -> 0% of each run, Pallas kernels for 14% -> 15%
where the time goes in v5:
time: 81.4 us; the launch traced here: 81.2 us
  starting transfers between devices  33.6 us (41%)
  waiting for transfers between devices  33.3 us (41%)
  Pallas kernels  14.1 us (17%)
    ppermute x13, waiting for transfers between devices, ring(): return lax.ppermute(value, ('head', 'batch'), ring_pairs(shift, gather))  27.8 us
    ppermute x5, starting transfers between devices, along(): lax.ppermute(value, 'seq', [(k, k + shift) for k in range(seq_count - shi...  17.8 us
    ppermute x13, starting transfers between devices, ring(): return lax.ppermute(value, ('head', 'batch'), ring_pairs(shift, gather))  15.8 us
    ppermute x5, waiting for transfers between devices, along(): lax.ppermute(value, 'seq', [(k, k + shift) for k in range(seq_count - shi...  5.48 us
    pallas_call x1, Pallas kernels, body(): pl.pallas_call(within_kernel, in_specs=[pl.BlockSpec(memory_space=pltpu.S...  4.26 us
    pallas_call x1, Pallas kernels, body(): pl.pallas_call(begin_kernel, in_specs=[near] * 6, out_specs=[near] * 2, s...  2.29 us
    pallas_call x1, Pallas kernels, body(): pl.pallas_call(state_kernel, in_specs=[pl.BlockSpec(memory_space=pltpu.HB...  2.17 us
    pallas_call x1, Pallas kernels, body(): pl.pallas_call(project_kernel, in_specs=[near] * len(operands), out_specs...  1.83 us
  transfers between devices with their start and end apart: 18, of which 9 were waited for; matrix products, arithmetic and copies ran while one was open for 0% of the time, Pallas kernels for 15%

profile of v5, /device:TPU:2, one launch (start us, length us, event | category | flops | bytes accessed | tf_op | source)
XLA Modules:
  0.0 81.2 jit_solution(2687061546053742203)
XLA Ops:
  0.0 1.5 %collective-permute-start.6 = (bf16[320,2560]{1,0:T(8,128)(2,1)}, bf16[320,2560]{1,0:T(8,128)(2,1)S(1)}, u32[]{:S(2)}, u32[]{:S(2)}) collective-permute-start(bf16[320,2560]{1,0:T(8,128)(2,1)} %refs_2_.1), channel_id=1, source_target_pairs={{0,2},{1,9},{2,4},{3,11},{4,6},{5,13},{6,0},{7,15},{8,10},{9,17},{... | collective-permute-start | bytes 4915208 | tf_op jit(solution)/shard_map/ppermute | solution.py:304
  1.5 0.8 collective-permute-start.7
  2.2 2.2 %state.1 = (bf16[8,320,128]{2,1,0:T(8,128)(2,1)S(1)}, bf16[344,128]{1,0:T(8,128)(2,1)S(1)}, f32[8,2048]{1,0:T(8,128)S(1)}, f32[8,2048]{1,0:T(8,128)S(1)}, bf16[3...) custom-call(bf16[320,2048]{1,0:T(8,128)(2,1)} %bitcast.7, ...), custom_call_target="tpu_custom_call" | custom-call | tf_op jit(solution)/shard_map/state/pallas_call | solution.py:330
  4.4 3.6 %collective-permute-start = (bf16[344,128]{1,0:T(8,128)(2,1)S(1)}, bf16[344,128]{1,0:T(8,128)(2,1)S(1)}, u32[]{:S(2)}, u32[]{:S(2)}) collective-permute-start(bf16[344,128]{1,0:T(8,128)(2,1)S(1)} %get-tuple-element.33.total_ref), channel_id=1, source_target_pairs={{0,32},{32,64},{64,96},{96,128},{128,160},{160,192},{192,224},{1,3... | collective-permute-start | bytes 264200 | tf_op jit(solution)/shard_map/ppermute | solution.py:350
  8.0 4.3 %within.1.out_ref = f32[320,2048]{1,0:T(8,128)S(1)} custom-call(f32[5]{0:T(128)S(1)} %copy-done.3, bf16[320,2048]{1,0:T(8,128)(2,1)S(1)} %get-tuple-element.34.x_ref, bf16[2048,128]{1,0:T(8,128)(2,1)S(1)} %get-tuple-element.35.b_ref, bf16[2048,128]{1,0:T(8,128)(2,1)S(1)} %get-tuple-element.36.c_ref, f32[8,2048]{1,0:T(8,128)S(1)} %get-tuple-element.37.cum_ref, ...), custom_call_target="tpu_custom_call" | custom-call | tf_op jit(solution)/shard_map/within/pallas_call | solution.py:353
  12.4 9.1 %collective-permute-done.6.refs_2_ = bf16[320,2560]{1,0:T(8,128)(2,1)S(1)} collective-permute-done((bf16[320,2560]{1,0:T(8,128)(2,1)}, bf16[320,2560]{1,0:T(8,128)(2,1)S(1)}, u32[]{:S(2)}, u32[]{:S(2)}) %collective-permute-start.6) | collective-permute-done | bytes 1638432 | tf_op jit(solution)/shard_map/ppermute | solution.py:304
  21.5 1.3 %collective-permute-done.7.refs_3_ = bf16[320,2560]{1,0:T(8,128)(2,1)S(1)} collective-permute-done((bf16[320,2560]{1,0:T(8,128)(2,1)}, bf16[320,2560]{1,0:T(8,128)(2,1)S(1)}, u32[]{:S(2)}, u32[]{:S(2)}) %collective-permute-start.7) | collective-permute-done | bytes 1638432 | tf_op jit(solution)/shard_map/ppermute | solution.py:304
  22.9 1.5 %collective-permute-start.8 = (bf16[160,2560]{1,0:T(8,128)(2,1)S(1)}, bf16[160,2560]{1,0:T(8,128)(2,1)S(1)}, u32[]{:S(2)}, u32[]{:S(2)}) collective-permute-start(bf16[160,2560]{1,0:T(8,128)(2,1)S(1)} %slice.6), channel_id=1, source_target_pairs={{0,2},{1,9},{2,4},{3,11},{4,6},{5,13},{6,0},{7,15},{8,10},{9,17},{... | collective-permute-start | bytes 2457608 | tf_op jit(solution)/shard_map/ppermute | solution.py:304
  24.4 0.7 collective-permute-start.9
  25.1 3.8 %collective-permute-start.1 = (bf16[344,128]{1,0:T(8,128)(2,1)S(1)}, bf16[344,128]{1,0:T(8,128)(2,1)S(1)}, u32[]{:S(2)}, u32[]{:S(2)}) collective-permute-start(bf16[344,128]{1,0:T(8,128)(2,1)S(1)} %pair.1), channel_id=1, source_target_pairs={{0,32},{32,64},{64,96},{96,128},{128,160},{160,192},{192,224},{1,3... | collective-permute-start | bytes 264200 | tf_op jit(solution)/shard_map/ppermute | solution.py:350
  28.9 7.7 %collective-permute-start.2 = (bf16[344,128]{1,0:T(8,128)(2,1)S(1)}, bf16[344,128]{1,0:T(8,128)(2,1)S(1)}, u32[]{:S(2)}, u32[]{:S(2)}) collective-permute-start(bf16[344,128]{1,0:T(8,128)(2,1)S(1)} %pair.1), channel_id=1, source_target_pairs={{0,96},{32,128},{64,160},{96,192},{128,224},{1,97},{33,129},{65,16... | collective-permute-start | bytes 264200 | tf_op jit(solution)/shard_map/ppermute | solution.py:350
  36.7 1.3 %collective-permute-start.3 = (bf16[344,128]{1,0:T(8,128)(2,1)S(1)}, bf16[344,128]{1,0:T(8,128)(2,1)S(1)}, u32[]{:S(2)}, u32[]{:S(2)}) collective-permute-start(bf16[344,128]{1,0:T(8,128)(2,1)S(1)} %pair.1), channel_id=1, source_target_pairs={{0,160},{32,192},{64,224},{1,161},{33,193},{65,225},{2,162},{34,19... | collective-permute-start | bytes 264200 | tf_op jit(solution)/shard_map/ppermute | solution.py:350
  38.0 1.3 %collective-permute-start.4 = (bf16[344,128]{1,0:T(8,128)(2,1)S(1)}, bf16[344,128]{1,0:T(8,128)(2,1)S(1)}, u32[]{:S(2)}, u32[]{:S(2)}) collective-permute-start(bf16[344,128]{1,0:T(8,128)(2,1)S(1)} %pair.1), channel_id=1, source_target_pairs={{0,224},{1,225},{2,226},{3,227},{4,228},{5,229},{6,230},{7,231},{8... | collective-permute-start | bytes 264200 | tf_op jit(solution)/shard_map/ppermute | solution.py:350
  39.3 4.1 %collective-permute-done.3.refs_2_ = bf16[344,128]{1,0:T(8,128)(2,1)S(1)} collective-permute-done((bf16[344,128]{1,0:T(8,128)(2,1)S(1)}, bf16[344,128]{1,0:T(8,128)(2,1)S(1)}, u32[]{:S(2)}, u32[]{:S(2)}) %collective-permute-start.3) | collective-permute-done | bytes 88096 | tf_op jit(solution)/shard_map/ppermute | solution.py:350
  43.5 1.3 %collective-permute-done.4.refs_3_ = bf16[344,128]{1,0:T(8,128)(2,1)S(1)} collective-permute-done((bf16[344,128]{1,0:T(8,128)(2,1)S(1)}, bf16[344,128]{1,0:T(8,128)(2,1)S(1)}, u32[]{:S(2)}, u32[]{:S(2)}) %collective-permute-start.4) | collective-permute-done | bytes 88096 | tf_op jit(solution)/shard_map/ppermute | solution.py:350
  44.8 1.3 %gate.1 = (bf16[320,512]{1,0:T(8,128)(2,1)S(1)}, bf16[320,512]{1,0:T(8,128)(2,1)S(1)}, bf16[320,512]{1,0:T(8,128)(2,1)S(1)}, bf16[320,512]{1,0:T(8,128)(2,1)S(1)}) custom-call(f32[320,2048]{1,0:T(8,128)S(1)} %within.1.out_ref, bf16[320,2048]{1,0:T(8,128)(2,1)S(1)} %bitcast.3, bf16[2048,128]{1,0:T(8,128)(2,1)S(1)} %get-tuple-element.36.c_ref, ...), custom_call_target="tpu_custom_call" | custom-call | tf_op jit(solution)/shard_map/gate/pallas_call | solution.py:378
  46.1 2.2 %collective-permute-start.5 = (bf16[320,512]{1,0:T(8,128)(2,1)S(1)}, bf16[320,512]{1,0:T(8,128)(2,1)S(1)}, u32[]{:S(2)}, u32[]{:S(2)}) collective-permute-start(bf16[320,512]{1,0:T(8,128)(2,1)S(1)} %get-tuple-element.44), channel_id=1, source_target_pairs={{0,4},{1,17},{2,6},{3,19},{4,0},{5,21},{6,2},{7,23},{8,12},{9,25},... | collective-permute-start | bytes 983048 | tf_op jit(solution)/shard_map/ppermute | solution.py:304
  48.3 2.0 %collective-permute-start.11 = (bf16[320,512]{1,0:T(8,128)(2,1)S(1)}, bf16[320,512]{1,0:T(8,128)(2,1)S(1)}, u32[]{:S(2)}, u32[]{:S(2)}) collective-permute-start(bf16[320,512]{1,0:T(8,128)(2,1)S(1)} %get-tuple-element.50), channel_id=1, source_target_pairs={{0,6},{1,25},{2,0},{3,27},{4,2},{5,29},{6,4},{7,31},{8,14},{9,1},{... | collective-permute-start | bytes 983048 | tf_op jit(solution)/shard_map/ppermute | solution.py:304
  50.3 4.5 %collective-permute-done.5.refs_1_ = bf16[320,512]{1,0:T(8,128)(2,1)S(1)} collective-permute-done((bf16[320,512]{1,0:T(8,128)(2,1)S(1)}, bf16[320,512]{1,0:T(8,128)(2,1)S(1)}, u32[]{:S(2)}, u32[]{:S(2)}) %collective-permute-start.5) | collective-permute-done | bytes 327712 | tf_op jit(solution)/shard_map/ppermute | solution.py:304
  54.9 2.3 %begin.1 = (f32[512,2560]{1,0:T(8,128)S(1)}, f32[8,512]{1,0:T(8,128)S(1)}) custom-call(f32[40,128]{1,0:T(8,128)S(1)} %bitcast.4, bf16[320,512]{1,0:T(8,128)(2,1)S(1)} %get-tuple-element.43.refs_0_, bf16[320,512]{1,0:T(8,128)(2,1)S(1)} %collective-permute-done.5.refs_1_, bf16[320,2560]{1,0:T(8,128)(2,1)S(1)} %copy-done, ...), custom_call_target="tpu_custom_call" | custom-call | tf_op jit(solution)/shard_map/begin/pallas_call | solution.py:393
  57.2 1.2 %collective-permute-done.10.refs_0_ = bf16[320,512]{1,0:T(8,128)(2,1)S(1)} collective-permute-done((bf16[320,512]{1,0:T(8,128)(2,1)S(1)}, bf16[320,512]{1,0:T(8,128)(2,1)S(1)}, u32[]{:S(2)}, u32[]{:S(2)}) %collective-permute-start.10) | collective-permute-done | bytes 327712 | tf_op jit(solution)/shard_map/ppermute | solution.py:304
  58.4 0.8 %opposite.1 = (bf16[136,1280]{1,0:T(8,128)(2,1)S(1)}, bf16[128,1280]{1,0:T(8,128)(2,1)S(1)}) custom-call(f32[40,128]{1,0:T(8,128)S(1)} %bitcast.5, f32[512,2560]{1,0:T(8,128)S(1)} %get-tuple-element.47.begun_ref, f32[8,512]{1,0:T(8,128)S(1)} %get-tuple-element.48.begun_squares, bf16[320,512]{1,0:T(8,128)(2,1)S(1)} %collective-permute-done.10.refs_0_, ...), custom_call_target="tpu_custom_call" | custom-call | tf_op jit(solution)/shard_map/opposite/pallas_call | solution.py:403
  59.2 0.4 collective-permute-start.12
  59.6 2.9 %collective-permute-start.13 = (bf16[128,1280]{1,0:T(8,128)(2,1)S(1)}, bf16[128,1280]{1,0:T(8,128)(2,1)S(1)}, u32[]{:S(2)}, u32[]{:S(2)}) collective-permute-start(bf16[128,1280]{1,0:T(8,128)(2,1)S(1)} %get-tuple-element.56), channel_id=1, source_target_pairs={{0,24},{1,7},{2,26},{3,1},{4,28},{5,3},{6,30},{7,5},{8,0},{9,15},{... | collective-permute-start | bytes 983048 | tf_op jit(solution)/shard_map/ppermute | solution.py:304
  62.5 1.8 %project.1 = (bf16[136,1280]{1,0:T(8,128)(2,1)S(1)}, bf16[128,1280]{1,0:T(8,128)(2,1)S(1)}, bf16[136,1280]{1,0:T(8,128)(2,1)S(1)}, bf16[128,1280]{1,0:T(8,128)(2...) custom-call(f32[40,128]{1,0:T(8,128)S(1)} %bitcast.6, f32[512,2560]{1,0:T(8,128)S(1)} %get-tuple-element.47.begun_ref, ...), custom_call_target="tpu_custom_call" | custom-call | tf_op jit(solution)/shard_map/project/pallas_call | solution.py:414
  64.7 2.5 %collective-permute-done.13.got_second = bf16[128,1280]{1,0:T(8,128)(2,1)S(1)} collective-permute-done((bf16[128,1280]{1,0:T(8,128)(2,1)S(1)}, bf16[128,1280]{1,0:T(8,128)(2,1)S(1)}, u32[]{:S(2)}, u32[]{:S(2)}) %collective-permute-start.13) | collective-permute-done | bytes 327712 | tf_op jit(solution)/shard_map/ppermute | solution.py:304
  67.1 0.7 collective-permute-done.12.got_first
  67.9 0.3 collective-permute-start.14
  68.2 1.2 %collective-permute-start.15 = (bf16[128,1280]{1,0:T(8,128)(2,1)S(1)}, bf16[128,1280]{1,0:T(8,128)(2,1)S(1)}, u32[]{:S(2)}, u32[]{:S(2)}) collective-permute-start(bf16[128,1280]{1,0:T(8,128)(2,1)S(1)} %get-tuple-element.58), channel_id=1, source_target_pairs={{0,8},{1,3},{2,10},{3,5},{4,12},{5,7},{6,14},{7,1},{8,16},{9,11},{... | collective-permute-start | bytes 983048 | tf_op jit(solution)/shard_map/ppermute | solution.py:304
  69.4 2.0 %collective-permute-start.17 = (bf16[128,1280]{1,0:T(8,128)(2,1)S(1)}, bf16[128,1280]{1,0:T(8,128)(2,1)S(1)}, u32[]{:S(2)}, u32[]{:S(2)}) collective-permute-start(bf16[128,1280]{1,0:T(8,128)(2,1)S(1)} %get-tuple-element.60), channel_id=1, source_target_pairs={{0,24},{1,7},{2,26},{3,1},{4,28},{5,3},{6,30},{7,5},{8,0},{9,15},{... | collective-permute-start | bytes 983048 | tf_op jit(solution)/shard_map/ppermute | solution.py:304
  71.5 8.6 %collective-permute-done.15.refs_3_ = bf16[128,1280]{1,0:T(8,128)(2,1)S(1)} collective-permute-done((bf16[128,1280]{1,0:T(8,128)(2,1)S(1)}, bf16[128,1280]{1,0:T(8,128)(2,1)S(1)}, u32[]{:S(2)}, u32[]{:S(2)}) %collective-permute-start.15) | collective-permute-done | bytes 327712 | tf_op jit(solution)/shard_map/ppermute | solution.py:304
  80.0 1.2 %finish.1 = bf16[128,2560]{1,0:T(8,128)(2,1)} custom-call(f32[128,2560]{1,0:T(8,128)S(1)} %get-tuple-element.51.refs_0_, f32[8,128]{1,0:T(8,128)S(1)} %get-tuple-element.52.refs_1_, bf16[136,1280]{1,0:T(8,128)(2,1)S(1)} %collective-permute-done.14.refs_2_, bf16[128,1280]{1,0:T(8,128)(2,1)S(1)} %collective-permute-done.15.refs_3_, ...), custom_call_target="tpu_custom_call" | custom-call | tf_op jit(solution)/shard_map/finish/pallas_call | solution.py:436
  (23 shorter events, 0.7 us)
Async XLA Ops:
  0.0 21.5 %collective-permute-start.6 = (bf16[320,2560]{1,0:T(8,128)(2,1)}, bf16[320,2560]{1,0:T(8,128)(2,1)S(1)}, u32[]{:S(2)}, u32[]{:S(2)}) collective-permute-start(bf16[320,2560]{1,0:T(8,128)(2,1)} %refs_2_.1), channel_id=1, source_target_pairs={{0,2},{1,9},{2,4},{3,11},{4,6},{5,13},{6,0},{7,15},{8,10},{9,17},{... | collective-permute-start | bytes 4915208 | tf_op jit(solution)/shard_map/ppermute | solution.py:304
  1.5 21.3 %collective-permute-start.7 = (bf16[320,2560]{1,0:T(8,128)(2,1)}, bf16[320,2560]{1,0:T(8,128)(2,1)S(1)}, u32[]{:S(2)}, u32[]{:S(2)}) collective-permute-start(bf16[320,2560]{1,0:T(8,128)(2,1)} %refs_2_.1), channel_id=1, source_target_pairs={{0,6},{1,25},{2,0},{3,27},{4,2},{5,29},{6,4},{7,31},{8,14},{9,1},{... | collective-permute-start | bytes 4915208 | tf_op jit(solution)/shard_map/ppermute | solution.py:304
  2.2 5.8 %copy-start.3 = (f32[5]{0:T(128)S(1)}, f32[5]{0:T(128)}, u32[]{:S(2)}) copy-start(f32[5]{0:T(128)} %skip_ref.1) | copy-start | bytes 64
  4.4 7.9 %collective-permute-start = (bf16[344,128]{1,0:T(8,128)(2,1)S(1)}, bf16[344,128]{1,0:T(8,128)(2,1)S(1)}, u32[]{:S(2)}, u32[]{:S(2)}) collective-permute-start(bf16[344,128]{1,0:T(8,128)(2,1)S(1)} %get-tuple-element.33.total_ref), channel_id=1, source_target_pairs={{0,32},{32,64},{64,96},{96,128},{128,160},{160,192},{192,224},{1,3... | collective-permute-start | bytes 264200 | tf_op jit(solution)/shard_map/ppermute | solution.py:350
  12.4 32.4 %copy-start.1 = (bf16[2048,320]{0,1:T(8,128)(2,1)S(1)}, bf16[2048,320]{0,1:T(8,128)(2,1)}, u32[]{:S(2)}) copy-start(bf16[2048,320]{0,1:T(8,128)(2,1)} %param.10) | copy-start | bytes 3932164
  22.9 32.0 %collective-permute-start.8 = (bf16[160,2560]{1,0:T(8,128)(2,1)S(1)}, bf16[160,2560]{1,0:T(8,128)(2,1)S(1)}, u32[]{:S(2)}, u32[]{:S(2)}) collective-permute-start(bf16[160,2560]{1,0:T(8,128)(2,1)S(1)} %slice.6), channel_id=1, source_target_pairs={{0,2},{1,9},{2,4},{3,11},{4,6},{5,13},{6,0},{7,15},{8,10},{9,17},{... | collective-permute-start | bytes 2457608 | tf_op jit(solution)/shard_map/ppermute | solution.py:304
  24.4 30.5 %collective-permute-start.9 = (bf16[160,2560]{1,0:T(8,128)(2,1)S(1)}, bf16[160,2560]{1,0:T(8,128)(2,1)S(1)}, u32[]{:S(2)}, u32[]{:S(2)}) collective-permute-start(bf16[160,2560]{1,0:T(8,128)(2,1)S(1)} %slice.7), channel_id=1, source_target_pairs={{0,6},{1,25},{2,0},{3,27},{4,2},{5,29},{6,4},{7,31},{8,14},{9,1},{... | collective-permute-start | bytes 2457608 | tf_op jit(solution)/shard_map/ppermute | solution.py:304
  25.1 12.9 %collective-permute-start.1 = (bf16[344,128]{1,0:T(8,128)(2,1)S(1)}, bf16[344,128]{1,0:T(8,128)(2,1)S(1)}, u32[]{:S(2)}, u32[]{:S(2)}) collective-permute-start(bf16[344,128]{1,0:T(8,128)(2,1)S(1)} %pair.1), channel_id=1, source_target_pairs={{0,32},{32,64},{64,96},{96,128},{128,160},{160,192},{192,224},{1,3... | collective-permute-start | bytes 264200 | tf_op jit(solution)/shard_map/ppermute | solution.py:350
  28.9 10.4 %collective-permute-start.2 = (bf16[344,128]{1,0:T(8,128)(2,1)S(1)}, bf16[344,128]{1,0:T(8,128)(2,1)S(1)}, u32[]{:S(2)}, u32[]{:S(2)}) collective-permute-start(bf16[344,128]{1,0:T(8,128)(2,1)S(1)} %pair.1), channel_id=1, source_target_pairs={{0,96},{32,128},{64,160},{96,192},{128,224},{1,97},{33,129},{65,16... | collective-permute-start | bytes 264200 | tf_op jit(solution)/shard_map/ppermute | solution.py:350
  36.7 6.8 %collective-permute-start.3 = (bf16[344,128]{1,0:T(8,128)(2,1)S(1)}, bf16[344,128]{1,0:T(8,128)(2,1)S(1)}, u32[]{:S(2)}, u32[]{:S(2)}) collective-permute-start(bf16[344,128]{1,0:T(8,128)(2,1)S(1)} %pair.1), channel_id=1, source_target_pairs={{0,160},{32,192},{64,224},{1,161},{33,193},{65,225},{2,162},{34,19... | collective-permute-start | bytes 264200 | tf_op jit(solution)/shard_map/ppermute | solution.py:350
  38.0 6.8 %collective-permute-start.4 = (bf16[344,128]{1,0:T(8,128)(2,1)S(1)}, bf16[344,128]{1,0:T(8,128)(2,1)S(1)}, u32[]{:S(2)}, u32[]{:S(2)}) collective-permute-start(bf16[344,128]{1,0:T(8,128)(2,1)S(1)} %pair.1), channel_id=1, source_target_pairs={{0,224},{1,225},{2,226},{3,227},{4,228},{5,229},{6,230},{7,231},{8... | collective-permute-start | bytes 264200 | tf_op jit(solution)/shard_map/ppermute | solution.py:350
  44.8 10.1 %copy-start = (bf16[320,2560]{1,0:T(8,128)(2,1)S(1)}, bf16[320,2560]{1,0:T(8,128)(2,1)}, u32[]{:S(2)}) copy-start(bf16[320,2560]{1,0:T(8,128)(2,1)} %refs_2_.1) | copy-start | bytes 4915204
  44.8 10.1 %copy-start.2 = (f32[5120]{0:T(1024)S(1)}, f32[5120]{0:T(1024)}, u32[]{:S(2)}) copy-start(f32[5120]{0:T(1024)} %param.16) | copy-start | bytes 61444
  46.1 8.8 %collective-permute-start.5 = (bf16[320,512]{1,0:T(8,128)(2,1)S(1)}, bf16[320,512]{1,0:T(8,128)(2,1)S(1)}, u32[]{:S(2)}, u32[]{:S(2)}) collective-permute-start(bf16[320,512]{1,0:T(8,128)(2,1)S(1)} %get-tuple-element.44), channel_id=1, source_target_pairs={{0,4},{1,17},{2,6},{3,19},{4,0},{5,21},{6,2},{7,23},{8,12},{9,25},... | collective-permute-start | bytes 983048 | tf_op jit(solution)/shard_map/ppermute | solution.py:304
  48.3 10.0 %collective-permute-start.10 = (bf16[320,512]{1,0:T(8,128)(2,1)S(1)}, bf16[320,512]{1,0:T(8,128)(2,1)S(1)}, u32[]{:S(2)}, u32[]{:S(2)}) collective-permute-start(bf16[320,512]{1,0:T(8,128)(2,1)S(1)} %get-tuple-element.49), channel_id=1, source_target_pairs={{0,2},{1,9},{2,4},{3,11},{4,6},{5,13},{6,0},{7,15},{8,10},{9,17},{... | collective-permute-start | bytes 983048 | tf_op jit(solution)/shard_map/ppermute | solution.py:304
  48.3 10.0 %collective-permute-start.11 = (bf16[320,512]{1,0:T(8,128)(2,1)S(1)}, bf16[320,512]{1,0:T(8,128)(2,1)S(1)}, u32[]{:S(2)}, u32[]{:S(2)}) collective-permute-start(bf16[320,512]{1,0:T(8,128)(2,1)S(1)} %get-tuple-element.50), channel_id=1, source_target_pairs={{0,6},{1,25},{2,0},{3,27},{4,2},{5,29},{6,4},{7,31},{8,14},{9,1},{... | collective-permute-start | bytes 983048 | tf_op jit(solution)/shard_map/ppermute | solution.py:304
  59.2 8.6 %collective-permute-start.12 = (bf16[136,1280]{1,0:T(8,128)(2,1)S(1)}, bf16[136,1280]{1,0:T(8,128)(2,1)S(1)}, u32[]{:S(2)}, u32[]{:S(2)}) collective-permute-start(bf16[136,1280]{1,0:T(8,128)(2,1)S(1)} %get-tuple-element.55), channel_id=1, source_target_pairs={{0,8},{1,3},{2,10},{3,5},{4,12},{5,7},{6,14},{7,1},{8,16},{9,11},{... | collective-permute-start | bytes 1044488 | tf_op jit(solution)/shard_map/ppermute | solution.py:304
  59.6 7.5 %collective-permute-start.13 = (bf16[128,1280]{1,0:T(8,128)(2,1)S(1)}, bf16[128,1280]{1,0:T(8,128)(2,1)S(1)}, u32[]{:S(2)}, u32[]{:S(2)}) collective-permute-start(bf16[128,1280]{1,0:T(8,128)(2,1)S(1)} %get-tuple-element.56), channel_id=1, source_target_pairs={{0,24},{1,7},{2,26},{3,1},{4,28},{5,3},{6,30},{7,5},{8,0},{9,15},{... | collective-permute-start | bytes 983048 | tf_op jit(solution)/shard_map/ppermute | solution.py:304
  64.4 15.7 %collective-permute-start.16 = (bf16[136,1280]{1,0:T(8,128)(2,1)S(1)}, bf16[136,1280]{1,0:T(8,128)(2,1)S(1)}, u32[]{:S(2)}, u32[]{:S(2)}) collective-permute-start(bf16[136,1280]{1,0:T(8,128)(2,1)S(1)} %get-tuple-element.59), channel_id=1, source_target_pairs={{0,24},{1,7},{2,26},{3,1},{4,28},{5,3},{6,30},{7,5},{8,0},{9,15},{... | collective-permute-start | bytes 1044488 | tf_op jit(solution)/shard_map/ppermute | solution.py:304
  67.9 12.1 %collective-permute-start.14 = (bf16[136,1280]{1,0:T(8,128)(2,1)S(1)}, bf16[136,1280]{1,0:T(8,128)(2,1)S(1)}, u32[]{:S(2)}, u32[]{:S(2)}) collective-permute-start(bf16[136,1280]{1,0:T(8,128)(2,1)S(1)} %get-tuple-element.57), channel_id=1, source_target_pairs={{0,8},{1,3},{2,10},{3,5},{4,12},{5,7},{6,14},{7,1},{8,16},{9,11},{... | collective-permute-start | bytes 1044488 | tf_op jit(solution)/shard_map/ppermute | solution.py:304
  68.2 11.8 %collective-permute-start.15 = (bf16[128,1280]{1,0:T(8,128)(2,1)S(1)}, bf16[128,1280]{1,0:T(8,128)(2,1)S(1)}, u32[]{:S(2)}, u32[]{:S(2)}) collective-permute-start(bf16[128,1280]{1,0:T(8,128)(2,1)S(1)} %get-tuple-element.58), channel_id=1, source_target_pairs={{0,8},{1,3},{2,10},{3,5},{4,12},{5,7},{6,14},{7,1},{8,16},{9,11},{... | collective-permute-start | bytes 983048 | tf_op jit(solution)/shard_map/ppermute | solution.py:304
  69.4 10.6 %collective-permute-start.17 = (bf16[128,1280]{1,0:T(8,128)(2,1)S(1)}, bf16[128,1280]{1,0:T(8,128)(2,1)S(1)}, u32[]{:S(2)}, u32[]{:S(2)}) collective-permute-start(bf16[128,1280]{1,0:T(8,128)(2,1)S(1)} %get-tuple-element.60), channel_id=1, source_target_pairs={{0,24},{1,7},{2,26},{3,1},{4,28},{5,3},{6,30},{7,5},{8,0},{9,15},{... | collective-permute-start | bytes 983048 | tf_op jit(solution)/shard_map/ppermute | solution.py:304

commit v6 on v5

--- a/solution.py
+++ b/solution.py
@@ -15,6 +15,7 @@
 SUB = 128
 EXTRA = 8
 PAD = 8
+PIECES = 4
 
 epsilon = 1e-05
 
@@ -54,9 +55,11 @@
     blocks = tokens // BLOCK
     group = lax.axis_index("head") * heads * GROUPS // HEAD_COUNT
     columns = pl.ds(pl.multiple_of(group * STATE, STATE), STATE)
-    sources = (decay_hbm, step_hbm, x_hbm, b_hbm.at[:, columns], c_hbm.at[:, columns])
-    targets = (decay_ref, step_ref, x_ref, b_ref, c_ref)
-    fetches = [pltpu.make_async_copy(sources[k], targets[k], sems.at[k]) for k in range(5)]
+    piece = tokens // PIECES
+    pieces = [slice(k * piece, (k + 1) * piece) for k in range(PIECES)]
+    sources = [decay_hbm, step_hbm, b_hbm.at[:, columns]] + [x_hbm.at[:, span] for span in pieces] + [c_hbm.at[:, columns]]
+    targets = [decay_ref, step_ref, b_ref] + [x_ref.at[:, span] for span in pieces] + [c_ref]
+    fetches = [pltpu.make_async_copy(sources[k], targets[k], sems.at[k]) for k in range(PIECES + 4)]
     for fetch in fetches:
         fetch.start()
     fetches[0].wait()
@@ -75,11 +78,13 @@
         cum_ref[:, span] = cumulative
         factor_ref[:, span] = jnp.exp(cumulative + offset)
         offset = offset + cumulative[:, BLOCK - 1 :]
-    for fetch in fetches[1:4]:
-        fetch.wait()
+    fetches[1].wait()
+    fetches[2].wait()
     state = jnp.zeros((heads * HEAD_DIM, STATE), f32)
     for c in range(blocks):
         span = slice(c * BLOCK, (c + 1) * BLOCK)
+        if c * BLOCK % piece == 0:
+            fetches[3 + c * BLOCK // piece].wait()
         cumulative = sums[c * PAD : (c + 1) * PAD]
         end = cumulative[:, BLOCK - 1 :]
         prefix_ref[c] = state.astype(bf16)
@@ -96,16 +101,7 @@
     total_ref[0 : heads * HEAD_DIM, :] = state.astype(bf16)
     parts = split3(jnp.broadcast_to(offset, (PAD, STATE)))
     total_ref[heads * HEAD_DIM :, :] = jnp.concatenate(parts, axis=0)
-    fetches[4].wait()
-
-
-def pair_kernel(total_ref, before_ref, pair_ref):
-    channels = total_ref.shape[0] - 3 * PAD
-    heads = channels // HEAD_DIM
-    logs = join3(total_ref[channels:, :], PAD)
-    decayed = per_head(jnp.exp(logs), heads, STATE) * before_ref[0:channels, :].astype(f32)
-    pair_ref[0:channels, :] = (total_ref[0:channels, :].astype(f32) + decayed).astype(bf16)
-    pair_ref[channels:, :] = jnp.concatenate(split3(logs + join3(before_ref[channels:, :], PAD)), axis=0)
+    fetches[-1].wait()
 
 
 def within_kernel(skip_ref, x_ref, b_ref, c_ref, cum_ref, step_ref, prefix_ref, out_ref):
@@ -341,7 +337,7 @@
             pltpu.VMEM((tokens, STATE), bf16),
             pltpu.VMEM((heads, tokens), f32),
         ],
-        scratch_shapes=[pltpu.VMEM((heads, tokens), f32), pltpu.SemaphoreType.DMA((5,))],
+        scratch_shapes=[pltpu.VMEM((heads, tokens), f32), pltpu.SemaphoreType.DMA((PIECES + 4,))],
         compiler_params=params,
         name="state",
     )(*[far(value) for value in (ssm_columns, b_proj, c_proj, step_size, log_decay)])
@@ -349,7 +345,9 @@
     def along(value, shift):
         return lax.ppermute(value, "seq", [(k, k + shift) for k in range(seq_count - shift)])
 
-    before = along(total, 1)
+    totals = []
+    for shift in range(1, seq_count):
+        totals.append(along(total, shift))
     local = pl.pallas_call(
         within_kernel,
         in_specs=[pl.BlockSpec(memory_space=pltpu.SMEM)] + [near] * 6,
@@ -358,18 +356,7 @@
         compiler_params=params,
         name="within",
     )(skip_gain, *hold(x_own, b_own, c_own, cum, step_own, prefix))
-    before, local = lax.optimization_barrier((before, local))
-    pair = pl.pallas_call(
-        pair_kernel,
-        in_specs=[near] * 2,
-        out_specs=near,
-        out_shape=pltpu.VMEM((payload, STATE), bf16),
-        compiler_params=params,
-        name="pair",
-    )(*hold(total, before))
-    totals = [along(pair, shift) for shift in range(1, seq_count, 2)]
-
-    weight_before, weight_after, pair = lax.optimization_barrier((weight_before, weight_after, pair))
+    local, weight_before, weight_after = lax.optimization_barrier((local, weight_before, weight_after))
     middle = channels // 2
     upper, lower = weight_before[:middle], weight_after[middle:]
     upper, lower = ring(upper, 1, True), ring(lower, following, True)

time: 81.4 us -> 92.6 us (1.14)
  the two profiles are of different devices: /device:TPU:2 before, /device:TPU:6 now
where the time goes in v6:
time: 92.6 us; the launch traced here: 92.4 us
  starting transfers between devices  39.4 us (43%)
  waiting for transfers between devices  38.2 us (41%)
  Pallas kernels  14.5 us (16%)
    ppermute x13, waiting for transfers between devices, ring(): return lax.ppermute(value, ('head', 'batch'), ring_pairs(shift, gather))  33.3 us
    ppermute x7, starting transfers between devices, along(): lax.ppermute(value, 'seq', [(k, k + shift) for k in range(seq_count - shi...  24 us
    ppermute x13, starting transfers between devices, ring(): return lax.ppermute(value, ('head', 'batch'), ring_pairs(shift, gather))  15.4 us
    ppermute x7, waiting for transfers between devices, along(): lax.ppermute(value, 'seq', [(k, k + shift) for k in range(seq_count - shi...  4.91 us
    pallas_call x1, Pallas kernels, body(): pl.pallas_call(within_kernel, in_specs=[pl.BlockSpec(memory_space=pltpu.S...  4.29 us
    pallas_call x1, Pallas kernels, body(): pl.pallas_call(state_kernel, in_specs=[pl.BlockSpec(memory_space=pltpu.HB...  2.57 us
    pallas_call x1, Pallas kernels, body(): pl.pallas_call(begin_kernel, in_specs=[near] * 6, out_specs=[near] * 2, s...  2.3 us
  transfers between devices with their start and end apart: 20, of which 10 were waited for; matrix products, arithmetic and copies ran while one was open for 0% of the time, Pallas kernels for 14%

profile of v6, /device:TPU:6, one launch (start us, length us, event | category | flops | bytes accessed | tf_op | source)
XLA Modules:
  0.0 92.4 jit_solution(8332555990008179754)
XLA Ops:
  0.0 2.2 %collective-permute-start = (bf16[320,2560]{1,0:T(8,128)(2,1)}, bf16[320,2560]{1,0:T(8,128)(2,1)S(1)}, u32[]{:S(2)}, u32[]{:S(2)}) collective-permute-start(bf16[320,2560]{1,0:T(8,128)(2,1)} %refs_2_.1), channel_id=1, source_target_pairs={{0,2},{1,9},{2,4},{3,11},{4,6},{5,13},{6,0},{7,15},{8,10},{9,17},{... | collective-permute-start | bytes 4915208 | tf_op jit(solution)/shard_map/ppermute | solution.py:300
  2.2 2.6 %state.1 = (bf16[8,320,128]{2,1,0:T(8,128)(2,1)S(1)}, bf16[344,128]{1,0:T(8,128)(2,1)S(1)}, f32[8,2048]{1,0:T(8,128)S(1)}, f32[8,2048]{1,0:T(8,128)S(1)}, bf16[3...) custom-call(bf16[320,2048]{1,0:T(8,128)(2,1)} %bitcast.7, ...), custom_call_target="tpu_custom_call" | custom-call | tf_op jit(solution)/shard_map/state/pallas_call | solution.py:326
  4.8 4.3 %within.1.out_ref = f32[320,2048]{1,0:T(8,128)S(1)} custom-call(f32[5]{0:T(128)S(1)} %copy-done.3, bf16[320,2048]{1,0:T(8,128)(2,1)S(1)} %get-tuple-element.32.x_ref, bf16[2048,128]{1,0:T(8,128)(2,1)S(1)} %get-tuple-element.33.b_ref, bf16[2048,128]{1,0:T(8,128)(2,1)S(1)} %get-tuple-element.34.c_ref, f32[8,2048]{1,0:T(8,128)S(1)} %get-tuple-element.35.cum_ref, ...), custom_call_target="tpu_custom_call" | custom-call | tf_op jit(solution)/shard_map/within/pallas_call | solution.py:351
  9.1 12.2 %collective-permute-done.refs_2_ = bf16[320,2560]{1,0:T(8,128)(2,1)S(1)} collective-permute-done((bf16[320,2560]{1,0:T(8,128)(2,1)}, bf16[320,2560]{1,0:T(8,128)(2,1)S(1)}, u32[]{:S(2)}, u32[]{:S(2)}) %collective-permute-start) | collective-permute-done | bytes 1638432 | tf_op jit(solution)/shard_map/ppermute | solution.py:300
  21.3 3.4 %collective-permute-done.1.refs_3_ = bf16[320,2560]{1,0:T(8,128)(2,1)S(1)} collective-permute-done((bf16[320,2560]{1,0:T(8,128)(2,1)}, bf16[320,2560]{1,0:T(8,128)(2,1)S(1)}, u32[]{:S(2)}, u32[]{:S(2)}) %collective-permute-start.1) | collective-permute-done | bytes 1638432 | tf_op jit(solution)/shard_map/ppermute | solution.py:300
  24.9 2.1 %collective-permute-start.11 = (bf16[160,2560]{1,0:T(8,128)(2,1)S(1)}, bf16[160,2560]{1,0:T(8,128)(2,1)S(1)}, u32[]{:S(2)}, u32[]{:S(2)}) collective-permute-start(bf16[160,2560]{1,0:T(8,128)(2,1)S(1)} %slice.7), channel_id=1, source_target_pairs={{0,6},{1,25},{2,0},{3,27},{4,2},{5,29},{6,4},{7,31},{8,14},{9,1},{... | collective-permute-start | bytes 2457608 | tf_op jit(solution)/shard_map/ppermute | solution.py:300
  27.0 2.1 %collective-permute-start.2 = (bf16[344,128]{1,0:T(8,128)(2,1)S(1)}, bf16[344,128]{1,0:T(8,128)(2,1)S(1)}, u32[]{:S(2)}, u32[]{:S(2)}) collective-permute-start(bf16[344,128]{1,0:T(8,128)(2,1)S(1)} %get-tuple-element.40), channel_id=1, source_target_pairs={{0,32},{32,64},{64,96},{96,128},{128,160},{160,192},{192,224},{1,3... | collective-permute-start | bytes 264200 | tf_op jit(solution)/shard_map/ppermute | solution.py:346
  29.1 5.2 %collective-permute-start.3 = (bf16[344,128]{1,0:T(8,128)(2,1)S(1)}, bf16[344,128]{1,0:T(8,128)(2,1)S(1)}, u32[]{:S(2)}, u32[]{:S(2)}) collective-permute-start(bf16[344,128]{1,0:T(8,128)(2,1)S(1)} %get-tuple-element.40), channel_id=1, source_target_pairs={{0,64},{32,96},{64,128},{96,160},{128,192},{160,224},{1,65},{33,97... | collective-permute-start | bytes 264200 | tf_op jit(solution)/shard_map/ppermute | solution.py:346
  34.3 5.9 %collective-permute-start.4 = (bf16[344,128]{1,0:T(8,128)(2,1)S(1)}, bf16[344,128]{1,0:T(8,128)(2,1)S(1)}, u32[]{:S(2)}, u32[]{:S(2)}) collective-permute-start(bf16[344,128]{1,0:T(8,128)(2,1)S(1)} %get-tuple-element.40), channel_id=1, source_target_pairs={{0,96},{32,128},{64,160},{96,192},{128,224},{1,97},{33,129},{65,16... | collective-permute-start | bytes 264200 | tf_op jit(solution)/shard_map/ppermute | solution.py:346
  40.3 2.4 %collective-permute-start.5 = (bf16[344,128]{1,0:T(8,128)(2,1)S(1)}, bf16[344,128]{1,0:T(8,128)(2,1)S(1)}, u32[]{:S(2)}, u32[]{:S(2)}) collective-permute-start(bf16[344,128]{1,0:T(8,128)(2,1)S(1)} %get-tuple-element.40), channel_id=1, source_target_pairs={{0,128},{32,160},{64,192},{96,224},{1,129},{33,161},{65,193},{97,2... | collective-permute-start | bytes 264200 | tf_op jit(solution)/shard_map/ppermute | solution.py:346
  42.7 5.0 %collective-permute-start.6 = (bf16[344,128]{1,0:T(8,128)(2,1)S(1)}, bf16[344,128]{1,0:T(8,128)(2,1)S(1)}, u32[]{:S(2)}, u32[]{:S(2)}) collective-permute-start(bf16[344,128]{1,0:T(8,128)(2,1)S(1)} %get-tuple-element.40), channel_id=1, source_target_pairs={{0,160},{32,192},{64,224},{1,161},{33,193},{65,225},{2,162},{34,19... | collective-permute-start | bytes 264200 | tf_op jit(solution)/shard_map/ppermute | solution.py:346
  47.7 2.2 %collective-permute-start.7 = (bf16[344,128]{1,0:T(8,128)(2,1)S(1)}, bf16[344,128]{1,0:T(8,128)(2,1)S(1)}, u32[]{:S(2)}, u32[]{:S(2)}) collective-permute-start(bf16[344,128]{1,0:T(8,128)(2,1)S(1)} %get-tuple-element.40), channel_id=1, source_target_pairs={{0,192},{32,224},{1,193},{33,225},{2,194},{34,226},{3,195},{35,227... | collective-permute-start | bytes 264200 | tf_op jit(solution)/shard_map/ppermute | solution.py:346
  49.8 1.3 %collective-permute-start.8 = (bf16[344,128]{1,0:T(8,128)(2,1)S(1)}, bf16[344,128]{1,0:T(8,128)(2,1)S(1)}, u32[]{:S(2)}, u32[]{:S(2)}) collective-permute-start(bf16[344,128]{1,0:T(8,128)(2,1)S(1)} %get-tuple-element.40), channel_id=1, source_target_pairs={{0,224},{1,225},{2,226},{3,227},{4,228},{5,229},{6,230},{7,231},{8... | collective-permute-start | bytes 264200 | tf_op jit(solution)/shard_map/ppermute | solution.py:346
  51.1 2.9 %collective-permute-done.6.refs_4_ = bf16[344,128]{1,0:T(8,128)(2,1)S(1)} collective-permute-done((bf16[344,128]{1,0:T(8,128)(2,1)S(1)}, bf16[344,128]{1,0:T(8,128)(2,1)S(1)}, u32[]{:S(2)}, u32[]{:S(2)}) %collective-permute-start.6) | collective-permute-done | bytes 88096 | tf_op jit(solution)/shard_map/ppermute | solution.py:346
  54.0 1.1 %collective-permute-done.7.refs_5_ = bf16[344,128]{1,0:T(8,128)(2,1)S(1)} collective-permute-done((bf16[344,128]{1,0:T(8,128)(2,1)S(1)}, bf16[344,128]{1,0:T(8,128)(2,1)S(1)}, u32[]{:S(2)}, u32[]{:S(2)}) %collective-permute-start.7) | collective-permute-done | bytes 88096 | tf_op jit(solution)/shard_map/ppermute | solution.py:346
  55.1 0.9 %collective-permute-done.8.refs_6_ = bf16[344,128]{1,0:T(8,128)(2,1)S(1)} collective-permute-done((bf16[344,128]{1,0:T(8,128)(2,1)S(1)}, bf16[344,128]{1,0:T(8,128)(2,1)S(1)}, u32[]{:S(2)}, u32[]{:S(2)}) %collective-permute-start.8) | collective-permute-done | bytes 88096 | tf_op jit(solution)/shard_map/ppermute | solution.py:346
  56.1 1.3 %gate.1 = (bf16[320,512]{1,0:T(8,128)(2,1)S(1)}, bf16[320,512]{1,0:T(8,128)(2,1)S(1)}, bf16[320,512]{1,0:T(8,128)(2,1)S(1)}, bf16[320,512]{1,0:T(8,128)(2,1)S(1)}) custom-call(f32[320,2048]{1,0:T(8,128)S(1)} %within.1.out_ref, bf16[320,2048]{1,0:T(8,128)(2,1)S(1)} %bitcast.3, bf16[2048,128]{1,0:T(8,128)(2,1)S(1)} %get-tuple-element.34.c_ref, ...), custom_call_target="tpu_custom_call" | custom-call | tf_op jit(solution)/shard_map/gate/pallas_call | solution.py:365
  57.4 1.2 %collective-permute-start.9 = (bf16[320,512]{1,0:T(8,128)(2,1)S(1)}, bf16[320,512]{1,0:T(8,128)(2,1)S(1)}, u32[]{:S(2)}, u32[]{:S(2)}) collective-permute-start(bf16[320,512]{1,0:T(8,128)(2,1)S(1)} %get-tuple-element.42), channel_id=1, source_target_pairs={{0,4},{1,17},{2,6},{3,19},{4,0},{5,21},{6,2},{7,23},{8,12},{9,25},... | collective-permute-start | bytes 983048 | tf_op jit(solution)/shard_map/ppermute | solution.py:300
  58.6 2.2 %collective-permute-start.12 = (bf16[320,512]{1,0:T(8,128)(2,1)S(1)}, bf16[320,512]{1,0:T(8,128)(2,1)S(1)}, u32[]{:S(2)}, u32[]{:S(2)}) collective-permute-start(bf16[320,512]{1,0:T(8,128)(2,1)S(1)} %get-tuple-element.47), channel_id=1, source_target_pairs={{0,2},{1,9},{2,4},{3,11},{4,6},{5,13},{6,0},{7,15},{8,10},{9,17},{... | collective-permute-start | bytes 983048 | tf_op jit(solution)/shard_map/ppermute | solution.py:300
  60.8 5.3 %collective-permute-done.9.refs_1_ = bf16[320,512]{1,0:T(8,128)(2,1)S(1)} collective-permute-done((bf16[320,512]{1,0:T(8,128)(2,1)S(1)}, bf16[320,512]{1,0:T(8,128)(2,1)S(1)}, u32[]{:S(2)}, u32[]{:S(2)}) %collective-permute-start.9) | collective-permute-done | bytes 327712 | tf_op jit(solution)/shard_map/ppermute | solution.py:300
  66.1 2.3 %begin.1 = (f32[512,2560]{1,0:T(8,128)S(1)}, f32[8,512]{1,0:T(8,128)S(1)}) custom-call(f32[40,128]{1,0:T(8,128)S(1)} %bitcast.4, bf16[320,512]{1,0:T(8,128)(2,1)S(1)} %get-tuple-element.41.refs_0_, bf16[320,512]{1,0:T(8,128)(2,1)S(1)} %collective-permute-done.9.refs_1_, bf16[320,2560]{1,0:T(8,128)(2,1)S(1)} %copy-done, ...), custom_call_target="tpu_custom_call" | custom-call | tf_op jit(solution)/shard_map/begin/pallas_call | solution.py:380
  68.4 1.1 %collective-permute-done.13.refs_1_ = bf16[320,512]{1,0:T(8,128)(2,1)S(1)} collective-permute-done((bf16[320,512]{1,0:T(8,128)(2,1)S(1)}, bf16[320,512]{1,0:T(8,128)(2,1)S(1)}, u32[]{:S(2)}, u32[]{:S(2)}) %collective-permute-start.13) | collective-permute-done | bytes 327712 | tf_op jit(solution)/shard_map/ppermute | solution.py:300
  69.6 0.8 opposite.1
  70.8 3.0 %collective-permute-start.15 = (bf16[128,1280]{1,0:T(8,128)(2,1)S(1)}, bf16[128,1280]{1,0:T(8,128)(2,1)S(1)}, u32[]{:S(2)}, u32[]{:S(2)}) collective-permute-start(bf16[128,1280]{1,0:T(8,128)(2,1)S(1)} %get-tuple-element.54), channel_id=1, source_target_pairs={{0,24},{1,7},{2,26},{3,1},{4,28},{5,3},{6,30},{7,5},{8,0},{9,15},{... | collective-permute-start | bytes 983048 | tf_op jit(solution)/shard_map/ppermute | solution.py:300
  73.7 1.8 %project.1 = (bf16[136,1280]{1,0:T(8,128)(2,1)S(1)}, bf16[128,1280]{1,0:T(8,128)(2,1)S(1)}, bf16[136,1280]{1,0:T(8,128)(2,1)S(1)}, bf16[128,1280]{1,0:T(8,128)(2...) custom-call(f32[40,128]{1,0:T(8,128)S(1)} %bitcast.6, f32[512,2560]{1,0:T(8,128)S(1)} %get-tuple-element.45.begun_ref, ...), custom_call_target="tpu_custom_call" | custom-call | tf_op jit(solution)/shard_map/project/pallas_call | solution.py:401
  75.6 0.6 collective-permute-start.18
  76.2 2.1 %collective-permute-done.15.got_second = bf16[128,1280]{1,0:T(8,128)(2,1)S(1)} collective-permute-done((bf16[128,1280]{1,0:T(8,128)(2,1)S(1)}, bf16[128,1280]{1,0:T(8,128)(2,1)S(1)}, u32[]{:S(2)}, u32[]{:S(2)}) %collective-permute-start.15) | collective-permute-done | bytes 327712 | tf_op jit(solution)/shard_map/ppermute | solution.py:300
  78.3 0.7 collective-permute-done.14.got_first
  79.5 1.5 %collective-permute-start.17 = (bf16[128,1280]{1,0:T(8,128)(2,1)S(1)}, bf16[128,1280]{1,0:T(8,128)(2,1)S(1)}, u32[]{:S(2)}, u32[]{:S(2)}) collective-permute-start(bf16[128,1280]{1,0:T(8,128)(2,1)S(1)} %get-tuple-element.56), channel_id=1, source_target_pairs={{0,8},{1,3},{2,10},{3,5},{4,12},{5,7},{6,14},{7,1},{8,16},{9,11},{... | collective-permute-start | bytes 983048 | tf_op jit(solution)/shard_map/ppermute | solution.py:300
  81.0 1.8 %collective-permute-start.19 = (bf16[128,1280]{1,0:T(8,128)(2,1)S(1)}, bf16[128,1280]{1,0:T(8,128)(2,1)S(1)}, u32[]{:S(2)}, u32[]{:S(2)}) collective-permute-start(bf16[128,1280]{1,0:T(8,128)(2,1)S(1)} %get-tuple-element.58), channel_id=1, source_target_pairs={{0,24},{1,7},{2,26},{3,1},{4,28},{5,3},{6,30},{7,5},{8,0},{9,15},{... | collective-permute-start | bytes 983048 | tf_op jit(solution)/shard_map/ppermute | solution.py:300
  82.8 8.5 %collective-permute-done.17.refs_3_ = bf16[128,1280]{1,0:T(8,128)(2,1)S(1)} collective-permute-done((bf16[128,1280]{1,0:T(8,128)(2,1)S(1)}, bf16[128,1280]{1,0:T(8,128)(2,1)S(1)}, u32[]{:S(2)}, u32[]{:S(2)}) %collective-permute-start.17) | collective-permute-done | bytes 327712 | tf_op jit(solution)/shard_map/ppermute | solution.py:300
  91.2 1.2 %finish.1 = bf16[128,2560]{1,0:T(8,128)(2,1)} custom-call(f32[128,2560]{1,0:T(8,128)S(1)} %get-tuple-element.49.refs_0_, f32[8,128]{1,0:T(8,128)S(1)} %get-tuple-element.50.refs_1_, bf16[136,1280]{1,0:T(8,128)(2,1)S(1)} %collective-permute-done.16.refs_2_, bf16[128,1280]{1,0:T(8,128)(2,1)S(1)} %collective-permute-done.17.refs_3_, ...), custom_call_target="tpu_custom_call" | custom-call | tf_op jit(solution)/shard_map/finish/pallas_call | solution.py:423
  (26 shorter events, 1.1 us)
Async XLA Ops:
  0.0 21.3 %collective-permute-start = (bf16[320,2560]{1,0:T(8,128)(2,1)}, bf16[320,2560]{1,0:T(8,128)(2,1)S(1)}, u32[]{:S(2)}, u32[]{:S(2)}) collective-permute-start(bf16[320,2560]{1,0:T(8,128)(2,1)} %refs_2_.1), channel_id=1, source_target_pairs={{0,2},{1,9},{2,4},{3,11},{4,6},{5,13},{6,0},{7,15},{8,10},{9,17},{... | collective-permute-start | bytes 4915208 | tf_op jit(solution)/shard_map/ppermute | solution.py:300
  2.2 22.5 %collective-permute-start.1 = (bf16[320,2560]{1,0:T(8,128)(2,1)}, bf16[320,2560]{1,0:T(8,128)(2,1)S(1)}, u32[]{:S(2)}, u32[]{:S(2)}) collective-permute-start(bf16[320,2560]{1,0:T(8,128)(2,1)} %refs_2_.1), channel_id=1, source_target_pairs={{0,6},{1,25},{2,0},{3,27},{4,2},{5,29},{6,4},{7,31},{8,14},{9,1},{... | collective-permute-start | bytes 4915208 | tf_op jit(solution)/shard_map/ppermute | solution.py:300
  2.2 2.6 %copy-start.3 = (f32[5]{0:T(128)S(1)}, f32[5]{0:T(128)}, u32[]{:S(2)}) copy-start(f32[5]{0:T(128)} %skip_ref.1) | copy-start | bytes 64
  9.1 47.0 %copy-start.1 = (bf16[2048,320]{0,1:T(8,128)(2,1)S(1)}, bf16[2048,320]{0,1:T(8,128)(2,1)}, u32[]{:S(2)}) copy-start(bf16[2048,320]{0,1:T(8,128)(2,1)} %param.10) | copy-start | bytes 3932164
  24.8 41.3 %collective-permute-start.10 = (bf16[160,2560]{1,0:T(8,128)(2,1)S(1)}, bf16[160,2560]{1,0:T(8,128)(2,1)S(1)}, u32[]{:S(2)}, u32[]{:S(2)}) collective-permute-start(bf16[160,2560]{1,0:T(8,128)(2,1)S(1)} %slice.6), channel_id=1, source_target_pairs={{0,2},{1,9},{2,4},{3,11},{4,6},{5,13},{6,0},{7,15},{8,10},{9,17},{... | collective-permute-start | bytes 2457608 | tf_op jit(solution)/shard_map/ppermute | solution.py:300
  24.9 41.2 %collective-permute-start.11 = (bf16[160,2560]{1,0:T(8,128)(2,1)S(1)}, bf16[160,2560]{1,0:T(8,128)(2,1)S(1)}, u32[]{:S(2)}, u32[]{:S(2)}) collective-permute-start(bf16[160,2560]{1,0:T(8,128)(2,1)S(1)} %slice.7), channel_id=1, source_target_pairs={{0,6},{1,25},{2,0},{3,27},{4,2},{5,29},{6,4},{7,31},{8,14},{9,1},{... | collective-permute-start | bytes 2457608 | tf_op jit(solution)/shard_map/ppermute | solution.py:300
  27.0 13.3 %collective-permute-start.2 = (bf16[344,128]{1,0:T(8,128)(2,1)S(1)}, bf16[344,128]{1,0:T(8,128)(2,1)S(1)}, u32[]{:S(2)}, u32[]{:S(2)}) collective-permute-start(bf16[344,128]{1,0:T(8,128)(2,1)S(1)} %get-tuple-element.40), channel_id=1, source_target_pairs={{0,32},{32,64},{64,96},{96,128},{128,160},{160,192},{192,224},{1,3... | collective-permute-start | bytes 264200 | tf_op jit(solution)/shard_map/ppermute | solution.py:346
  29.1 13.5 %collective-permute-start.3 = (bf16[344,128]{1,0:T(8,128)(2,1)S(1)}, bf16[344,128]{1,0:T(8,128)(2,1)S(1)}, u32[]{:S(2)}, u32[]{:S(2)}) collective-permute-start(bf16[344,128]{1,0:T(8,128)(2,1)S(1)} %get-tuple-element.40), channel_id=1, source_target_pairs={{0,64},{32,96},{64,128},{96,160},{128,192},{160,224},{1,65},{33,97... | collective-permute-start | bytes 264200 | tf_op jit(solution)/shard_map/ppermute | solution.py:346
  34.3 13.3 %collective-permute-start.4 = (bf16[344,128]{1,0:T(8,128)(2,1)S(1)}, bf16[344,128]{1,0:T(8,128)(2,1)S(1)}, u32[]{:S(2)}, u32[]{:S(2)}) collective-permute-start(bf16[344,128]{1,0:T(8,128)(2,1)S(1)} %get-tuple-element.40), channel_id=1, source_target_pairs={{0,96},{32,128},{64,160},{96,192},{128,224},{1,97},{33,129},{65,16... | collective-permute-start | bytes 264200 | tf_op jit(solution)/shard_map/ppermute | solution.py:346
  40.3 9.5 %collective-permute-start.5 = (bf16[344,128]{1,0:T(8,128)(2,1)S(1)}, bf16[344,128]{1,0:T(8,128)(2,1)S(1)}, u32[]{:S(2)}, u32[]{:S(2)}) collective-permute-start(bf16[344,128]{1,0:T(8,128)(2,1)S(1)} %get-tuple-element.40), channel_id=1, source_target_pairs={{0,128},{32,160},{64,192},{96,224},{1,129},{33,161},{65,193},{97,2... | collective-permute-start | bytes 264200 | tf_op jit(solution)/shard_map/ppermute | solution.py:346
  42.7 11.3 %collective-permute-start.6 = (bf16[344,128]{1,0:T(8,128)(2,1)S(1)}, bf16[344,128]{1,0:T(8,128)(2,1)S(1)}, u32[]{:S(2)}, u32[]{:S(2)}) collective-permute-start(bf16[344,128]{1,0:T(8,128)(2,1)S(1)} %get-tuple-element.40), channel_id=1, source_target_pairs={{0,160},{32,192},{64,224},{1,161},{33,193},{65,225},{2,162},{34,19... | collective-permute-start | bytes 264200 | tf_op jit(solution)/shard_map/ppermute | solution.py:346
  47.7 7.4 %collective-permute-start.7 = (bf16[344,128]{1,0:T(8,128)(2,1)S(1)}, bf16[344,128]{1,0:T(8,128)(2,1)S(1)}, u32[]{:S(2)}, u32[]{:S(2)}) collective-permute-start(bf16[344,128]{1,0:T(8,128)(2,1)S(1)} %get-tuple-element.40), channel_id=1, source_target_pairs={{0,192},{32,224},{1,193},{33,225},{2,194},{34,226},{3,195},{35,227... | collective-permute-start | bytes 264200 | tf_op jit(solution)/shard_map/ppermute | solution.py:346
  49.8 6.2 %collective-permute-start.8 = (bf16[344,128]{1,0:T(8,128)(2,1)S(1)}, bf16[344,128]{1,0:T(8,128)(2,1)S(1)}, u32[]{:S(2)}, u32[]{:S(2)}) collective-permute-start(bf16[344,128]{1,0:T(8,128)(2,1)S(1)} %get-tuple-element.40), channel_id=1, source_target_pairs={{0,224},{1,225},{2,226},{3,227},{4,228},{5,229},{6,230},{7,231},{8... | collective-permute-start | bytes 264200 | tf_op jit(solution)/shard_map/ppermute | solution.py:346
  56.0 10.1 %copy-start = (bf16[320,2560]{1,0:T(8,128)(2,1)S(1)}, bf16[320,2560]{1,0:T(8,128)(2,1)}, u32[]{:S(2)}) copy-start(bf16[320,2560]{1,0:T(8,128)(2,1)} %refs_2_.1) | copy-start | bytes 4915204
  56.0 10.1 %copy-start.2 = (f32[5120]{0:T(1024)S(1)}, f32[5120]{0:T(1024)}, u32[]{:S(2)}) copy-start(f32[5120]{0:T(1024)} %param.16) | copy-start | bytes 61444
  57.4 8.7 %collective-permute-start.9 = (bf16[320,512]{1,0:T(8,128)(2,1)S(1)}, bf16[320,512]{1,0:T(8,128)(2,1)S(1)}, u32[]{:S(2)}, u32[]{:S(2)}) collective-permute-start(bf16[320,512]{1,0:T(8,128)(2,1)S(1)} %get-tuple-element.42), channel_id=1, source_target_pairs={{0,4},{1,17},{2,6},{3,19},{4,0},{5,21},{6,2},{7,23},{8,12},{9,25},... | collective-permute-start | bytes 983048 | tf_op jit(solution)/shard_map/ppermute | solution.py:300
  58.6 9.8 %collective-permute-start.12 = (bf16[320,512]{1,0:T(8,128)(2,1)S(1)}, bf16[320,512]{1,0:T(8,128)(2,1)S(1)}, u32[]{:S(2)}, u32[]{:S(2)}) collective-permute-start(bf16[320,512]{1,0:T(8,128)(2,1)S(1)} %get-tuple-element.47), channel_id=1, source_target_pairs={{0,2},{1,9},{2,4},{3,11},{4,6},{5,13},{6,0},{7,15},{8,10},{9,17},{... | collective-permute-start | bytes 983048 | tf_op jit(solution)/shard_map/ppermute | solution.py:300
  60.8 8.8 %collective-permute-start.13 = (bf16[320,512]{1,0:T(8,128)(2,1)S(1)}, bf16[320,512]{1,0:T(8,128)(2,1)S(1)}, u32[]{:S(2)}, u32[]{:S(2)}) collective-permute-start(bf16[320,512]{1,0:T(8,128)(2,1)S(1)} %get-tuple-element.48), channel_id=1, source_target_pairs={{0,6},{1,25},{2,0},{3,27},{4,2},{5,29},{6,4},{7,31},{8,14},{9,1},{... | collective-permute-start | bytes 983048 | tf_op jit(solution)/shard_map/ppermute | solution.py:300
  70.4 8.6 %collective-permute-start.14 = (bf16[136,1280]{1,0:T(8,128)(2,1)S(1)}, bf16[136,1280]{1,0:T(8,128)(2,1)S(1)}, u32[]{:S(2)}, u32[]{:S(2)}) collective-permute-start(bf16[136,1280]{1,0:T(8,128)(2,1)S(1)} %get-tuple-element.53), channel_id=1, source_target_pairs={{0,8},{1,3},{2,10},{3,5},{4,12},{5,7},{6,14},{7,1},{8,16},{9,11},{... | collective-permute-start | bytes 1044488 | tf_op jit(solution)/shard_map/ppermute | solution.py:300
  70.8 7.6 %collective-permute-start.15 = (bf16[128,1280]{1,0:T(8,128)(2,1)S(1)}, bf16[128,1280]{1,0:T(8,128)(2,1)S(1)}, u32[]{:S(2)}, u32[]{:S(2)}) collective-permute-start(bf16[128,1280]{1,0:T(8,128)(2,1)S(1)} %get-tuple-element.54), channel_id=1, source_target_pairs={{0,24},{1,7},{2,26},{3,1},{4,28},{5,3},{6,30},{7,5},{8,0},{9,15},{... | collective-permute-start | bytes 983048 | tf_op jit(solution)/shard_map/ppermute | solution.py:300
  75.6 15.7 %collective-permute-start.18 = (bf16[136,1280]{1,0:T(8,128)(2,1)S(1)}, bf16[136,1280]{1,0:T(8,128)(2,1)S(1)}, u32[]{:S(2)}, u32[]{:S(2)}) collective-permute-start(bf16[136,1280]{1,0:T(8,128)(2,1)S(1)} %get-tuple-element.57), channel_id=1, source_target_pairs={{0,24},{1,7},{2,26},{3,1},{4,28},{5,3},{6,30},{7,5},{8,0},{9,15},{... | collective-permute-start | bytes 1044488 | tf_op jit(solution)/shard_map/ppermute | solution.py:300
  79.1 12.1 %collective-permute-start.16 = (bf16[136,1280]{1,0:T(8,128)(2,1)S(1)}, bf16[136,1280]{1,0:T(8,128)(2,1)S(1)}, u32[]{:S(2)}, u32[]{:S(2)}) collective-permute-start(bf16[136,1280]{1,0:T(8,128)(2,1)S(1)} %get-tuple-element.55), channel_id=1, source_target_pairs={{0,8},{1,3},{2,10},{3,5},{4,12},{5,7},{6,14},{7,1},{8,16},{9,11},{... | collective-permute-start | bytes 1044488 | tf_op jit(solution)/shard_map/ppermute | solution.py:300
  79.5 11.7 %collective-permute-start.17 = (bf16[128,1280]{1,0:T(8,128)(2,1)S(1)}, bf16[128,1280]{1,0:T(8,128)(2,1)S(1)}, u32[]{:S(2)}, u32[]{:S(2)}) collective-permute-start(bf16[128,1280]{1,0:T(8,128)(2,1)S(1)} %get-tuple-element.56), channel_id=1, source_target_pairs={{0,8},{1,3},{2,10},{3,5},{4,12},{5,7},{6,14},{7,1},{8,16},{9,11},{... | collective-permute-start | bytes 983048 | tf_op jit(solution)/shard_map/ppermute | solution.py:300
  81.0 10.2 %collective-permute-start.19 = (bf16[128,1280]{1,0:T(8,128)(2,1)S(1)}, bf16[128,1280]{1,0:T(8,128)(2,1)S(1)}, u32[]{:S(2)}, u32[]{:S(2)}) collective-permute-start(bf16[128,1280]{1,0:T(8,128)(2,1)S(1)} %get-tuple-element.58), channel_id=1, source_target_pairs={{0,24},{1,7},{2,26},{3,1},{4,28},{5,3},{6,30},{7,5},{8,0},{9,15},{... | collective-permute-start | bytes 983048 | tf_op jit(solution)/shard_map/ppermute | solution.py:300
